TPU v7x, 32 devices: a whole 2x2x4 slice. The times are simulated.
32 devices in a mesh: lat: 4 (over z), lon: 8 (over y, x, core).
Axes of the slice: x: 2, y: 2, z: 4, core: 2. Of those that a mesh axis runs over, the one named last changes fastest.
Arguments:
- zonal_wind: float32 [32, 32, 2048], P(None, 'lat', 'lon'), may hold values from -6 to 6
- merid_wind: float32 [32, 32, 2048], P(None, 'lat', 'lon'), may hold values from -6 to 6
- vertical_wind: float32 [32, 32, 2048], P(None, 'lat', 'lon'), may hold values from -6 to 6
- pressure: float32 [32, 32, 2048], P(None, 'lat', 'lon'), may hold values from -6 to 6
- zonal_coef: float32 [32], P('lat'), may hold values from 0.05 to 0.4
- merid_coef: float32 [32], P('lat'), may hold values from 0.05 to 0.4
- level_coef: float32 [32], replicated, may hold values from 0.3 to 1.5
- sound_coef: float32 [32, 32, 2048], P(None, 'lat', 'lon'), may hold values from 0.2 to 2
- cutoff: int32 [32], replicated, may hold values from 1 to 511
- filter_mask: int32 [32], replicated, may hold values from 0 to 1, as said below
Outputs:
- zonal_next: float32 [32, 32, 2048], P(None, 'lat', 'lon')
- merid_next: float32 [32, 32, 2048], P(None, 'lat', 'lon')
- vertical_next: float32 [32, 32, 2048], P(None, 'lat', 'lon')
- pressure_next: float32 [32, 32, 2048], P(None, 'lat', 'lon')
Inputs may be any that keep to these rules, and one draw needn't show every extreme that they name: `filter_mask`: for every latitude j below 16 exactly one of j and j + 16 is filtered; the filtered ones are the first n and the last 16 - n latitudes, for some n from 4 to 12.
All inputs are finite; a program needn't handle non-finite values.
Results may differ from a plain program's by a relative error of at most 0.0001.
Values sent between devices are 32-bit elements; how exact they have to be, the bound alone decides.
No kernel may reach another device: no remote copies, remote signals or barrier semaphores. Data moves between devices by JAX's collectives and lax.ppermute only.
A program may use at most 64 MiB of HBM per device.

v0:
```python
import math

import jax
import jax.numpy as jnp
from jax import lax
from jax.sharding import PartitionSpec as P

SUBSTEPS = 2


def extended(block, sides, width):
    for axis, dim in sides:
        count = lax.axis_size(axis)
        forward = [(i, i + 1) for i in range(count - 1)]
        forward.append((count - 1, 0))
        backward = [(target, source) for source, target in forward]
        low = lax.ppermute(
            lax.slice_in_dim(block, block.shape[dim] - width, None, axis=dim), axis, forward
        )
        high = lax.ppermute(lax.slice_in_dim(block, 0, width, axis=dim), axis, backward)
        block = jnp.concatenate([low, block, high], axis=dim)
    return block


def rim_fix(padded, lat_dim):
    band_index = lax.axis_index("lat")
    bands = lax.axis_size("lat")
    extent = padded.shape[lat_dim]
    position = lax.broadcasted_iota(jnp.int32, padded.shape, lat_dim)
    first_edge = jnp.logical_and(position == 0, band_index == 0)
    final_edge = jnp.logical_and(position == extent - 1, band_index == bands - 1)
    return jnp.where(jnp.logical_or(first_edge, final_edge), 0.0, padded)


def dft_tables(length):
    half_len = length // 2
    sample = lax.broadcasted_iota(jnp.int32, (length, length), 0)
    column = lax.broadcasted_iota(jnp.int32, (length, length), 1)
    is_cosine = column <= half_len
    wavenum = jnp.where(is_cosine, column, column - half_len)
    phase = sample * wavenum % length
    angle = 2.0 * math.pi / length * phase.astype(jnp.float32)
    forward = jnp.where(is_cosine, jnp.cos(angle), jnp.sin(angle))
    single = jnp.logical_and(is_cosine, jnp.logical_or(wavenum == 0, wavenum == half_len))
    weight = jnp.where(single, 1.0, 2.0) / length
    inverse = jnp.transpose(forward * weight)
    wave_row = wavenum[0].astype(jnp.float32)
    return (forward, inverse, wave_row)


def damping(wave_row, limits):
    bound_col = limits[:, None]
    ratio = bound_col / jnp.maximum(wave_row[None, :], 1.0)
    return jnp.where(wave_row[None, :] > bound_col, ratio * ratio, 1.0)


def transform_band(block, limits, forward, inverse, wave_row):
    circles = lax.all_to_all(block, "lon", split_axis=1, concat_axis=3, tiled=True)
    spectra = jnp.einsum("vetj,jc->vetc", circles, forward, precision=lax.Precision.HIGHEST)
    scaled = spectra * damping(wave_row, limits)
    damped = jnp.einsum("vetc,cj->vetj", scaled, inverse, precision=lax.Precision.HIGHEST)
    return lax.all_to_all(damped, "lon", split_axis=3, concat_axis=1, tiled=True)


def filtered_increments(increments, own_flags, own_limits, forward, inverse, wave_row):
    flag_cols = own_flags[:, None]
    damped = transform_band(increments, own_limits, forward, inverse, wave_row)
    return jnp.where(flag_cols, damped, increments)


def column_solve(vertical_wind, pstar, level_coef, sound_coef):
    levels = vertical_wind.shape[0]
    zero_slab = jnp.zeros_like(vertical_wind[0])
    ratios = []
    values = []
    prev_ratio = zero_slab
    prev_value = zero_slab
    for level in range(levels):
        alpha = level_coef[level]
        below = alpha * sound_coef[level]
        if level + 1 < levels:
            above = alpha * sound_coef[level + 1]
            rhs = vertical_wind[level] - alpha * (pstar[level + 1] - pstar[level])
        else:
            above = zero_slab
            rhs = vertical_wind[level] + alpha * pstar[level]
        pivot = 1.0 + below + above + below * prev_ratio
        prev_ratio = -above / pivot
        prev_value = (rhs + below * prev_value) / pivot
        ratios.append(prev_ratio)
        values.append(prev_value)
    solved = [zero_slab] * levels
    upper_value = values[levels - 1]
    solved[levels - 1] = upper_value
    for level in range(levels - 2, -1, -1):
        upper_value = values[level] - ratios[level] * upper_value
        solved[level] = upper_value
    new_wind = jnp.stack(solved)
    wind_below = jnp.concatenate([zero_slab[None], new_wind[:-1]], axis=0)
    new_pressure = pstar - sound_coef * (new_wind - wind_below)
    return (new_wind, new_pressure)


def body(
    zonal_wind,
    merid_wind,
    vertical_wind,
    pressure,
    zonal_coef,
    merid_coef,
    level_coef,
    sound_coef,
    cutoff,
    filter_mask,
):
    lat_rows = pressure.shape[1]
    start = lax.axis_index("lat") * lat_rows
    own_flags = lax.dynamic_slice_in_dim(filter_mask, start, lat_rows) > 0
    own_limits = lax.dynamic_slice_in_dim(cutoff, start, lat_rows).astype(jnp.float32)
    forward, inverse, wave_row = dft_tables(pressure.shape[2] * lax.axis_size("lon"))
    zonal_rows = zonal_coef[None, :, None]
    merid_rows = merid_coef[None, :, None]
    for step in range(SUBSTEPS):
        padded = extended(pressure, (("lat", 1), ("lon", 2)), 1)
        padded = rim_fix(padded, 1)
        zonal_step = -zonal_rows * (padded[:, 1:-1, 2:] - padded[:, 1:-1, :-2])
        merid_step = -merid_rows * (padded[:, 2:, 1:-1] - padded[:, :-2, 1:-1])
        increments = jnp.stack([zonal_step, merid_step])
        damped = filtered_increments(increments, own_flags, own_limits, forward, inverse, wave_row)
        winds = jnp.stack([zonal_wind, merid_wind]) + damped
        wind_pad = extended(winds, (("lat", 2), ("lon", 3)), 1)
        wind_pad = rim_fix(wind_pad, 2)
        diverge = zonal_rows * (wind_pad[0, :, 1:-1, 2:] - wind_pad[0, :, 1:-1, :-2])
        diverge = diverge + merid_rows * (wind_pad[1, :, 2:, 1:-1] - wind_pad[1, :, :-2, 1:-1])
        pstar = pressure - sound_coef * diverge
        vertical_wind, pressure = column_solve(vertical_wind, pstar, level_coef, sound_coef)
        zonal_wind = winds[0]
        merid_wind = winds[1]
    return (zonal_wind, merid_wind, vertical_wind, pressure)


def solution(mesh):
    in_specs = (
        P(None, "lat", "lon"),
        P(None, "lat", "lon"),
        P(None, "lat", "lon"),
        P(None, "lat", "lon"),
        P("lat"),
        P("lat"),
        P(),
        P(None, "lat", "lon"),
        P(),
        P(),
    )
    out_specs = (
        P(None, "lat", "lon"),
        P(None, "lat", "lon"),
        P(None, "lat", "lon"),
        P(None, "lat", "lon"),
    )
    return jax.shard_map(body, mesh=mesh, in_specs=in_specs, out_specs=out_specs, check_vma=False)
```

profile of v0, /device:TPU:0, one launch (start us, length us, event | category | flops | bytes accessed | tf_op | source)
XLA Modules:
  0.0 585.0 jit_solution(11969171518378575389)
XLA Ops:
  0.7 1.1 fusion.87
  1.8 5.1 collective-permute-start.1
  7.0 2.1 iota_select_fusion
  9.1 3.5 collective-permute-done
  12.9 0.5 collective-permute-start.3
  13.5 6.0 %collective-permute-done.3 = f32[32,10,1]{2,1,0:T(8,128)S(1)} collective-permute-done((f32[32,10,1]{2,1,0:T(8,128)S(1)}, f32[32,10,1]{2,1,0:T(8,128)S(1)}, u32[]{:S(2)}, u32[]{:S(2)}) %collective-permute-start.3) | collective-permute-done | bytes 1312 | tf_op jit(solution)/shard_map/ppermute | solution.py:20
  19.5 3.0 collective-permute-done.2
  22.5 0.5 maximum_select_fusion.2
  23.4 0.8 pad_maximum_fusion.3
  24.2 3.8 all-to-all-start
  28.2 9.5 %all-to-all-done = f32[2,32,8,256]{3,2,0,1:T(8,128)S(1)} async-done(((f32[2,32,8,256]{3,2,0,1:T(8,128)}), f32[2,32,8,256]{3,2,0,1:T(8,128)S(1)}, u32[]{:S(2)}, u32[]{:S(2)}) %all-to-all-start) | async-done | bytes 524320 | tf_op jit(solution)/shard_map/all_to_all | solution.py:58
  38.0 75.8 %fusion.15 = f32[2,4,8,2048]{3,2,1,0:T(8,128)S(1)} fusion(f32[2,4,8,2048]{3,2,1,0:T(8,128)S(1)} %all_to_all.55, s32[2048]{0:T(1024)S(1)} %iota_add_fusion, pred[2048]{0:T(1024)(128)(4,1)S(1)} %iota_compare_fusion, f32[8,2048]{1,0:T(8,128)S(1)} %fusion.44), kind=kOutput, calls=%fused_computation.21 | convolution fusion | flops 3288465408 | bytes 1124352 | tf_op jit(solution)/shard_map/vetj,jc->vetc/dot_general | solution.py:59
  113.9 82.4 %fusion.5 = f32[2,4,8,2048]{3,2,1,0:T(8,128)S(1)} fusion(f32[2,4,8,2048]{3,2,1,0:T(8,128)S(1)} %fusion.15, s32[2048]{0:T(1024)S(1)} %iota_add_fusion, pred[2048]{0:T(1024)(128)(4,1)S(1)} %iota_compare_fusion), kind=kOutput, calls=%fused_computation.8 | convolution fusion | flops 3317694464 | bytes 1058816 | tf_op jit(solution)/shard_map/vetc,cj->vetj/dot_general | solution.py:61
  196.4 5.8 copy.23
  202.1 12.3 %reshape.77 = f32[8,1,16384]{2,1,0:T(1,128)} reshape(f32[2048,2,4,8]{3,2,1,0:T(4,128)} %bitcast.161) | data formatting | bytes 1048576
  214.4 3.6 all-to-all-start.1
  218.1 9.6 %all-to-all-done.1 = f32[8,1,16384]{2,1,0:T(1,128)S(1)} async-done(((f32[8,1,16384]{2,1,0:T(1,128)}), f32[8,1,16384]{2,1,0:T(1,128)S(1)}, u32[]{:S(2)}, u32[]{:S(2)}) %all-to-all-start.1) | async-done | bytes 524320 | tf_op jit(solution)/shard_map/all_to_all | solution.py:62
  227.7 0.6 broadcast.9464
  228.2 1.9 reduce
  230.1 13.2 %reshape.78 = f32[2048,2,4,8]{3,2,1,0:T(4,128)} reshape(f32[8,16384]{1,0:T(8,128)S(1)} %reduce) | data formatting | bytes 1048576
  243.3 6.7 %copy.24 = f32[2,4,8,8,256]{4,2,0,1,3:T(8,128)S(1)} copy(f32[2,4,8,8,256]{2,1,0,4,3:T(4,128)} %bitcast.162) | data formatting | bytes 1048576 | tf_op jit(solution)/shard_map/all_to_all | solution.py:62
  250.6 1.7 collective-permute-start.4
  252.3 0.7 fusion.88
  253.0 1.5 collective-permute-done.5
  254.5 2.1 collective-permute-done.4
  257.2 0.9 collective-permute-start.6
  258.1 0.7 fusion.89
  258.8 10.3 %collective-permute-done.7 = f32[2,32,10,1]{3,2,1,0:T(8,128)S(1)} collective-permute-done((f32[2,32,10,1]{3,2,1,0:T(8,128)S(1)}, f32[2,32,10,1]{3,2,1,0:T(8,128)S(1)}, u32[]{:S(2)}, u32[]{:S(2)}) %collective-permute-start.7) | collective-permute-done | bytes 2592 | tf_op jit(solution)/shard_map/ppermute | solution.py:20
  269.1 1.4 collective-permute-done.6
  270.5 1.2 maximum_select_fusion
  272.0 20.4 %add_divide_fusion.32 = (f32[1,8,256]{2,1,0:T(8,128)S(1)}, f32[1,8,256]{2,1,0:T(8,128)S(1)}, f32[1,8,256]{2,1,0:T(8,128)S(1)}, f32[1,8,256]{2,1,0:T(8,128)S(1)},...) fusion(f32[32,8,256]{2,1,0:T(8,128)S(1)} %copy-done.6, ...), kind=kLoop, calls=%fused_computation.313 | loop fusion | flops 882688 | bytes 1523836 | tf_op jit(solution)/shard_map/div | solution.py:89
  292.5 2.0 constant_dynamic-update-slice_fusion.62
  295.1 0.5 collective-permute-start.9
  295.5 1.6 collective-permute-start.8
  297.2 2.2 collective-permute-done.9
  299.4 1.8 collective-permute-done.8
  301.5 0.5 collective-permute-start.10
  302.0 5.6 collective-permute-done.11
  307.6 2.2 collective-permute-done.10
  309.8 0.5 maximum_select_fusion.3
  310.4 1.0 fusion.32
  311.4 12.3 %all_to_all.72 = f32[2,32,8,256]{3,2,0,1:T(8,128)S(1)} all-to-all(f32[2,32,8,256]{3,2,0,1:T(8,128)S(1)} %copy.29), channel_id=1, replica_groups=mesh['lat'=4,'lon'=8] {'lon'}, dimensions={1} | all-to-all | bytes 1048576 | tf_op jit(solution)/shard_map/all_to_all | solution.py:58
  324.1 0.9 all_to_all.63
  325.0 77.2 %fusion.18 = f32[2,4,8,2048]{3,2,1,0:T(8,128)S(1)} fusion(f32[2,4,8,2048]{3,2,1,0:T(8,128)} %all_to_all.63, s32[2048]{0:T(1024)} %copy-done.21, pred[2048]{0:T(1024)(128)(4,1)} %copy-done.24, f32[8,2048]{1,0:T(8,128)} %copy-done.20), kind=kOutput, calls=%fused_computation.22 | convolution fusion | flops 3288465408 | bytes 1124352 | tf_op jit(solution)/shard_map/vetj,jc->vetc/dot_general | solution.py:59
  402.2 82.1 %fusion.3 = f32[2,4,8,2048]{3,2,1,0:T(8,128)S(1)} fusion(f32[2,4,8,2048]{3,2,1,0:T(8,128)S(1)} %fusion.18, s32[2048]{0:T(1024)S(1)} %copy-done.22, pred[2048]{0:T(1024)(128)(4,1)S(1)} %copy-done.25), kind=kOutput, calls=%fused_computation.6 | convolution fusion | flops 3317694464 | bytes 1058816 | tf_op jit(solution)/shard_map/vetc,cj->vetj/dot_general | solution.py:61
  484.3 5.8 copy.31
  490.1 11.6 %reshape.79 = f32[8,1,16384]{2,1,0:T(1,128)S(1)} reshape(f32[2048,2,4,8]{3,2,1,0:T(4,128)} %bitcast.163) | data formatting | bytes 1048576
  501.7 12.8 %all_to_all.73 = f32[8,1,16384]{2,1,0:T(1,128)} all-to-all(f32[8,1,16384]{2,1,0:T(1,128)S(1)} %reshape.79), channel_id=1, replica_groups=mesh['lat'=4,'lon'=8] {'lon'}, dimensions={0} | all-to-all | bytes 1048576 | tf_op jit(solution)/shard_map/all_to_all | solution.py:62
  514.5 2.9 reduce.1
  517.4 13.2 %reshape.80 = f32[2048,2,4,8]{3,2,1,0:T(4,128)} reshape(f32[8,16384]{1,0:T(8,128)S(1)} %reduce.1) | data formatting | bytes 1048576
  530.7 6.7 %copy.32 = f32[2,4,8,8,256]{4,2,1,3,0:T(8,128)S(1)} copy(f32[2,4,8,8,256]{2,1,0,4,3:T(4,128)} %bitcast.164) | data formatting | bytes 1048576 | tf_op jit(solution)/shard_map/all_to_all | solution.py:62
  537.3 1.0 copy_add_fusion
  538.7 1.7 collective-permute-start.12
  540.5 2.9 collective-permute-done.13
  543.4 1.4 collective-permute-done.12
  545.3 0.7 collective-permute-start.14
  546.0 0.8 slice_bitcast_fusion.2
  546.8 10.5 %collective-permute-done.15 = f32[2,32,10,1]{3,2,0,1:T(8,128)S(1)} collective-permute-done((f32[2,32,10,1]{3,2,0,1:T(8,128)S(1)}, f32[2,32,10,1]{3,2,0,1:T(8,128)S(1)}, u32[]{:S(2)}, u32[]{:S(2)}) %collective-permute-start.15) | collective-permute-done | bytes 2592 | tf_op jit(solution)/shard_map/ppermute | solution.py:20
  557.3 1.3 collective-permute-done.14
  558.6 1.8 maximum_select_fusion.1
  560.3 1.0 fusion.25
  561.3 20.7 %add_divide_fusion.1 = (f32[1,8,256]{2,1,0:T(8,128)S(1)}, f32[1,8,256]{2,1,0:T(8,128)S(1)}, f32[1,8,256]{2,1,0:T(8,128)S(1)}, f32[1,8,256]{2,1,0:T(8,128)S(1)}, ...) fusion(f32[1,8,256]{2,1,0:T(8,128)S(1)} %get-tuple-element.102,, ...), kind=kLoop, calls=%fused_computation.248 | loop fusion | flops 452608 | bytes 1269884 | tf_op jit(solution)/shard_map/div | solution.py:89
  582.0 1.5 constant_dynamic-update-slice_fusion.125
  584.0 0.8 multiply_subtract_fusion
  (167 shorter events, 4.7 us)
Async XLA Ops:
  0.6 12.0 %copy-start.3 = (f32[32,8,256]{2,1,0:T(8,128)S(1)}, f32[32,8,256]{2,1,0:T(8,128)}, u32[]{:S(2)}) copy-start(f32[32,8,256]{2,1,0:T(8,128)} %param.13) | copy-start | bytes 786436
  0.6 12.8 %copy-start.27 = (f32[8]{0:T(128)S(1)}, f32[8]{0:T(128)}, u32[]{:S(2)}) copy-start(f32[8]{0:T(128)} %param.14) | copy-start | bytes 100
  0.7 12.8 %copy-start.28 = (f32[8]{0:T(128)S(1)}, f32[8]{0:T(128)}, u32[]{:S(2)}) copy-start(f32[8]{0:T(128)} %param.15) | copy-start | bytes 100
  0.7 27.3 %copy-start.31 = (s32[32]{0:T(128)S(1)}, s32[32]{0:T(128)}, u32[]{:S(2)}) copy-start(s32[32]{0:T(128)} %param.18) | copy-start | bytes 388
  1.8 7.3 %collective-permute-start.1 = (f32[32,1,256]{2,1,0:T(1,128)S(1)}, f32[32,1,256]{2,1,0:T(1,128)S(1)}, u32[]{:S(2)}, u32[]{:S(2)}) collective-permute-start(f32[32,1,256]{2,1,0:T(1,128)S(1)} %get-tuple-element.213), channel_id=1, source_target_pairs={{8,0},{16,8},{24,16},{0,24},{9,1},{17,9},{25,17},{1,25},{10,2},{18... | collective-permute-start | bytes 98312 | tf_op jit(solution)/shard_map/ppermute | solution.py:20
  6.9 5.7 collective-permute-start
  6.9 106.9 %copy-start.21 = (s32[2048]{0:T(1024)}, s32[2048]{0:T(1024)S(1)}, u32[]{:S(2)}) copy-start(s32[2048]{0:T(1024)S(1)} %iota_add_fusion) | copy-start | bytes 24580
  6.9 106.9 %copy-start.24 = (pred[2048]{0:T(1024)(128)(4,1)}, pred[2048]{0:T(1024)(128)(4,1)S(1)}, u32[]{:S(2)}) copy-start(pred[2048]{0:T(1024)(128)(4,1)S(1)} %iota_compare_fusion) | copy-start | bytes 6148
  12.9 6.7 %collective-permute-start.3 = (f32[32,10,1]{2,1,0:T(8,128)S(1)}, f32[32,10,1]{2,1,0:T(8,128)S(1)}, u32[]{:S(2)}, u32[]{:S(2)}) collective-permute-start(f32[32,10,1]{2,1,0:T(8,128)S(1)} %get-tuple-element.209), channel_id=1, source_target_pairs={{1,0},{2,1},{3,2},{4,3},{5,4},{6,5},{7,6},{0,7},{9,8},{10,9},{11,1... | collective-permute-start | bytes 3848 | tf_op jit(solution)/shard_map/ppermute | solution.py:20
  13.4 9.2 %collective-permute-start.2 = (f32[32,10,1]{2,1,0:T(8,128)S(1)}, f32[32,10,1]{2,1,0:T(8,128)S(1)}, u32[]{:S(2)}, u32[]{:S(2)}) collective-permute-start(f32[32,10,1]{2,1,0:T(8,128)S(1)} %get-tuple-element.208), channel_id=1, source_target_pairs={{0,1},{1,2},{2,3},{3,4},{4,5},{5,6},{6,7},{7,0},{8,9},{9,10},{10,1... | collective-permute-start | bytes 3848 | tf_op jit(solution)/shard_map/ppermute | solution.py:17
  13.4 296.4 %copy-start.26 = (pred[10]{0:T(512)(128)(4,1)}, pred[10]{0:T(512)(128)(4,1)S(1)}, u32[]{:S(2)}) copy-start(pred[10]{0:T(512)(128)(4,1)S(1)} %and_or_fusion) | copy-start | bytes 34
  13.5 100.4 %copy-start.29 = (f32[8]{0:T(128)}, f32[8]{0:T(128)S(1)}, u32[]{:S(2)}) copy-start(f32[8]{0:T(128)S(1)} %neg.2118) | copy-start | bytes 100
  13.5 100.4 %copy-start.30 = (f32[8]{0:T(128)}, f32[8]{0:T(128)S(1)}, u32[]{:S(2)}) copy-start(f32[8]{0:T(128)S(1)} %neg.2119) | copy-start | bytes 100
  24.2 13.4 %all-to-all-start = ((f32[2,32,8,256]{3,2,0,1:T(8,128)}), f32[2,32,8,256]{3,2,0,1:T(8,128)S(1)}, u32[]{:S(2)}, u32[]{:S(2)}) async-start(f32[2,32,8,256]{3,2,0,1:T(8,128)} %pad_maximum_fusion.3), calls=%async_computation | async-start | bytes 1048576 | tf_op jit(solution)/shard_map/all_to_all | solution.py:58
  28.2 85.7 %copy-start.20 = (f32[8,2048]{1,0:T(8,128)}, f32[8,2048]{1,0:T(8,128)S(1)}, u32[]{:S(2)}) copy-start(f32[8,2048]{1,0:T(8,128)S(1)} %fusion.44) | copy-start | bytes 196612
  196.3 21.7 %copy-start.32 = (s32[32]{0:T(128)S(1)}, s32[32]{0:T(128)}, u32[]{:S(2)}) copy-start(s32[32]{0:T(128)} %param.19) | copy-start | bytes 388
  196.3 53.7 %copy-start.1 = (f32[32,8,256]{2,1,0:T(8,128)S(1)}, f32[32,8,256]{2,1,0:T(8,128)}, u32[]{:S(2)}) copy-start(f32[32,8,256]{2,1,0:T(8,128)} %param.11) | copy-start | bytes 786436
  196.3 53.7 %copy-start.2 = (f32[32,8,256]{2,1,0:T(8,128)S(1)}, f32[32,8,256]{2,1,0:T(8,128)}, u32[]{:S(2)}) copy-start(f32[32,8,256]{2,1,0:T(8,128)} %param.10) | copy-start | bytes 786436
  202.1 50.2 %copy-start.4 = (f32[32]{0:T(128)S(1)}, f32[32]{0:T(128)}, u32[]{:S(2)}) copy-start(f32[32]{0:T(128)} %param.16) | copy-start | bytes 388
  214.4 57.3 %copy-start = (f32[32,8,256]{2,1,0:T(8,128)S(1)}, f32[32,8,256]{2,1,0:T(8,128)}, u32[]{:S(2)}) copy-start(f32[32,8,256]{2,1,0:T(8,128)} %param.17) | copy-start | bytes 786436
  214.4 57.6 %copy-start.6 = (f32[32,8,256]{2,1,0:T(8,128)S(1)}, f32[32,8,256]{2,1,0:T(8,128)}, u32[]{:S(2)}) copy-start(f32[32,8,256]{2,1,0:T(8,128)} %param.12) | copy-start | bytes 786436
  214.4 13.3 %all-to-all-start.1 = ((f32[8,1,16384]{2,1,0:T(1,128)}), f32[8,1,16384]{2,1,0:T(1,128)S(1)}, u32[]{:S(2)}, u32[]{:S(2)}) async-start(f32[8,1,16384]{2,1,0:T(1,128)} %reshape.77), calls=%async_computation.1 | async-start | bytes 1048576 | tf_op jit(solution)/shard_map/all_to_all | solution.py:62
  218.1 74.3 %copy-start.23 = (pred[8]{0:T(512)(128)(4,1)}, pred[8]{0:T(512)(128)(4,1)S(1)}, u32[]{:S(2)}) copy-start(pred[8]{0:T(512)(128)(4,1)S(1)} %dynamic-slice_compare_fusion) | copy-start | bytes 28
  250.2 4.3 collective-permute-start.5
  250.6 6.1 %collective-permute-start.4 = (f32[2,32,1,256]{3,2,1,0:T(1,128)S(1)}, f32[2,32,1,256]{3,2,1,0:T(1,128)S(1)}, u32[]{:S(2)}, u32[]{:S(2)}) collective-permute-start(f32[2,32,1,256]{3,2,1,0:T(1,128)S(1)} %get-tuple-element.206), channel_id=1, source_target_pairs={{0,8},{8,16},{16,24},{24,0},{1,9},{9,17},{17,25},{25,1},{2,10},{10... | collective-permute-start | bytes 196616 | tf_op jit(solution)/shard_map/ppermute | solution.py:17
  257.2 11.9 %collective-permute-start.7 = (f32[2,32,10,1]{3,2,1,0:T(8,128)S(1)}, f32[2,32,10,1]{3,2,1,0:T(8,128)S(1)}, u32[]{:S(2)}, u32[]{:S(2)}) collective-permute-start(f32[2,32,10,1]{3,2,1,0:T(8,128)S(1)} %get-tuple-element.195), channel_id=1, source_target_pairs={{1,0},{2,1},{3,2},{4,3},{5,4},{6,5},{7,6},{0,7},{9,8},{10,9},{11,1... | collective-permute-start | bytes 7688 | tf_op jit(solution)/shard_map/ppermute | solution.py:20
  257.2 13.3 %collective-permute-start.6 = (f32[2,32,10,1]{3,2,1,0:T(8,128)S(1)}, f32[2,32,10,1]{3,2,1,0:T(8,128)S(1)}, u32[]{:S(2)}, u32[]{:S(2)}) collective-permute-start(f32[2,32,10,1]{3,2,1,0:T(8,128)S(1)} %get-tuple-element.194), channel_id=1, source_target_pairs={{0,1},{1,2},{2,3},{3,4},{4,5},{5,6},{6,7},{7,0},{8,9},{9,10},{10,1... | collective-permute-start | bytes 7688 | tf_op jit(solution)/shard_map/ppermute | solution.py:17
  294.5 29.2 %copy-start.7 = (f32[1,8,256]{2,1,0:T(8,128)}, f32[1,8,256]{2,1,0:T(8,128)S(1)}, u32[]{:S(2)}) copy-start(f32[1,8,256]{2,1,0:T(8,128)S(1)} %get-tuple-element.88) | copy-start | bytes 24580
  294.5 29.2 %copy-start.8 = (f32[1,8,256]{2,1,0:T(8,128)}, f32[1,8,256]{2,1,0:T(8,128)S(1)}, u32[]{:S(2)}) copy-start(f32[1,8,256]{2,1,0:T(8,128)S(1)} %get-tuple-element.89) | copy-start | bytes 24580
  294.5 29.2 %copy-start.9 = (f32[1,8,256]{2,1,0:T(8,128)}, f32[1,8,256]{2,1,0:T(8,128)S(1)}, u32[]{:S(2)}) copy-start(f32[1,8,256]{2,1,0:T(8,128)S(1)} %get-tuple-element.90) | copy-start | bytes 24580
  294.5 29.2 %copy-start.10 = (f32[1,8,256]{2,1,0:T(8,128)}, f32[1,8,256]{2,1,0:T(8,128)S(1)}, u32[]{:S(2)}) copy-start(f32[1,8,256]{2,1,0:T(8,128)S(1)} %get-tuple-element.91) | copy-start | bytes 24580
  294.5 29.2 %copy-start.11 = (f32[1,8,256]{2,1,0:T(8,128)}, f32[1,8,256]{2,1,0:T(8,128)S(1)}, u32[]{:S(2)}) copy-start(f32[1,8,256]{2,1,0:T(8,128)S(1)} %get-tuple-element.92) | copy-start | bytes 24580
  294.5 29.2 %copy-start.12 = (f32[1,8,256]{2,1,0:T(8,128)}, f32[1,8,256]{2,1,0:T(8,128)S(1)}, u32[]{:S(2)}) copy-start(f32[1,8,256]{2,1,0:T(8,128)S(1)} %get-tuple-element.93) | copy-start | bytes 24580
  294.5 29.2 %copy-start.13 = (f32[1,8,256]{2,1,0:T(8,128)}, f32[1,8,256]{2,1,0:T(8,128)S(1)}, u32[]{:S(2)}) copy-start(f32[1,8,256]{2,1,0:T(8,128)S(1)} %get-tuple-element.94) | copy-start | bytes 24580
  294.5 29.2 %copy-start.14 = (f32[1,8,256]{2,1,0:T(8,128)}, f32[1,8,256]{2,1,0:T(8,128)S(1)}, u32[]{:S(2)}) copy-start(f32[1,8,256]{2,1,0:T(8,128)S(1)} %get-tuple-element.95) | copy-start | bytes 24580
  294.5 29.2 %copy-start.15 = (f32[1,8,256]{2,1,0:T(8,128)}, f32[1,8,256]{2,1,0:T(8,128)S(1)}, u32[]{:S(2)}) copy-start(f32[1,8,256]{2,1,0:T(8,128)S(1)} %get-tuple-element.96) | copy-start | bytes 24580
  294.5 29.2 %copy-start.16 = (f32[1,8,256]{2,1,0:T(8,128)}, f32[1,8,256]{2,1,0:T(8,128)S(1)}, u32[]{:S(2)}) copy-start(f32[1,8,256]{2,1,0:T(8,128)S(1)} %get-tuple-element.97) | copy-start | bytes 24580
  294.5 29.2 %copy-start.17 = (f32[1,8,256]{2,1,0:T(8,128)}, f32[1,8,256]{2,1,0:T(8,128)S(1)}, u32[]{:S(2)}) copy-start(f32[1,8,256]{2,1,0:T(8,128)S(1)} %get-tuple-element.98) | copy-start | bytes 24580
  294.5 29.2 %copy-start.18 = (f32[1,8,256]{2,1,0:T(8,128)}, f32[1,8,256]{2,1,0:T(8,128)S(1)}, u32[]{:S(2)}) copy-start(f32[1,8,256]{2,1,0:T(8,128)S(1)} %get-tuple-element.99) | copy-start | bytes 24580
  294.6 29.2 %copy-start.19 = (f32[1,8,256]{2,1,0:T(8,128)}, f32[1,8,256]{2,1,0:T(8,128)S(1)}, u32[]{:S(2)}) copy-start(f32[1,8,256]{2,1,0:T(8,128)S(1)} %get-tuple-element.68) | copy-start | bytes 24580
  295.1 4.3 collective-permute-start.9
  295.5 5.7 collective-permute-start.8
  301.5 6.1 %collective-permute-start.11 = (f32[32,10,1]{2,1,0:T(8,128)S(1)}, f32[32,10,1]{2,1,0:T(8,128)S(1)}, u32[]{:S(2)}, u32[]{:S(2)}) collective-permute-start(f32[32,10,1]{2,1,0:T(8,128)S(1)} %get-tuple-element.205), channel_id=1, source_target_pairs={{1,0},{2,1},{3,2},{4,3},{5,4},{6,5},{7,6},{0,7},{9,8},{10,9},{11,1... | collective-permute-start | bytes 3848 | tf_op jit(solution)/shard_map/ppermute | solution.py:20
  301.5 8.3 %collective-permute-start.10 = (f32[32,10,1]{2,1,0:T(8,128)S(1)}, f32[32,10,1]{2,1,0:T(8,128)S(1)}, u32[]{:S(2)}, u32[]{:S(2)}) collective-permute-start(f32[32,10,1]{2,1,0:T(8,128)S(1)} %get-tuple-element.204), channel_id=1, source_target_pairs={{0,1},{1,2},{2,3},{3,4},{4,5},{5,6},{6,7},{7,0},{8,9},{9,10},{10,1... | collective-permute-start | bytes 3848 | tf_op jit(solution)/shard_map/ppermute | solution.py:17
  325.0 77.2 %copy-start.22 = (s32[2048]{0:T(1024)S(1)}, s32[2048]{0:T(1024)}, u32[]{:S(2)}) copy-start(s32[2048]{0:T(1024)} %copy-done.21) | copy-start | bytes 24580
  325.0 77.2 %copy-start.25 = (pred[2048]{0:T(1024)(128)(4,1)S(1)}, pred[2048]{0:T(1024)(128)(4,1)}, u32[]{:S(2)}) copy-start(pred[2048]{0:T(1024)(128)(4,1)} %copy-done.24) | copy-start | bytes 6148
  538.4 5.0 collective-permute-start.13
  538.7 6.1 %collective-permute-start.12 = (f32[2,32,1,256]{3,2,0,1:T(1,128)S(1)}, f32[2,32,1,256]{3,2,0,1:T(1,128)S(1)}, u32[]{:S(2)}, u32[]{:S(2)}) collective-permute-start(f32[2,32,1,256]{3,2,0,1:T(1,128)S(1)} %get-tuple-element.200), channel_id=1, source_target_pairs={{0,8},{8,16},{16,24},{24,0},{1,9},{9,17},{17,25},{25,1},{2,10},{10... | collective-permute-start | bytes 196616 | tf_op jit(solution)/shard_map/ppermute | solution.py:17
  545.2 12.1 %collective-permute-start.15 = (f32[2,32,10,1]{3,2,0,1:T(8,128)S(1)}, f32[2,32,10,1]{3,2,0,1:T(8,128)S(1)}, u32[]{:S(2)}, u32[]{:S(2)}) collective-permute-start(f32[2,32,10,1]{3,2,0,1:T(8,128)S(1)} %get-tuple-element.193), channel_id=1, source_target_pairs={{1,0},{2,1},{3,2},{4,3},{5,4},{6,5},{7,6},{0,7},{9,8},{10,9},{11,1... | collective-permute-start | bytes 7688 | tf_op jit(solution)/shard_map/ppermute | solution.py:20
  545.3 13.3 %collective-permute-start.14 = (f32[2,32,10,1]{3,2,0,1:T(8,128)S(1)}, f32[2,32,10,1]{3,2,0,1:T(8,128)S(1)}, u32[]{:S(2)}, u32[]{:S(2)}) collective-permute-start(f32[2,32,10,1]{3,2,0,1:T(8,128)S(1)} %get-tuple-element.192), channel_id=1, source_target_pairs={{0,1},{1,2},{2,3},{3,4},{4,5},{5,6},{6,7},{7,0},{8,9},{9,10},{10,1... | collective-permute-start | bytes 7688 | tf_op jit(solution)/shard_map/ppermute | solution.py:17
  584.0 0.8 copy-start.5
where the time goes:
time: 589 us; the launch traced here: 585 us
  matrix products  318 us (54%)
  local copies, waits for them, and re-layouts  82 us (14%)
  waiting for transfers between devices  74.9 us (13%)
  other arithmetic  61.9 us (11%)
  blocking collectives  25.1 us (4%)
  starting transfers between devices  21.6 us (4%)
    dot_general x2, matrix products, transform_band(): jnp.einsum('vetc,cj->vetj', scaled, inverse, precision=lax.Precision.HIGH...  165 us
    dot_general x2, matrix products, transform_band(): jnp.einsum('vetj,jc->vetc', circles, forward, precision=lax.Precision.HIG...  153 us
    unnamed x129, local copies, waits for them, and re-layouts  50.8 us
    div x2, other arithmetic, column_solve(): prev_value = (rhs + below * prev_value) / pivot  41.1 us
    ppermute x8, waiting for transfers between devices, extended(): lax.ppermute(lax.slice_in_dim(block, 0, width, axis=dim), axis, backward)  39.1 us
    ppermute x8, waiting for transfers between devices, extended(): lax.ppermute(lax.slice_in_dim(block, block.shape[dim] - width, None, axis...  16.8 us
    all_to_all x3, local copies, waits for them, and re-layouts, transform_band(): lax.all_to_all(damped, 'lon', split_axis=3, concat_axis=1, tiled=True)  13.9 us
    all_to_all x1, blocking collectives, transform_band(): lax.all_to_all(damped, 'lon', split_axis=3, concat_axis=1, tiled=True)  12.8 us
  transfers between devices with their start and end apart: 18, of which 17 were waited for; matrix products, arithmetic and copies ran while one was open for 1% of the time, Pallas kernels for 0%

commit v1 on v0

v1 whole, which is shorter than its diff:
```python
import functools
import math

import jax
import jax.numpy as jnp
import numpy as np
from jax import lax
from jax.experimental import pallas as pl
from jax.experimental.pallas import tpu as pltpu
from jax.sharding import PartitionSpec as P

SUBSTEPS = 2
LANES = 128
F32 = jnp.float32
BF16 = jnp.bfloat16


def cmul_const(re, im, cr, ci):
    if im is None:
        return (re * cr if cr != 0.0 else None, re * ci if ci != 0.0 else None)
    return (re * cr - im * ci, re * ci + im * cr)


def add(a, b):
    if a is None:
        return b
    return a if b is None else a + b


def sub(a, b):
    if b is None:
        return a
    return -b if a is None else a - b


def neg(a):
    return None if a is None else -a


def unit(num, den):
    turn = num % den
    table = {0: (1.0, 0.0), den / 4: (0.0, 1.0), den / 2: (-1.0, 0.0), 3 * den / 4: (0.0, -1.0)}
    if turn in table:
        return table[turn]
    angle = 2.0 * math.pi * turn / den
    return math.cos(angle), math.sin(angle)


def rotate(z, num, den):
    cr, ci = unit(num, den)
    re, im = z
    if (cr, ci) == (1.0, 0.0):
        return z
    if (cr, ci) == (0.0, 1.0):
        return (neg(im), re)
    if (cr, ci) == (0.0, -1.0):
        return (im, neg(re))
    return cmul_const(re, im, cr, ci)


def real_dft(pieces):
    n = len(pieces)
    if n == 1:
        return [(pieces[0], None)]
    even, odd = real_dft(pieces[0::2]), real_dft(pieces[1::2])
    out = [None] * (n // 2 + 1)
    for s in range(n // 4 + 1 if n > 2 else 1):
        er, ei = even[s]
        tr, ti = rotate(odd[s], -s, n)
        out[n // 2 - s] = (sub(er, tr), sub(ti, ei))
        out[s] = (add(er, tr), add(ei, ti))
    return out


def real_dft_inverse(groups):
    n = 2 * (len(groups) - 1)
    if n == 0:
        return [groups[0][0]]
    if n == 2:
        a, b = groups[0][0], groups[1][0]
        return [a + b, a - b]
    even, odd = [], []
    for s in range(n // 4 + 1):
        ar, ai = groups[s]
        br, bi = groups[n // 2 - s]
        even.append((add(ar, br), sub(ai, bi)))
        odd.append(rotate((sub(ar, br), add(ai, bi)), s, n))
    if True:
        even[0] = (even[0][0], None)
        odd[0] = (odd[0][0], None)
        even[-1] = (even[-1][0], None)
        odd[-1] = (odd[-1][0], None)
    out = [None] * n
    out[0::2] = real_dft_inverse(even)
    out[1::2] = real_dft_inverse(odd)
    return out


def tables(length):
    pieces = length // LANES
    groups = pieces // 2 + 1
    lane = np.arange(LANES)
    angle = 2.0 * np.pi / LANES * (np.outer(lane, lane) % LANES)
    cos, sin = np.cos(angle), np.sin(angle)
    matrix = np.block([[cos, -sin], [sin, cos]])

    def halves(m):
        m = m.astype(np.float32)
        high = m.astype(BF16)
        return np.stack([high, (m - high.astype(np.float32)).astype(BF16)])

    weights = np.stack([halves(matrix), halves(matrix.T)])
    s = np.arange(groups)[:, None]
    turn = 2.0 * np.pi / length * (s * lane[None, :])
    wavenum = pieces * lane[None, :] + s
    wavenum = np.minimum(wavenum, length - wavenum).astype(np.float64)
    slope = 2.0 * np.sin(2.0 * np.pi / length * (pieces * lane[None, :] + s))
    rows = np.stack([np.cos(turn), np.sin(turn), wavenum, 1.0 / np.maximum(wavenum, 1.0) ** 2, slope])
    return weights, rows.astype(np.float32)


def transform_kernel(plan, full, x_ref, coef_ref, weight_ref, table_ref, *refs):
    outs, (lhs_ref, spec_ref, work_ref) = refs[:-3], refs[-3:]
    stacks, stack_step, nl, piece_step, skip, band = plan
    _, tall, width = x_ref.shape
    per = width // LANES
    pieces = nl * per
    groups = pieces // 2 + 1
    rows = stacks * tall
    length = pieces * LANES

    def block(stack, l):
        return stack * stack_step + l * piece_step

    def product(which, count):
        total = jnp.dot(lhs_ref[0, :count], weight_ref[which, 0], preferred_element_type=F32)
        total += jnp.dot(lhs_ref[1, :count], weight_ref[which, 0], preferred_element_type=F32)
        return total + jnp.dot(lhs_ref[0, :count], weight_ref[which, 1], preferred_element_type=F32)

    def put(row, re, im):
        for half, part in enumerate((re, im)):
            high = part.astype(BF16)
            low = (part - high.astype(F32)).astype(BF16)
            lhs_ref[0, row:row + rows, half * LANES:(half + 1) * LANES] = high
            lhs_ref[1, row:row + rows, half * LANES:(half + 1) * LANES] = low

    chunks = []
    for l in range(nl):
        for h in range(per):
            chunks.append(jnp.concatenate([x_ref[block(z, l), :, h * LANES:(h + 1) * LANES] for z in range(stacks)], axis=0))
    zero = jnp.zeros((rows, LANES), F32)
    for s, (re, im) in enumerate(real_dft(chunks)):
        if s:
            cr, ci = table_ref[0, s:s + 1], table_ref[1, s:s + 1]
            if im is None:
                re, im = re * cr, -re * ci
            else:
                re, im = re * cr + im * ci, im * cr - re * ci
        put(s * rows, re, zero if im is None else im)
    spec_ref[...] = product(0, groups * rows)

    limit, has_up, has_down, zonal2, merid, merid_up, merid_down = (coef_ref[i] for i in range(7))
    limit2 = limit * limit

    def above(a):
        return pltpu.roll(a, rows - 1, 0)

    def below(a):
        return pltpu.roll(a, 1, 0)

    for s in range(groups):
        wavenum, inverse2, slope = (table_ref[i, s:s + 1] for i in (2, 3, 4))
        factor = jnp.where(wavenum > limit, limit2 * inverse2, 1.0)
        parts = [spec_ref[s * rows:(s + 1) * rows, half * LANES:(half + 1) * LANES] for half in (0, 1)]
        zonal = zonal2 * (slope * slope)
        filtered = [factor * part for part in parts]
        merids, divs = [], []
        for part, filt in zip(parts, filtered):
            across = factor * (has_up * above(part) - has_down * below(part))
            flux = merid * across
            merids.append(across)
            divs.append(zonal * filt - merid_up * above(flux) + merid_down * below(flux))
        put(s * rows, *divs)
        if full:
            put((groups + s) * rows, -slope * filtered[1], slope * filtered[0])
            put((2 * groups + s) * rows, *merids)

    count = (3 if full else 1) * groups * rows
    work_ref[...] = product(1, count)
    for field in range(3 if full else 1):
        spectrum = []
        for s in range(groups):
            base = (field * groups + s) * rows
            re = work_ref[base:base + rows, :LANES]
            im = work_ref[base:base + rows, LANES:]
            if s:
                cr, ci = table_ref[0, s:s + 1], table_ref[1, s:s + 1]
                re, im = re * cr - im * ci, (None if s == groups - 1 else re * ci + im * cr)
            else:
                im = None
            spectrum.append((re, im))
        result = real_dft_inverse(spectrum)
        target, offset = (outs[0], 0) if field == 0 else (outs[1], (field - 1) * band)
        for l in range(nl):
            for h in range(per):
                piece = result[l * per + h] * (1.0 / length)
                for z in range(stacks):
                    first = z * tall + skip
                    target[block(z, l), offset:offset + band, h * LANES:(h + 1) * LANES] = piece[first:first + band]


def transform(x, coefs, weights, table, plan, full):
    blocks, tall, width = x.shape
    band = plan[5]
    rows = plan[0] * tall
    groups = table.shape[1]
    count = (3 if full else 1) * groups * rows
    shapes = [jax.ShapeDtypeStruct((blocks, band, width), F32)]
    if full:
        shapes.append(jax.ShapeDtypeStruct((blocks, 2 * band, width), F32))
    return pl.pallas_call(
        functools.partial(transform_kernel, plan, full),
        out_shape=shapes,
        scratch_shapes=[
            pltpu.VMEM((2, count, 2 * LANES), BF16),
            pltpu.VMEM((groups * rows, 2 * LANES), F32),
            pltpu.VMEM((count, 2 * LANES), F32),
        ],
        cost_estimate=pl.CostEstimate(flops=6 * 2 * 65536 * count, bytes_accessed=8 * x.size, transcendentals=0),
        name="transform_all" if full else "transform_div",
    )(x, coefs, weights, table)


def factor_kernel(level_ref, sound_ref, inv_ref, carry_ref, ratio_ref):
    levels = sound_ref.shape[0]
    prev = jnp.zeros(sound_ref.shape[1:], F32)
    for k in range(levels):
        alpha = level_ref[k]
        below = alpha * sound_ref[k]
        above = alpha * sound_ref[k + 1] if k + 1 < levels else jnp.zeros_like(below)
        inv = 1.0 / (1.0 + below + above + below * prev)
        prev = -above * inv
        inv_ref[k] = inv
        carry_ref[k] = below * inv
        ratio_ref[k] = prev


def factor(level_coef, sound):
    shape = jax.ShapeDtypeStruct(sound.shape, F32)
    return pl.pallas_call(
        factor_kernel,
        in_specs=[pl.BlockSpec(memory_space=pltpu.SMEM), pl.BlockSpec(memory_space=pltpu.VMEM)],
        out_shape=[shape] * 3,
        cost_estimate=pl.CostEstimate(flops=10 * sound.size, bytes_accessed=16 * sound.size, transcendentals=0),
        name="factor_columns",
    )(level_coef, sound)


def column_kernel(first, level_ref, sound_ref, inv_ref, carry_ref, ratio_ref, base_ref, div_ref, p_ref, w_ref, *outs):
    w_out, p_out = outs[0], outs[1]
    levels = sound_ref.shape[0]

    def star(k):
        return p_ref[k] - sound_ref[k] * (base_ref[k] + div_ref[k])

    here = star(0)
    value = None
    for k in range(levels):
        alpha = level_ref[k]
        p_out[k] = here
        if k + 1 < levels:
            upper = star(k + 1)
            rhs = w_ref[k] - alpha * (upper - here)
            here = upper
        else:
            rhs = w_ref[k] + alpha * here
        scaled = rhs * inv_ref[k]
        value = scaled if value is None else scaled + carry_ref[k] * value
        w_out[k] = value
    upper = w_out[levels - 1]
    for k in range(levels - 1, -1, -1):
        lower = w_out[k - 1] - ratio_ref[k - 1] * upper if k else None
        if k:
            w_out[k - 1] = lower
        fresh = p_out[k] - sound_ref[k] * (upper if lower is None else upper - lower)
        p_out[k] = fresh
        if first:
            outs[2][k] = p_ref[k] + fresh
        upper = lower


def column(level_coef, sound, factors, base, div, p, w, first):
    shape = jax.ShapeDtypeStruct(sound.shape, F32)
    return pl.pallas_call(
        functools.partial(column_kernel, first),
        in_specs=[pl.BlockSpec(memory_space=pltpu.SMEM)] + [pl.BlockSpec(memory_space=pltpu.VMEM)] * 8,
        out_shape=[shape] * (3 if first else 2),
        cost_estimate=pl.CostEstimate(flops=20 * sound.size, bytes_accessed=40 * sound.size, transcendentals=0),
        name="column_first" if first else "column_last",
    )(level_coef, sound, *factors, base, div, p, w)


def shifted(block, axis, step):
    count = lax.axis_size(axis)
    return lax.ppermute(block, axis, [(i, (i + step) % count) for i in range(count)])


def exchange(block, axes):
    return lax.all_to_all(block, axes, split_axis=0, concat_axis=0, tiled=True)


def lat_edges(last, first):
    count = lax.axis_size("lat")
    low = lax.ppermute(last, "lat", [(i, i + 1) for i in range(count - 1)])
    high = lax.ppermute(first, "lat", [(i + 1, i) for i in range(count - 1)])
    return low, high


def latitude_data(zonal_coef, merid_coef, merid_wind, halo):
    levels, band, width = merid_wind.shape
    nz, me = lax.axis_size("lat"), lax.axis_index("lat")
    if halo:
        v_low, v_high = lat_edges(merid_wind[:, -1], merid_wind[:, 0])
        own = jnp.stack([zonal_coef, merid_coef])
        low, high = lat_edges(own[:, -halo:], own[:, :halo])
        zonal, merid = jnp.concatenate([low, own, high], axis=1)
        return zonal, merid, v_low, v_high
    target = lax.broadcasted_iota(jnp.int32, (nz, 1, 1), 0)
    edges = jnp.where(target == me + 1, merid_wind[None, :, band - 1], 0.0)
    edges = jnp.where(target == me - 1, merid_wind[None, :, 0], edges)
    own = jnp.concatenate([zonal_coef, merid_coef])
    own = jnp.broadcast_to(jnp.pad(own, (0, width - 2 * band)), (nz, 8, width))
    sent = jnp.concatenate([edges, own], axis=1).reshape(nz * (levels + 8), width)
    got = exchange(sent, "lat").reshape(nz, levels + 8, width)
    padded = jnp.pad(got[:, :levels], ((1, 1), (0, 0), (0, 0)))
    v_low = lax.dynamic_index_in_dim(padded, me, 0, keepdims=False)
    v_high = lax.dynamic_index_in_dim(padded, me + 2, 0, keepdims=False)
    zonal = got[:, levels, :band].reshape(nz * band)
    merid = got[:, levels, band:2 * band].reshape(nz * band)
    return zonal, merid, v_low, v_high


def body(
    zonal_wind,
    merid_wind,
    vertical_wind,
    pressure,
    zonal_coef,
    merid_coef,
    level_coef,
    sound_coef,
    cutoff,
    filter_mask,
):
    levels, band, width = pressure.shape
    nz, nl = lax.axis_size("lat"), lax.axis_size("lon")
    length = width * nl
    lats = band * nz
    me = lax.axis_index("lat")
    both = ("lat", "lon")
    weights, table = tables(length)

    if levels % (nz * nl) == 0:
        axes, halo, tall = both, 0, band
        depth = levels // (nz * nl)
        plan = (nz * depth, 1, nl, depth, 0, band)
        if depth == 1:
            plan = (nz, nl, nl, 1, 0, band)
    else:
        axes, halo, tall = "lon", 2, -(-(band + 4) // 8) * 8
        depth = levels // nl
        plan = (depth, 1, nl, depth, 2, band)

    def spread(field):
        if halo:
            low, high = lat_edges(field[:, -halo:], field[:, :halo])
            field = jnp.concatenate([low, field, high], axis=1)
            field = jnp.pad(field, ((0, 0), (0, tall - band - 2 * halo), (0, 0)))
        return exchange(field, axes)

    circles = spread(pressure)

    zonal_all, merid_all, v_low, v_high = latitude_data(zonal_coef, merid_coef, merid_wind, halo)
    row = jnp.arange(lats + 2 * halo) - halo
    has_up = (row < lats - 1).astype(F32)
    has_down = (row > 0).astype(F32)
    limit = jnp.pad(jnp.where(filter_mask > 0, cutoff, length).astype(F32), (halo, halo), constant_values=1.0)
    coefs = jnp.stack([limit, has_up, has_down])
    if halo:
        coefs = lax.dynamic_slice_in_dim(coefs, me * band, band + 2 * halo, 1)
    coefs = jnp.concatenate([coefs, (zonal_all * zonal_all)[None], merid_all[None], merid_all * coefs[1:3]])
    if halo:
        coefs = jnp.tile(jnp.pad(coefs, ((0, 0), (0, tall - band - 2 * halo))), (1, depth))
    coefs = jnp.broadcast_to(coefs[:, :, None], coefs.shape + (LANES,))

    u_low = shifted(zonal_wind[:, :, -1:], "lon", 1)
    u_high = shifted(zonal_wind[:, :, :1], "lon", -1)
    zonal_rows, merid_rows = zonal_coef[None, :, None], merid_coef[None, :, None]
    u_diff = jnp.concatenate([zonal_wind[:, :, 1:], u_high], 2) - jnp.concatenate([u_low, zonal_wind[:, :, :-1]], 2)
    v_diff = jnp.concatenate([merid_wind[:, 1:], v_high[:, None]], 1) - jnp.concatenate([v_low[:, None], merid_wind[:, :-1]], 1)
    base = zonal_rows * u_diff + merid_rows * v_diff

    factors = factor(level_coef, sound_coef)

    (div,) = transform(circles, coefs, weights, table, plan, False)
    div = exchange(div, axes)
    w, p, total = column(level_coef, sound_coef, factors, base, div, pressure, vertical_wind, True)
    div, winds = transform(spread(total), coefs, weights, table, plan, True)
    div = exchange(div, axes)
    winds = exchange(winds, axes)
    w, p = column(level_coef, sound_coef, factors, base, div, p, w, False)
    u = zonal_wind - zonal_rows * winds[:, :band]
    v = merid_wind - merid_rows * winds[:, band:]
    return (u, v, w, p)


def solution(mesh):
    spec = P(None, "lat", "lon")
    in_specs = (spec, spec, spec, spec, P("lat"), P("lat"), P(), spec, P(), P())
    return jax.shard_map(body, mesh=mesh, in_specs=in_specs, out_specs=(spec,) * 4, check_vma=False)
```

time: 589 us -> 102 us (0.17)
  matrix products: 318 us -> 0 us
  local copies, waits for them, and re-layouts: 82 us -> 3.81 us
  other arithmetic: 61.9 us -> 2.76 us
  waiting for transfers between devices: 74.9 us -> 35.2 us
  Pallas kernels: 0 us -> 13.3 us
    dot_general x4 -> x0, matrix products: 318 us -> none  [the longest x2 165 us: transform_band(): jnp.einsum('vetc,cj->vetj', scaled, inverse, precision=lax.Precision.HIGH...]
    ppermute x16 -> x2, waiting for transfers between devices: 55.9 us -> 0.01 us  [shifted(): lax.ppermute(block, axis, [(i, (i + step) % count) for i in range(count)])]
    unnamed x129 -> x16, local copies, waits for them, and re-layouts: 50.8 us -> 1.37 us
    div x2 -> x0, other arithmetic: 41.1 us -> none  [column_solve(): prev_value = (rhs + below * prev_value) / pivot]
    all_to_all x2 -> x4, waiting for transfers between devices: 19 us -> 35.2 us  [exchange(): return lax.all_to_all(block, axes, split_axis=0, concat_axis=0, tiled=True)]
    all_to_all x7 -> x0, local copies, waits for them, and re-layouts: 15.5 us -> none  [the longest x3 13.9 us: transform_band(): lax.all_to_all(damped, 'lon', split_axis=3, concat_axis=1, tiled=True)]
    pallas_call x0 -> x5, Pallas kernels: none -> 13.3 us  [the longest x2 6.16 us: transform(): pl.pallas_call(functools.partial(transform_kernel, plan, full), out_shape...]
    ppermute x16 -> x2, starting transfers between devices: 14.2 us -> 1.66 us  [shifted(): lax.ppermute(block, axis, [(i, (i + step) % count) for i in range(count)])]
  transfers between devices with their start and end apart: 18 -> 6, of which waited for: 17 -> 4; matrix products, arithmetic and copies ran while one was open for 1% -> 2% of each run, Pallas kernels for 0% -> 7%
where the time goes in v1:
time: 102 us; the launch traced here: 101 us
  waiting for transfers between devices  35.2 us (35%)
  blocking collectives  27.7 us (27%)
  starting transfers between devices  17.2 us (17%)
  Pallas kernels  13.3 us (13%)
  local copies, waits for them, and re-layouts  3.81 us (4%)
  other arithmetic  2.76 us (3%)
    all_to_all x4, waiting for transfers between devices, exchange(): return lax.all_to_all(block, axes, split_axis=0, concat_axis=0, tiled=True)  35.2 us
    all_to_all x2, blocking collectives, exchange(): return lax.all_to_all(block, axes, split_axis=0, concat_axis=0, tiled=True)  27.7 us
    all_to_all x4, starting transfers between devices, exchange(): return lax.all_to_all(block, axes, split_axis=0, concat_axis=0, tiled=True)  15.6 us
    pallas_call x2, Pallas kernels, transform(): pl.pallas_call(functools.partial(transform_kernel, plan, full), out_shape...  6.16 us
    pallas_call x2, Pallas kernels, column(): pl.pallas_call(functools.partial(column_kernel, first), in_specs=[pl.Bloc...  5.01 us
    pallas_call x1, Pallas kernels, factor(): pl.pallas_call(factor_kernel, in_specs=[pl.BlockSpec(memory_space=pltpu.S...  2.12 us
  transfers between devices with their start and end apart: 6, of which 4 were waited for; matrix products, arithmetic and copies ran while one was open for 2% of the time, Pallas kernels for 7%

profile of v1, /device:TPU:0, one launch (start us, length us, event | category | flops | bytes accessed | tf_op | source)
XLA Modules:
  0.0 100.9 jit_solution(4909371809819989832)
XLA Ops:
  0.6 1.1 %fusion.9 = (f32[32,1,256]{2,1,0:T(1,128)S(1)}, f32[32,1,256]{2,1,0:T(1,128)S(1)}) fusion(f32[32,8,256]{2,1,0:T(8,128)} %param.13), kind=kLoop, calls=%fused_computation.28 | loop fusion | bytes 131072 | tf_op jit(solution)/shard_map/slice | solution.py:330
  1.7 0.0 copy-start.4
  1.7 0.0 copy-start.5
  1.8 0.6 copy-done.4
  2.4 0.0 copy-done.5
  2.4 0.1 select_maximum_fusion
  2.5 0.1 select_select_fusion
  2.6 0.0 copy-start
  2.6 0.7 pad_maximum_fusion
  3.3 6.3 %all-to-all-start = ((f32[4,40,256]{2,1,0:T(8,128)}), f32[4,40,256]{2,1,0:T(8,128)S(1)}, u32[]{:S(2)}, u32[]{:S(2)}) async-start(f32[4,40,256]{2,1,0:T(8,128)} %pad_maximum_fusion), calls=%async_computation | async-start | bytes 327680 | tf_op jit(solution)/shard_map/all_to_all | solution.py:309
  9.6 0.0 copy-done
  9.6 0.0 copy-start.6
  9.6 0.0 copy-start.7
  9.6 0.1 fusion.10
  9.7 0.0 copy-start.1
  9.7 1.7 %collective-permute-start = (f32[32,8,1]{2,1,0:T(8,128)S(1)}, f32[32,8,1]{2,1,0:T(8,128)S(1)}, u32[]{:S(2)}, u32[]{:S(2)}) collective-permute-start(f32[32,8,1]{2,1,0:T(8,128)S(1)} %get-tuple-element.33), channel_id=1, source_target_pairs={{0,7},{1,0},{2,1},{3,2},{4,3},{5,4},{6,5},{7,6},{8,15},{9,8},{10,9... | collective-permute-start | bytes 3080 | tf_op jit(solution)/shard_map/ppermute | solution.py:305
  11.4 0.0 collective-permute-start.1
  11.4 0.0 copy-done.6
  11.4 0.0 copy-done.7
  11.4 2.1 %factor_columns.1 = (f32[32,8,256]{2,1,0:T(8,128)}, f32[32,8,256]{2,1,0:T(8,128)}, f32[32,8,256]{2,1,0:T(8,128)}) custom-call(f32[32]{0:T(128)} %level_ref.5, f32[32,8,256]{2,1,0:T(8,128)} %sound_ref.5), custom_call_target="tpu_custom_call" | custom-call | flops 655360 | bytes 1048576 | tf_op jit(solution)/shard_map/factor_columns/pallas_call | solution.py:250
  13.5 0.0 copy-done.1
  13.6 2.5 %all-to-all-done = f32[4,40,256]{2,1,0:T(8,128)S(1)} async-done(((f32[4,40,256]{2,1,0:T(8,128)}), f32[4,40,256]{2,1,0:T(8,128)S(1)}, u32[]{:S(2)}, u32[]{:S(2)}) %all-to-all-start) | async-done | bytes 163872 | tf_op jit(solution)/shard_map/all_to_all | solution.py:309
  16.0 4.0 %all-to-all-start.1 = ((f32[32,8,256]{2,1,0:T(8,128)}), f32[32,8,256]{2,1,0:T(8,128)S(1)}, u32[]{:S(2)}, u32[]{:S(2)}) async-start(f32[32,8,256]{2,1,0:T(8,128)} %p_ref.1), calls=%async_computation.1 | async-start | bytes 524288 | tf_op jit(solution)/shard_map/all_to_all | solution.py:309
  20.1 0.1 slice_reduce_fusion
  20.2 0.1 mul.57
  20.3 0.1 broadcast_in_dim_reshape_squeeze.4
  20.4 0.1 mul.56
  20.5 10.2 %all-to-all-done.1.x_ref = f32[32,8,256]{2,1,0:T(8,128)S(1)} async-done(((f32[32,8,256]{2,1,0:T(8,128)}), f32[32,8,256]{2,1,0:T(8,128)S(1)}, u32[]{:S(2)}, u32[]{:S(2)}) %all-to-all-start.1) | async-done | bytes 262176 | tf_op jit(solution)/shard_map/all_to_all | solution.py:309
  30.7 0.0 copy-start.3
  30.7 0.7 broadcast_in_dim.73.coef_ref
  31.4 0.0 copy-done.3
  31.4 2.8 %transform_div.1 = f32[32,8,256]{2,1,0:T(8,128)} custom-call(f32[32,8,256]{2,1,0:T(8,128)} %copy-done.3, f32[7,32,128]{2,1,0:T(8,128)} %broadcast_in_dim.73.coef_ref, bf16[2,2,256,256]{3,2,1,0:T(8,128)(2,1)} %constant.35.clone.weight_ref, f32[5,9,128]{2,1,0:T(8,128)} %constant.36.clone.table_ref), custom_call_target="tpu_custom_call" | custom-call | flops 226492416 | bytes 524288 | tf_op jit(solution)/shard_map/transform_div/pallas_call | solution.py:221
  34.3 2.6 %all-to-all-start.2 = ((f32[32,8,256]{2,1,0:T(8,128)}), f32[32,8,256]{2,1,0:T(8,128)S(1)}, u32[]{:S(2)}, u32[]{:S(2)}) async-start(f32[32,8,256]{2,1,0:T(8,128)} %transform_div.1), calls=%async_computation.2 | async-start | bytes 524288 | tf_op jit(solution)/shard_map/all_to_all | solution.py:309
  36.9 0.1 fusion.11
  37.1 0.0 collective-permute-done
  37.1 0.0 collective-permute-done.1
  37.1 0.9 fusion.3.base_ref
  38.0 9.4 %all-to-all-done.2.div_ref = f32[32,8,256]{2,1,0:T(8,128)S(1)} async-done(((f32[32,8,256]{2,1,0:T(8,128)}), f32[32,8,256]{2,1,0:T(8,128)S(1)}, u32[]{:S(2)}, u32[]{:S(2)}) %all-to-all-start.2) | async-done | bytes 262176 | tf_op jit(solution)/shard_map/all_to_all | solution.py:309
  47.4 0.0 copy-start.2
  47.4 0.7 copy-done.2
  48.1 2.5 %column_first.1 = (f32[32,8,256]{2,1,0:T(8,128)}, f32[32,8,256]{2,1,0:T(8,128)}, f32[32,8,256]{2,1,0:T(8,128)}) custom-call(f32[32]{0:T(128)} %level_ref.5, f32[32,8,256]{2,1,0:T(8,128)} %sound_ref.5, f32[32,8,256]{2,1,0:T(8,128)} %get-tuple-element.14.inv_ref, f32[32,8,256]{2,1,0:T(8,128)} %get-tuple-element.15.carry_ref, ...), custom_call_target="tpu_custom_call" | custom-call | flops 1310720 | bytes 2621440 | tf_op jit(solution)/shard_map/column_first/pallas_call | solution.py:294
  50.7 13.9 %all_to_all.31.x_ref = f32[32,8,256]{2,1,0:T(8,128)} all-to-all(f32[32,8,256]{2,1,0:T(8,128)} %get-tuple-element.17), channel_id=1, replica_groups=mesh['lat'=4,'lon'=8] {'lat','lon'}, dimensions={0} | all-to-all | bytes 524288 | tf_op jit(solution)/shard_map/all_to_all | solution.py:309
  64.5 3.3 %transform_all.1 = (f32[32,8,256]{2,1,0:T(8,128)}, f32[32,16,256]{2,1,0:T(8,128)}) custom-call(f32[32,8,256]{2,1,0:T(8,128)} %all_to_all.31.x_ref, f32[7,32,128]{2,1,0:T(8,128)} %broadcast_in_dim.73.coef_ref, bf16[2,2,256,256]{3,2,1,0:T(8,128)(2,1)} %constant.35.clone.weight_ref, f32[5,9,128]{2,1,0:T(8,128)} %constant.36.clone.table_ref), custom_call_target="tpu_custom_call" | custom-call | flops 679477248 | bytes 524288 | tf_op jit(solution)/shard_map/transform_all/pallas_call | solution.py:221
  67.9 13.9 %all_to_all.32.div_ref = f32[32,8,256]{2,1,0:T(8,128)} all-to-all(f32[32,8,256]{2,1,0:T(8,128)} %get-tuple-element.19), channel_id=1, replica_groups=mesh['lat'=4,'lon'=8] {'lat','lon'}, dimensions={0} | all-to-all | bytes 524288 | tf_op jit(solution)/shard_map/all_to_all | solution.py:309
  81.7 2.6 %all-to-all-start.4 = ((f32[32,16,256]{2,1,0:T(8,128)}), f32[32,16,256]{2,1,0:T(8,128)S(1)}, u32[]{:S(2)}, u32[]{:S(2)}) async-start(f32[32,16,256]{2,1,0:T(8,128)} %get-tuple-element.18), calls=%async_computation.4 | async-start | bytes 1048576 | tf_op jit(solution)/shard_map/all_to_all | solution.py:309
  84.3 2.5 %column_last.1 = (f32[32,8,256]{2,1,0:T(8,128)}, f32[32,8,256]{2,1,0:T(8,128)}) custom-call(f32[32]{0:T(128)} %level_ref.5, f32[32,8,256]{2,1,0:T(8,128)} %sound_ref.5, f32[32,8,256]{2,1,0:T(8,128)} %get-tuple-element.14.inv_ref, f32[32,8,256]{2,1,0:T(8,128)} %get-tuple-element.15.carry_ref, f32[32,8,256]{2,1,0:T(8,128)} %get-tuple-element.16.ratio_ref, ...), custom_call_target="tpu_custom_call" | custom-call | flops 1310720 | bytes 2621440 | tf_op jit(solution)/shard_map/column_last/pallas_call | solution.py:294
  86.8 13.2 %all-to-all-done.4 = f32[32,16,256]{2,1,0:T(8,128)S(1)} async-done(((f32[32,16,256]{2,1,0:T(8,128)}), f32[32,16,256]{2,1,0:T(8,128)S(1)}, u32[]{:S(2)}, u32[]{:S(2)}) %all-to-all-start.4) | async-done | bytes 524320 | tf_op jit(solution)/shard_map/all_to_all | solution.py:309
  100.0 0.9 fusion
  (12 shorter events, 0.2 us)
Async XLA Ops:
  1.7 0.7 copy-start.4
  1.7 0.7 copy-start.5
  2.6 7.0 %copy-start = (f32[32,8,256]{2,1,0:T(8,128)S(1)}, f32[32,8,256]{2,1,0:T(8,128)}, u32[]{:S(2)}) copy-start(f32[32,8,256]{2,1,0:T(8,128)} %param.12) | copy-start | bytes 786436
  3.3 12.8 %all-to-all-start = ((f32[4,40,256]{2,1,0:T(8,128)}), f32[4,40,256]{2,1,0:T(8,128)S(1)}, u32[]{:S(2)}, u32[]{:S(2)}) async-start(f32[4,40,256]{2,1,0:T(8,128)} %pad_maximum_fusion), calls=%async_computation | async-start | bytes 327680 | tf_op jit(solution)/shard_map/all_to_all | solution.py:309
  9.6 1.8 %copy-start.6 = (s32[32]{0:T(128)S(1)}, s32[32]{0:T(128)}, u32[]{:S(2)}) copy-start(s32[32]{0:T(128)} %param.20) | copy-start | bytes 388
  9.6 1.8 %copy-start.7 = (s32[32]{0:T(128)S(1)}, s32[32]{0:T(128)}, u32[]{:S(2)}) copy-start(s32[32]{0:T(128)} %param.21) | copy-start | bytes 388
  9.7 3.8 %copy-start.1 = (f32[32,8,256]{2,1,0:T(8,128)S(1)}, f32[32,8,256]{2,1,0:T(8,128)}, u32[]{:S(2)}) copy-start(f32[32,8,256]{2,1,0:T(8,128)} %param.13) | copy-start | bytes 786436
  9.7 27.4 %collective-permute-start = (f32[32,8,1]{2,1,0:T(8,128)S(1)}, f32[32,8,1]{2,1,0:T(8,128)S(1)}, u32[]{:S(2)}, u32[]{:S(2)}) collective-permute-start(f32[32,8,1]{2,1,0:T(8,128)S(1)} %get-tuple-element.33), channel_id=1, source_target_pairs={{0,7},{1,0},{2,1},{3,2},{4,3},{5,4},{6,5},{7,6},{8,15},{9,8},{10,9... | collective-permute-start | bytes 3080 | tf_op jit(solution)/shard_map/ppermute | solution.py:305
  11.4 25.7 %collective-permute-start.1 = (f32[32,8,1]{2,1,0:T(8,128)S(1)}, f32[32,8,1]{2,1,0:T(8,128)S(1)}, u32[]{:S(2)}, u32[]{:S(2)}) collective-permute-start(f32[32,8,1]{2,1,0:T(8,128)S(1)} %get-tuple-element.32), channel_id=1, source_target_pairs={{0,1},{1,2},{2,3},{3,4},{4,5},{5,6},{6,7},{7,0},{8,9},{9,10},{10,1... | collective-permute-start | bytes 3080 | tf_op jit(solution)/shard_map/ppermute | solution.py:305
  16.0 14.6 %all-to-all-start.1 = ((f32[32,8,256]{2,1,0:T(8,128)}), f32[32,8,256]{2,1,0:T(8,128)S(1)}, u32[]{:S(2)}, u32[]{:S(2)}) async-start(f32[32,8,256]{2,1,0:T(8,128)} %p_ref.1), calls=%async_computation.1 | async-start | bytes 524288 | tf_op jit(solution)/shard_map/all_to_all | solution.py:309
  30.7 0.8 copy-start.3
  34.3 13.2 %all-to-all-start.2 = ((f32[32,8,256]{2,1,0:T(8,128)}), f32[32,8,256]{2,1,0:T(8,128)S(1)}, u32[]{:S(2)}, u32[]{:S(2)}) async-start(f32[32,8,256]{2,1,0:T(8,128)} %transform_div.1), calls=%async_computation.2 | async-start | bytes 524288 | tf_op jit(solution)/shard_map/all_to_all | solution.py:309
  47.4 0.7 copy-start.2
  81.7 18.2 %all-to-all-start.4 = ((f32[32,16,256]{2,1,0:T(8,128)}), f32[32,16,256]{2,1,0:T(8,128)S(1)}, u32[]{:S(2)}, u32[]{:S(2)}) async-start(f32[32,16,256]{2,1,0:T(8,128)} %get-tuple-element.18), calls=%async_computation.4 | async-start | bytes 1048576 | tf_op jit(solution)/shard_map/all_to_all | solution.py:309

commit v2 on v1

--- a/solution.py
+++ b/solution.py
@@ -9,10 +9,11 @@
 from jax.experimental.pallas import tpu as pltpu
 from jax.sharding import PartitionSpec as P
 
-SUBSTEPS = 2
+
 LANES = 128
 F32 = jnp.float32
 BF16 = jnp.bfloat16
+KERNEL = pltpu.CompilerParams(vmem_limit_bytes=8 << 20)
 
 
 def cmul_const(re, im, cr, ci):
@@ -85,11 +86,10 @@
         br, bi = groups[n // 2 - s]
         even.append((add(ar, br), sub(ai, bi)))
         odd.append(rotate((sub(ar, br), add(ai, bi)), s, n))
-    if True:
-        even[0] = (even[0][0], None)
-        odd[0] = (odd[0][0], None)
-        even[-1] = (even[-1][0], None)
-        odd[-1] = (odd[-1][0], None)
+    even[0] = (even[0][0], None)
+    odd[0] = (odd[0][0], None)
+    even[-1] = (even[-1][0], None)
+    odd[-1] = (odd[-1][0], None)
     out = [None] * n
     out[0::2] = real_dft_inverse(even)
     out[1::2] = real_dft_inverse(odd)
@@ -119,8 +119,7 @@
     return weights, rows.astype(np.float32)
 
 
-def transform_kernel(plan, full, x_ref, coef_ref, weight_ref, table_ref, *refs):
-    outs, (lhs_ref, spec_ref, work_ref) = refs[:-3], refs[-3:]
+def transform_kernel(plan, full, x_ref, coef_ref, weight_ref, table_ref, out_ref, lhs_ref, spec_ref, work_ref):
     stacks, stack_step, nl, piece_step, skip, band = plan
     _, tall, width = x_ref.shape
     per = width // LANES
@@ -159,7 +158,8 @@
         put(s * rows, re, zero if im is None else im)
     spec_ref[...] = product(0, groups * rows)
 
-    limit, has_up, has_down, zonal2, merid, merid_up, merid_down = (coef_ref[i] for i in range(7))
+    limit, has_up, has_down, zonal, merid = (jnp.broadcast_to(coef_ref[:, i:i + 1], (rows, LANES)) for i in range(5))
+    zonal2, merid_up, merid_down = zonal * zonal, merid * has_up, merid * has_down
     limit2 = limit * limit
 
     def above(a):
@@ -172,14 +172,14 @@
         wavenum, inverse2, slope = (table_ref[i, s:s + 1] for i in (2, 3, 4))
         factor = jnp.where(wavenum > limit, limit2 * inverse2, 1.0)
         parts = [spec_ref[s * rows:(s + 1) * rows, half * LANES:(half + 1) * LANES] for half in (0, 1)]
-        zonal = zonal2 * (slope * slope)
+        spread2 = zonal2 * (slope * slope)
         filtered = [factor * part for part in parts]
         merids, divs = [], []
         for part, filt in zip(parts, filtered):
             across = factor * (has_up * above(part) - has_down * below(part))
             flux = merid * across
             merids.append(across)
-            divs.append(zonal * filt - merid_up * above(flux) + merid_down * below(flux))
+            divs.append(spread2 * filt - merid_up * above(flux) + merid_down * below(flux))
         put(s * rows, *divs)
         if full:
             put((groups + s) * rows, -slope * filtered[1], slope * filtered[0])
@@ -200,13 +200,13 @@
                 im = None
             spectrum.append((re, im))
         result = real_dft_inverse(spectrum)
-        target, offset = (outs[0], 0) if field == 0 else (outs[1], (field - 1) * band)
+        offset = field * band
         for l in range(nl):
             for h in range(per):
                 piece = result[l * per + h] * (1.0 / length)
                 for z in range(stacks):
                     first = z * tall + skip
-                    target[block(z, l), offset:offset + band, h * LANES:(h + 1) * LANES] = piece[first:first + band]
+                    out_ref[block(z, l), offset:offset + band, h * LANES:(h + 1) * LANES] = piece[first:first + band]
 
 
 def transform(x, coefs, weights, table, plan, full):
@@ -214,18 +214,17 @@
     band = plan[5]
     rows = plan[0] * tall
     groups = table.shape[1]
-    count = (3 if full else 1) * groups * rows
-    shapes = [jax.ShapeDtypeStruct((blocks, band, width), F32)]
-    if full:
-        shapes.append(jax.ShapeDtypeStruct((blocks, 2 * band, width), F32))
+    fields = 3 if full else 1
+    count = fields * groups * rows
     return pl.pallas_call(
         functools.partial(transform_kernel, plan, full),
-        out_shape=shapes,
+        out_shape=jax.ShapeDtypeStruct((blocks, fields * band, width), F32),
         scratch_shapes=[
             pltpu.VMEM((2, count, 2 * LANES), BF16),
             pltpu.VMEM((groups * rows, 2 * LANES), F32),
             pltpu.VMEM((count, 2 * LANES), F32),
         ],
+        compiler_params=KERNEL,
         cost_estimate=pl.CostEstimate(flops=6 * 2 * 65536 * count, bytes_accessed=8 * x.size, transcendentals=0),
         name="transform_all" if full else "transform_div",
     )(x, coefs, weights, table)
@@ -251,17 +250,21 @@
         factor_kernel,
         in_specs=[pl.BlockSpec(memory_space=pltpu.SMEM), pl.BlockSpec(memory_space=pltpu.VMEM)],
         out_shape=[shape] * 3,
+        compiler_params=KERNEL,
         cost_estimate=pl.CostEstimate(flops=10 * sound.size, bytes_accessed=16 * sound.size, transcendentals=0),
         name="factor_columns",
     )(level_coef, sound)
 
 
-def column_kernel(first, level_ref, sound_ref, inv_ref, carry_ref, ratio_ref, base_ref, div_ref, p_ref, w_ref, *outs):
-    w_out, p_out = outs[0], outs[1]
-    levels = sound_ref.shape[0]
+def column_kernel(first, level_ref, sound_ref, inv_ref, carry_ref, ratio_ref, base_ref, div_ref, p_ref, w_ref, *refs):
+    if first:
+        w_out, p_out, sum_out = refs
+    else:
+        u_ref, v_ref, rows_ref, u_out, v_out, w_out, p_out = refs
+    levels, band, _ = sound_ref.shape
 
     def star(k):
-        return p_ref[k] - sound_ref[k] * (base_ref[k] + div_ref[k])
+        return p_ref[k] - sound_ref[k] * (base_ref[k] + div_ref[k, :band])
 
     here = star(0)
     value = None
@@ -277,6 +280,10 @@
         scaled = rhs * inv_ref[k]
         value = scaled if value is None else scaled + carry_ref[k] * value
         w_out[k] = value
+        if not first:
+            zonal, merid = rows_ref[:, 0:1], rows_ref[:, 1:2]
+            u_out[k] = u_ref[k] - zonal * div_ref[k, band:2 * band]
+            v_out[k] = v_ref[k] - merid * div_ref[k, 2 * band:]
     upper = w_out[levels - 1]
     for k in range(levels - 1, -1, -1):
         lower = w_out[k - 1] - ratio_ref[k - 1] * upper if k else None
@@ -285,19 +292,21 @@
         fresh = p_out[k] - sound_ref[k] * (upper if lower is None else upper - lower)
         p_out[k] = fresh
         if first:
-            outs[2][k] = p_ref[k] + fresh
+            sum_out[k] = p_ref[k] + fresh
         upper = lower
 
 
-def column(level_coef, sound, factors, base, div, p, w, first):
-    shape = jax.ShapeDtypeStruct(sound.shape, F32)
+def column(first, level_coef, *operands):
+    shape = jax.ShapeDtypeStruct(operands[0].shape, F32)
+    size = operands[0].size
     return pl.pallas_call(
         functools.partial(column_kernel, first),
-        in_specs=[pl.BlockSpec(memory_space=pltpu.SMEM)] + [pl.BlockSpec(memory_space=pltpu.VMEM)] * 8,
-        out_shape=[shape] * (3 if first else 2),
-        cost_estimate=pl.CostEstimate(flops=20 * sound.size, bytes_accessed=40 * sound.size, transcendentals=0),
+        in_specs=[pl.BlockSpec(memory_space=pltpu.SMEM)] + [pl.BlockSpec(memory_space=pltpu.VMEM)] * len(operands),
+        out_shape=[shape] * (3 if first else 4),
+        compiler_params=KERNEL,
+        cost_estimate=pl.CostEstimate(flops=20 * size, bytes_accessed=40 * size, transcendentals=0),
         name="column_first" if first else "column_last",
-    )(level_coef, sound, *factors, base, div, p, w)
+    )(level_coef, *operands)
 
 
 def shifted(block, axis, step):
@@ -316,31 +325,24 @@
     return low, high
 
 
-def latitude_data(zonal_coef, merid_coef, merid_wind, halo):
-    levels, band, width = merid_wind.shape
+def latitude_data(coefs, halo):
     nz, me = lax.axis_size("lat"), lax.axis_index("lat")
     if halo:
-        v_low, v_high = lat_edges(merid_wind[:, -1], merid_wind[:, 0])
-        own = jnp.stack([zonal_coef, merid_coef])
-        low, high = lat_edges(own[:, -halo:], own[:, :halo])
-        zonal, merid = jnp.concatenate([low, own, high], axis=1)
-        return zonal, merid, v_low, v_high
-    target = lax.broadcasted_iota(jnp.int32, (nz, 1, 1), 0)
-    edges = jnp.where(target == me + 1, merid_wind[None, :, band - 1], 0.0)
-    edges = jnp.where(target == me - 1, merid_wind[None, :, 0], edges)
-    own = jnp.concatenate([zonal_coef, merid_coef])
-    own = jnp.broadcast_to(jnp.pad(own, (0, width - 2 * band)), (nz, 8, width))
-    sent = jnp.concatenate([edges, own], axis=1).reshape(nz * (levels + 8), width)
-    got = exchange(sent, "lat").reshape(nz, levels + 8, width)
-    padded = jnp.pad(got[:, :levels], ((1, 1), (0, 0), (0, 0)))
-    v_low = lax.dynamic_index_in_dim(padded, me, 0, keepdims=False)
-    v_high = lax.dynamic_index_in_dim(padded, me + 2, 0, keepdims=False)
-    zonal = got[:, levels, :band].reshape(nz * band)
-    merid = got[:, levels, band:2 * band].reshape(nz * band)
-    return zonal, merid, v_low, v_high
-
-
-def body(
+        low, high = lat_edges(coefs[-halo:], coefs[:halo])
+        return jnp.concatenate([low, coefs, high], axis=0)
+    got = [coefs]
+    for step in range(1, nz):
+        got.append(lax.ppermute(coefs, "lat", [(i, (i + step) % nz) for i in range(nz)]))
+    blocks = []
+    for z in range(nz):
+        block = got[0]
+        for k in range(1, nz):
+            block = jnp.where((me - z) % nz == k, got[k], block)
+        blocks.append(block)
+    return jnp.concatenate(blocks, axis=0)
+
+
+def program(
     zonal_wind,
     merid_wind,
     vertical_wind,
@@ -380,41 +382,35 @@
 
     circles = spread(pressure)
 
-    zonal_all, merid_all, v_low, v_high = latitude_data(zonal_coef, merid_coef, merid_wind, halo)
     row = jnp.arange(lats + 2 * halo) - halo
-    has_up = (row < lats - 1).astype(F32)
-    has_down = (row > 0).astype(F32)
     limit = jnp.pad(jnp.where(filter_mask > 0, cutoff, length).astype(F32), (halo, halo), constant_values=1.0)
-    coefs = jnp.stack([limit, has_up, has_down])
+    known = jnp.stack([limit, (row < lats - 1).astype(F32), (row > 0).astype(F32)], axis=1)
     if halo:
-        coefs = lax.dynamic_slice_in_dim(coefs, me * band, band + 2 * halo, 1)
-    coefs = jnp.concatenate([coefs, (zonal_all * zonal_all)[None], merid_all[None], merid_all * coefs[1:3]])
+        known = lax.dynamic_slice_in_dim(known, me * band, band + 2 * halo, 0)
+    coefs = jnp.concatenate([known, latitude_data(jnp.stack([zonal_coef, merid_coef], axis=1), halo)], axis=1)
     if halo:
-        coefs = jnp.tile(jnp.pad(coefs, ((0, 0), (0, tall - band - 2 * halo))), (1, depth))
-    coefs = jnp.broadcast_to(coefs[:, :, None], coefs.shape + (LANES,))
-
+        coefs = jnp.tile(jnp.pad(coefs, ((0, tall - band - 2 * halo), (0, 0))), (depth, 1))
+
+    v_low, v_high = lat_edges(merid_wind[:, -1:], merid_wind[:, :1])
     u_low = shifted(zonal_wind[:, :, -1:], "lon", 1)
     u_high = shifted(zonal_wind[:, :, :1], "lon", -1)
     zonal_rows, merid_rows = zonal_coef[None, :, None], merid_coef[None, :, None]
     u_diff = jnp.concatenate([zonal_wind[:, :, 1:], u_high], 2) - jnp.concatenate([u_low, zonal_wind[:, :, :-1]], 2)
-    v_diff = jnp.concatenate([merid_wind[:, 1:], v_high[:, None]], 1) - jnp.concatenate([v_low[:, None], merid_wind[:, :-1]], 1)
+    v_diff = jnp.concatenate([merid_wind[:, 1:], v_high], 1) - jnp.concatenate([v_low, merid_wind[:, :-1]], 1)
     base = zonal_rows * u_diff + merid_rows * v_diff
 
     factors = factor(level_coef, sound_coef)
 
-    (div,) = transform(circles, coefs, weights, table, plan, False)
+    div = transform(circles, coefs, weights, table, plan, False)
     div = exchange(div, axes)
-    w, p, total = column(level_coef, sound_coef, factors, base, div, pressure, vertical_wind, True)
-    div, winds = transform(spread(total), coefs, weights, table, plan, True)
-    div = exchange(div, axes)
-    winds = exchange(winds, axes)
-    w, p = column(level_coef, sound_coef, factors, base, div, p, w, False)
-    u = zonal_wind - zonal_rows * winds[:, :band]
-    v = merid_wind - merid_rows * winds[:, band:]
-    return (u, v, w, p)
+    w, p, total = column(True, level_coef, sound_coef, *factors, base, div, pressure, vertical_wind)
+    fields = transform(spread(total), coefs, weights, table, plan, True)
+    fields = exchange(fields, axes)
+    rows = jnp.stack([zonal_coef, merid_coef], axis=1)
+    return column(False, level_coef, sound_coef, *factors, base, fields, p, w, zonal_wind, merid_wind, rows)
 
 
 def solution(mesh):
     spec = P(None, "lat", "lon")
     in_specs = (spec, spec, spec, spec, P("lat"), P("lat"), P(), spec, P(), P())
-    return jax.shard_map(body, mesh=mesh, in_specs=in_specs, out_specs=(spec,) * 4, check_vma=False)
+    return jax.shard_map(program, mesh=mesh, in_specs=in_specs, out_specs=(spec,) * 4, check_vma=False)

time: 102 us -> 79.4 us (0.78)
  blocking collectives: 27.7 us -> 12.8 us
  starting transfers between devices: 17.2 us -> 24.6 us
  Pallas kernels: 13.3 us -> 7.08 us
  waiting for transfers between devices: 35.2 us -> 29.6 us
  other arithmetic: 2.76 us -> 1.35 us
  local copies, waits for them, and re-layouts: 3.81 us -> 2.63 us
    all_to_all x2 -> x1, blocking collectives: 27.7 us -> 12.8 us  [exchange(): return lax.all_to_all(block, axes, split_axis=0, concat_axis=0, tiled=True)]
    ppermute x0 -> x5, starting transfers between devices: none -> 12.1 us  [the longest x3 7.04 us: latitude_data(): lax.ppermute(coefs, 'lat', [(i, (i + step) % nz) for i in range(nz)])]
    all_to_all x4 -> x3, starting transfers between devices: 15.6 us -> 9.81 us  [exchange(): return lax.all_to_all(block, axes, split_axis=0, concat_axis=0, tiled=True)]
    all_to_all x4 -> x3, waiting for transfers between devices: 35.2 us -> 29.5 us  [exchange(): return lax.all_to_all(block, axes, split_axis=0, concat_axis=0, tiled=True)]
    pallas_call x2, Pallas kernels: 5.01 us -> 2.35 us  [column(): pl.pallas_call(functools.partial(column_kernel, first), in_specs=[pl.Bloc...]
    pallas_call x2, Pallas kernels: 6.16 us -> 3.91 us  [transform(): pl.pallas_call(functools.partial(transform_kernel, plan, full), out_shape...]
    pallas_call x1, Pallas kernels: 2.12 us -> 0.82 us  [factor(): pl.pallas_call(factor_kernel, in_specs=[pl.BlockSpec(memory_space=pltpu.S...]
    slice x5 -> x4, local copies, waits for them, and re-layouts: 1.35 us -> 0.3 us  [the longest x1 0.13 us: program(): zonal_wind[:, :, :-1]]
  transfers between devices with their start and end apart: 6 -> 10, of which waited for: 4 -> 3; matrix products, arithmetic and copies ran while one was open for 2% -> 2% of each run, Pallas kernels for 7% -> 3%
where the time goes in v2:
time: 79.4 us; the launch traced here: 79 us
  waiting for transfers between devices  29.6 us (37%)
  starting transfers between devices  24.6 us (31%)
  blocking collectives  12.8 us (16%)
  Pallas kernels  7.08 us (9%)
  local copies, waits for them, and re-layouts  2.63 us (3%)
  other arithmetic  1.35 us (2%)
  between operations  0.99 us (1%)
    all_to_all x3, waiting for transfers between devices, exchange(): return lax.all_to_all(block, axes, split_axis=0, concat_axis=0, tiled=True)  29.5 us
    all_to_all x1, blocking collectives, exchange(): return lax.all_to_all(block, axes, split_axis=0, concat_axis=0, tiled=True)  12.8 us
    all_to_all x3, starting transfers between devices, exchange(): return lax.all_to_all(block, axes, split_axis=0, concat_axis=0, tiled=True)  9.81 us
    ppermute x3, starting transfers between devices, latitude_data(): lax.ppermute(coefs, 'lat', [(i, (i + step) % nz) for i in range(nz)])  7.04 us
    pallas_call x2, Pallas kernels, transform(): pl.pallas_call(functools.partial(transform_kernel, plan, full), out_shape...  3.91 us
    ppermute x1, starting transfers between devices, lat_edges(): low = lax.ppermute(last, 'lat', [(i, i + 1) for i in range(count - 1)])  3.81 us
    ppermute x2, starting transfers between devices, shifted(): lax.ppermute(block, axis, [(i, (i + step) % count) for i in range(count)])  2.68 us
    pallas_call x2, Pallas kernels, column(): pl.pallas_call(functools.partial(column_kernel, first), in_specs=[pl.Bloc...  2.35 us
  transfers between devices with their start and end apart: 10, of which 3 were waited for; matrix products, arithmetic and copies ran while one was open for 2% of the time, Pallas kernels for 3%

profile of v2, /device:TPU:0, one launch (start us, length us, event | category | flops | bytes accessed | tf_op | source)
XLA Modules:
  0.0 79.0 jit_solution(5646067176419117333)
XLA Ops:
  0.6 0.0 copy-start.10
  0.6 0.0 copy-start.11
  0.7 0.6 copy-done.10
  1.3 0.0 copy-done.11
  1.3 0.0 copy-start.1
  1.3 0.0 copy-start
  1.3 3.1 %collective-permute-start.6 = (f32[8,2]{0,1:T(2,128)S(1)}, f32[8,2]{0,1:T(2,128)S(1)}, u32[]{:S(2)}, u32[]{:S(2)}) collective-permute-start(f32[8,2]{0,1:T(2,128)S(1)} %pad_maximum_fusion), channel_id=1, source_target_pairs={{0,8},{8,16},{16,24},{24,0},{1,9},{9,17},{17,25},{25,1},{2,10},{10... | collective-permute-start | bytes 200 | tf_op jit(solution)/shard_map/ppermute | solution.py:335
  4.4 2.6 %collective-permute-start.5 = (f32[8,2]{0,1:T(2,128)S(1)}, f32[8,2]{0,1:T(2,128)S(1)}, u32[]{:S(2)}, u32[]{:S(2)}) collective-permute-start(f32[8,2]{0,1:T(2,128)S(1)} %pad_maximum_fusion), channel_id=1, source_target_pairs={{0,16},{8,24},{16,0},{24,8},{1,17},{9,25},{17,1},{25,9},{2,18},{10... | collective-permute-start | bytes 200 | tf_op jit(solution)/shard_map/ppermute | solution.py:335
  7.0 1.3 %collective-permute-start.4 = (f32[8,2]{0,1:T(2,128)S(1)}, f32[8,2]{0,1:T(2,128)S(1)}, u32[]{:S(2)}, u32[]{:S(2)}) collective-permute-start(f32[8,2]{0,1:T(2,128)S(1)} %pad_maximum_fusion), channel_id=1, source_target_pairs={{0,24},{8,0},{16,8},{24,16},{1,25},{9,1},{17,9},{25,17},{2,26},{10... | collective-permute-start | bytes 200 | tf_op jit(solution)/shard_map/ppermute | solution.py:335
  8.4 2.9 %all-to-all-start = ((f32[32,8,256]{2,1,0:T(8,128)}), f32[32,8,256]{2,1,0:T(8,128)S(1)}, u32[]{:S(2)}, u32[]{:S(2)}) async-start(f32[32,8,256]{2,1,0:T(8,128)} %p_ref.1), calls=%async_computation | async-start | bytes 524288 | tf_op jit(solution)/shard_map/all_to_all | solution.py:318
  11.3 0.0 copy-done.1
  11.3 0.0 copy-start.4
  11.4 3.8 %collective-permute-start.3 = (f32[32,1,256]{2,1,0:T(1,128)S(1)}, f32[32,1,256]{2,1,0:T(1,128)S(1)}, u32[]{:S(2)}, u32[]{:S(2)}) collective-permute-start(f32[32,1,256]{2,1,0:T(1,128)S(1)} %get-tuple-element.16), channel_id=1, source_target_pairs={{0,8},{8,16},{16,24},{1,9},{9,17},{17,25},{2,10},{10,18},{18,26},{... | collective-permute-start | bytes 98312 | tf_op jit(solution)/shard_map/ppermute | solution.py:323
  15.2 1.3 %collective-permute-start.2 = (f32[32,1,256]{2,1,0:T(1,128)S(1)}, f32[32,1,256]{2,1,0:T(1,128)S(1)}, u32[]{:S(2)}, u32[]{:S(2)}) collective-permute-start(f32[32,1,256]{2,1,0:T(1,128)S(1)} %get-tuple-element.17), channel_id=1, source_target_pairs={{8,0},{16,8},{24,16},{9,1},{17,9},{25,17},{10,2},{18,10},{26,18},{... | collective-permute-start | bytes 98312 | tf_op jit(solution)/shard_map/ppermute | solution.py:324
  16.6 0.0 copy-done
  16.6 0.0 copy-start.12
  16.6 0.0 copy-start.13
  16.6 0.1 fusion.7
  16.7 0.5 copy-done.12
  17.3 0.0 copy-done.13
  17.3 0.0 copy-start.8
  17.3 0.0 collective-permute-done.6
  17.3 0.1 collective-permute-start.1
  17.4 0.0 collective-permute-done.5
  17.4 2.6 %collective-permute-start = (f32[32,8,1]{2,1,0:T(8,128)S(1)}, f32[32,8,1]{2,1,0:T(8,128)}, u32[]{:S(2)}, u32[]{:S(2)}) collective-permute-start(f32[32,8,1]{2,1,0:T(8,128)S(1)} %get-tuple-element.21), channel_id=1, source_target_pairs={{0,7},{1,0},{2,1},{3,2},{4,3},{5,4},{6,5},{7,6},{8,15},{9,8},{10,9... | collective-permute-start | bytes 3080 | tf_op jit(solution)/shard_map/ppermute | solution.py:314
  20.0 0.0 collective-permute-done.4
  20.0 0.1 maximum_maximum_fusion
  20.1 0.1 copy.19.coef_ref
  20.2 1.7 %all-to-all-done.x_ref = f32[32,8,256]{2,1,0:T(8,128)S(1)} async-done(((f32[32,8,256]{2,1,0:T(8,128)}), f32[32,8,256]{2,1,0:T(8,128)S(1)}, u32[]{:S(2)}, u32[]{:S(2)}) %all-to-all-start) | async-done | bytes 262176 | tf_op jit(solution)/shard_map/all_to_all | solution.py:318
  21.9 0.0 copy-done.4
  21.9 0.0 copy-done.8
  21.9 1.6 %transform_div.1 = f32[32,8,256]{2,1,0:T(8,128)} custom-call(f32[32,8,256]{2,1,0:T(8,128)S(1)} %all-to-all-done.x_ref, f32[32,5]{1,0:T(8,128)S(1)} %copy.19.coef_ref, bf16[2,2,256,256]{3,2,1,0:T(8,128)(2,1)S(1)} %copy-done.4, f32[5,9,128]{2,1,0:T(8,128)S(1)} %copy-done.8), custom_call_target="tpu_custom_call" | custom-call | flops 226492416 | bytes 524288 | tf_op jit(solution)/shard_map/transform_div/pallas_call | solution.py:219
  23.5 4.1 %all-to-all-start.1 = ((f32[32,8,256]{2,1,0:T(8,128)}), f32[32,8,256]{2,1,0:T(8,128)S(1)}, u32[]{:S(2)}, u32[]{:S(2)}) async-start(f32[32,8,256]{2,1,0:T(8,128)} %transform_div.1), calls=%async_computation.1 | async-start | bytes 524288 | tf_op jit(solution)/shard_map/all_to_all | solution.py:318
  27.7 0.1 fusion.8
  27.8 0.0 copy-start.2
  27.8 0.0 copy-start.9
  27.9 0.9 %copy-done.2 = f32[32,8,256]{2,1,0:T(8,128)S(1)} copy-done((f32[32,8,256]{2,1,0:T(8,128)S(1)}, f32[32,8,256]{2,1,0:T(8,128)}, u32[]{:S(2)}) %copy-start.2) | copy-done | bytes 262168
  28.8 0.0 copy-done.9
  28.8 0.8 %factor_columns.1 = (f32[32,8,256]{2,1,0:T(8,128)S(1)}, f32[32,8,256]{2,1,0:T(8,128)S(1)}, f32[32,8,256]{2,1,0:T(8,128)S(1)}) custom-call(f32[32]{0:T(128)S(1)} %copy-done.9, f32[32,8,256]{2,1,0:T(8,128)S(1)} %copy-done.2), custom_call_target="tpu_custom_call" | custom-call | flops 655360 | bytes 1048576 | tf_op jit(solution)/shard_map/factor_columns/pallas_call | solution.py:249
  29.6 0.0 collective-permute-done.1
  29.6 0.0 collective-permute-done
  29.6 0.0 collective-permute-done.3
  29.6 0.0 collective-permute-done.2
  29.6 0.0 copy-start.3
  29.7 0.0 copy-start.5
  29.7 1.2 %fusion.1.base_ref = f32[32,8,256]{2,1,0:T(8,128)S(1)} fusion(f32[32,8,1]{2,1,0:T(8,128)} %collective-permute-done, f32[32,8,255]{2,1,0:T(8,128)S(1)} %get-tuple-element.23, f32[32,8,255]{2,1,0:T(8,128)S(1)} %get-tuple-element.22, f32[32,8,1]{2,1,0:T(8,128)} %collective-permute-done.1, f32[32,1,256]{2,1,0:T(1,128)S(1)} %collective-permute-done.2, ...), kind=kLoop, calls=%fused_computation.2 | loop fusion | flops 589824 | bytes 1310784 | tf_op jit(solution)/shard_map/add | solution.py:400
  30.9 7.4 %all-to-all-done.1.div_ref = f32[32,8,256]{2,1,0:T(8,128)S(1)} async-done(((f32[32,8,256]{2,1,0:T(8,128)}), f32[32,8,256]{2,1,0:T(8,128)S(1)}, u32[]{:S(2)}, u32[]{:S(2)}) %all-to-all-start.1) | async-done | bytes 262176 | tf_op jit(solution)/shard_map/all_to_all | solution.py:318
  38.2 0.0 copy-done.3
  38.2 0.0 copy-done.5
  38.3 0.7 column_first.1
  39.0 0.0 copy-start.6
  39.0 12.8 %all_to_all.20.x_ref = f32[32,8,256]{2,1,0:T(8,128)S(1)} all-to-all(f32[32,8,256]{2,1,0:T(8,128)S(1)} %get-tuple-element.13), channel_id=1, replica_groups=mesh['lat'=4,'lon'=8] {'lat','lon'}, dimensions={0} | all-to-all | bytes 524288 | tf_op jit(solution)/shard_map/all_to_all | solution.py:318
  51.8 0.0 copy-done.6
  51.8 2.3 %transform_all.1 = f32[32,24,256]{2,1,0:T(8,128)} custom-call(f32[32,8,256]{2,1,0:T(8,128)S(1)} %all_to_all.20.x_ref, f32[32,5]{1,0:T(8,128)S(1)} %copy.19.coef_ref, bf16[2,2,256,256]{3,2,1,0:T(8,128)(2,1)S(1)} %copy-done.4, f32[5,9,128]{2,1,0:T(8,128)S(1)} %copy-done.8), custom_call_target="tpu_custom_call" | custom-call | flops 679477248 | bytes 524288 | tf_op jit(solution)/shard_map/transform_all/pallas_call | solution.py:219
  54.0 0.0 copy-start.7
  54.0 2.8 %all-to-all-start.3 = ((f32[32,24,256]{2,1,0:T(8,128)}), f32[32,24,256]{2,1,0:T(8,128)S(1)}, u32[]{:S(2)}, u32[]{:S(2)}) async-start(f32[32,24,256]{2,1,0:T(8,128)} %transform_all.1), calls=%async_computation.3 | async-start | bytes 1572864 | tf_op jit(solution)/shard_map/all_to_all | solution.py:318
  56.8 0.1 copy.21.refs_2_
  56.9 20.5 %all-to-all-done.3.div_ref = f32[32,24,256]{2,1,0:T(8,128)S(1)} async-done(((f32[32,24,256]{2,1,0:T(8,128)}), f32[32,24,256]{2,1,0:T(8,128)S(1)}, u32[]{:S(2)}, u32[]{:S(2)}) %all-to-all-start.3) | async-done | bytes 786464 | tf_op jit(solution)/shard_map/all_to_all | solution.py:318
  77.4 0.0 copy-done.7
  77.4 1.6 %column_last.1 = (f32[32,8,256]{2,1,0:T(8,128)}, f32[32,8,256]{2,1,0:T(8,128)}, f32[32,8,256]{2,1,0:T(8,128)}, f32[32,8,256]{2,1,0:T(8,128)}) custom-call(f32[32]{0:T(128)S(1)} %copy-done.9, f32[32,8,256]{2,1,0:T(8,128)S(1)} %copy-done.2, f32[32,8,256]{2,1,0:T(8,128)S(1)} %get-tuple-element.10.inv_ref, f32[32,8,256]{2,1,0:T(8,128)S(1)} %get-tuple-element.11.carry_ref, ...), custom_call_target="tpu_custom_call" | custom-call | flops 1310720 | bytes 2621440 | tf_op jit(solution)/shard_map/column_last/pallas_call | solution.py:302
  (7 shorter events, 0.1 us)
Async XLA Ops:
  0.6 0.7 copy-start.10
  0.6 0.7 copy-start.11
  1.3 10.0 %copy-start.1 = (f32[32,8,256]{2,1,0:T(8,128)S(1)}, f32[32,8,256]{2,1,0:T(8,128)}, u32[]{:S(2)}) copy-start(f32[32,8,256]{2,1,0:T(8,128)} %refs_1_.1) | copy-start | bytes 786436
  1.3 15.3 %copy-start = (f32[32,8,256]{2,1,0:T(8,128)S(1)}, f32[32,8,256]{2,1,0:T(8,128)}, u32[]{:S(2)}) copy-start(f32[32,8,256]{2,1,0:T(8,128)} %refs_0_.1) | copy-start | bytes 786436
  1.3 16.0 %collective-permute-start.6 = (f32[8,2]{0,1:T(2,128)S(1)}, f32[8,2]{0,1:T(2,128)S(1)}, u32[]{:S(2)}, u32[]{:S(2)}) collective-permute-start(f32[8,2]{0,1:T(2,128)S(1)} %pad_maximum_fusion), channel_id=1, source_target_pairs={{0,8},{8,16},{16,24},{24,0},{1,9},{9,17},{17,25},{25,1},{2,10},{10... | collective-permute-start | bytes 200 | tf_op jit(solution)/shard_map/ppermute | solution.py:335
  4.4 12.9 %collective-permute-start.5 = (f32[8,2]{0,1:T(2,128)S(1)}, f32[8,2]{0,1:T(2,128)S(1)}, u32[]{:S(2)}, u32[]{:S(2)}) collective-permute-start(f32[8,2]{0,1:T(2,128)S(1)} %pad_maximum_fusion), channel_id=1, source_target_pairs={{0,16},{8,24},{16,0},{24,8},{1,17},{9,25},{17,1},{25,9},{2,18},{10... | collective-permute-start | bytes 200 | tf_op jit(solution)/shard_map/ppermute | solution.py:335
  7.0 13.0 %collective-permute-start.4 = (f32[8,2]{0,1:T(2,128)S(1)}, f32[8,2]{0,1:T(2,128)S(1)}, u32[]{:S(2)}, u32[]{:S(2)}) collective-permute-start(f32[8,2]{0,1:T(2,128)S(1)} %pad_maximum_fusion), channel_id=1, source_target_pairs={{0,24},{8,0},{16,8},{24,16},{1,25},{9,1},{17,9},{25,17},{2,26},{10... | collective-permute-start | bytes 200 | tf_op jit(solution)/shard_map/ppermute | solution.py:335
  8.4 13.5 %all-to-all-start = ((f32[32,8,256]{2,1,0:T(8,128)}), f32[32,8,256]{2,1,0:T(8,128)S(1)}, u32[]{:S(2)}, u32[]{:S(2)}) async-start(f32[32,8,256]{2,1,0:T(8,128)} %p_ref.1), calls=%async_computation | async-start | bytes 524288 | tf_op jit(solution)/shard_map/all_to_all | solution.py:318
  11.3 10.6 %copy-start.4 = (bf16[2,2,256,256]{3,2,1,0:T(8,128)(2,1)S(1)}, bf16[2,2,256,256]{3,2,1,0:T(8,128)(2,1)}, u32[]{:S(2)}) copy-start(bf16[2,2,256,256]{3,2,1,0:T(8,128)(2,1)} %constant.67.clone.weight_ref) | copy-start | bytes 1572868
  11.4 18.2 %collective-permute-start.3 = (f32[32,1,256]{2,1,0:T(1,128)S(1)}, f32[32,1,256]{2,1,0:T(1,128)S(1)}, u32[]{:S(2)}, u32[]{:S(2)}) collective-permute-start(f32[32,1,256]{2,1,0:T(1,128)S(1)} %get-tuple-element.16), channel_id=1, source_target_pairs={{0,8},{8,16},{16,24},{1,9},{9,17},{17,25},{2,10},{10,18},{18,26},{... | collective-permute-start | bytes 98312 | tf_op jit(solution)/shard_map/ppermute | solution.py:323
  15.2 14.4 %collective-permute-start.2 = (f32[32,1,256]{2,1,0:T(1,128)S(1)}, f32[32,1,256]{2,1,0:T(1,128)S(1)}, u32[]{:S(2)}, u32[]{:S(2)}) collective-permute-start(f32[32,1,256]{2,1,0:T(1,128)S(1)} %get-tuple-element.17), channel_id=1, source_target_pairs={{8,0},{16,8},{24,16},{9,1},{17,9},{25,17},{10,2},{18,10},{26,18},{... | collective-permute-start | bytes 98312 | tf_op jit(solution)/shard_map/ppermute | solution.py:324
  16.6 0.7 copy-start.12
  16.6 0.7 copy-start.13
  17.3 4.6 %copy-start.8 = (f32[5,9,128]{2,1,0:T(8,128)S(1)}, f32[5,9,128]{2,1,0:T(8,128)}, u32[]{:S(2)}) copy-start(f32[5,9,128]{2,1,0:T(8,128)} %constant.68.clone.table_ref) | copy-start | bytes 69124
  17.3 12.3 %collective-permute-start.1 = (f32[32,8,1]{2,1,0:T(8,128)S(1)}, f32[32,8,1]{2,1,0:T(8,128)}, u32[]{:S(2)}, u32[]{:S(2)}) collective-permute-start(f32[32,8,1]{2,1,0:T(8,128)S(1)} %get-tuple-element.20), channel_id=1, source_target_pairs={{0,1},{1,2},{2,3},{3,4},{4,5},{5,6},{6,7},{7,0},{8,9},{9,10},{10,1... | collective-permute-start | bytes 3080 | tf_op jit(solution)/shard_map/ppermute | solution.py:314
  17.4 12.2 %collective-permute-start = (f32[32,8,1]{2,1,0:T(8,128)S(1)}, f32[32,8,1]{2,1,0:T(8,128)}, u32[]{:S(2)}, u32[]{:S(2)}) collective-permute-start(f32[32,8,1]{2,1,0:T(8,128)S(1)} %get-tuple-element.21), channel_id=1, source_target_pairs={{0,7},{1,0},{2,1},{3,2},{4,3},{5,4},{6,5},{7,6},{8,15},{9,8},{10,9... | collective-permute-start | bytes 3080 | tf_op jit(solution)/shard_map/ppermute | solution.py:314
  23.5 14.7 %all-to-all-start.1 = ((f32[32,8,256]{2,1,0:T(8,128)}), f32[32,8,256]{2,1,0:T(8,128)S(1)}, u32[]{:S(2)}, u32[]{:S(2)}) async-start(f32[32,8,256]{2,1,0:T(8,128)} %transform_div.1), calls=%async_computation.1 | async-start | bytes 524288 | tf_op jit(solution)/shard_map/all_to_all | solution.py:318
  27.8 1.0 %copy-start.2 = (f32[32,8,256]{2,1,0:T(8,128)S(1)}, f32[32,8,256]{2,1,0:T(8,128)}, u32[]{:S(2)}) copy-start(f32[32,8,256]{2,1,0:T(8,128)} %sound_ref.5) | copy-start | bytes 786436
  27.8 0.9 %copy-start.9 = (f32[32]{0:T(128)S(1)}, f32[32]{0:T(128)}, u32[]{:S(2)}) copy-start(f32[32]{0:T(128)} %level_ref.5) | copy-start | bytes 388
  29.6 8.6 %copy-start.3 = (f32[32,8,256]{2,1,0:T(8,128)S(1)}, f32[32,8,256]{2,1,0:T(8,128)}, u32[]{:S(2)}) copy-start(f32[32,8,256]{2,1,0:T(8,128)} %p_ref.1) | copy-start | bytes 786436
  29.7 8.6 %copy-start.5 = (f32[32,8,256]{2,1,0:T(8,128)S(1)}, f32[32,8,256]{2,1,0:T(8,128)}, u32[]{:S(2)}) copy-start(f32[32,8,256]{2,1,0:T(8,128)} %w_ref.1) | copy-start | bytes 786436
  39.0 12.8 %copy-start.6 = (f32[32,8,256]{2,1,0:T(8,128)}, f32[32,8,256]{2,1,0:T(8,128)S(1)}, u32[]{:S(2)}) copy-start(f32[32,8,256]{2,1,0:T(8,128)S(1)} %get-tuple-element.14.p_ref) | copy-start | bytes 786436
  54.0 23.3 %copy-start.7 = (f32[32,8,256]{2,1,0:T(8,128)S(1)}, f32[32,8,256]{2,1,0:T(8,128)}, u32[]{:S(2)}) copy-start(f32[32,8,256]{2,1,0:T(8,128)} %copy-done.6) | copy-start | bytes 786436
  54.0 23.3 %all-to-all-start.3 = ((f32[32,24,256]{2,1,0:T(8,128)}), f32[32,24,256]{2,1,0:T(8,128)S(1)}, u32[]{:S(2)}, u32[]{:S(2)}) async-start(f32[32,24,256]{2,1,0:T(8,128)} %transform_all.1), calls=%async_computation.3 | async-start | bytes 1572864 | tf_op jit(solution)/shard_map/all_to_all | solution.py:318

commit v3 on v2

v3 whole, which is shorter than its diff:
```python
import functools
import math
from typing import NamedTuple

import jax
import jax.numpy as jnp
import numpy as np
from jax import lax
from jax.experimental import pallas as pl
from jax.experimental.pallas import tpu as pltpu
from jax.sharding import PartitionSpec as P


LANES = 128
F32 = jnp.float32
BF16 = jnp.bfloat16
KERNEL = pltpu.CompilerParams(vmem_limit_bytes=8 << 20)
ALONE = pltpu.CompilerParams(vmem_limit_bytes=60 << 20)


class Plan(NamedTuple):
    packed: bool
    offsets: tuple
    depth: int
    nl: int
    per: int
    tall: int
    skip: int
    band: int

    def fields(self, full):
        if not full:
            return "d"
        return "uv" if self.packed else "duv"


def cmul_const(re, im, cr, ci):
    if im is None:
        return (re * cr if cr != 0.0 else None, re * ci if ci != 0.0 else None)
    return (re * cr - im * ci, re * ci + im * cr)


def add(a, b):
    if a is None:
        return b
    return a if b is None else a + b


def sub(a, b):
    if b is None:
        return a
    return -b if a is None else a - b


def neg(a):
    return None if a is None else -a


def unit(num, den):
    turn = num % den
    table = {0: (1.0, 0.0), den / 4: (0.0, 1.0), den / 2: (-1.0, 0.0), 3 * den / 4: (0.0, -1.0)}
    if turn in table:
        return table[turn]
    angle = 2.0 * math.pi * turn / den
    return math.cos(angle), math.sin(angle)


def rotate(z, num, den):
    cr, ci = unit(num, den)
    re, im = z
    if (cr, ci) == (1.0, 0.0):
        return z
    if (cr, ci) == (0.0, 1.0):
        return (neg(im), re)
    if (cr, ci) == (0.0, -1.0):
        return (im, neg(re))
    return cmul_const(re, im, cr, ci)


def real_dft(pieces):
    n = len(pieces)
    if n == 1:
        return [(pieces[0], None)]
    even, odd = real_dft(pieces[0::2]), real_dft(pieces[1::2])
    out = [None] * (n // 2 + 1)
    for s in range(n // 4 + 1 if n > 2 else 1):
        er, ei = even[s]
        tr, ti = rotate(odd[s], -s, n)
        out[n // 2 - s] = (sub(er, tr), sub(ti, ei))
        out[s] = (add(er, tr), add(ei, ti))
    return out


def real_dft_inverse(groups):
    n = 2 * (len(groups) - 1)
    if n == 0:
        return [groups[0][0]]
    if n == 2:
        a, b = groups[0][0], groups[1][0]
        return [a + b, a - b]
    even, odd = [], []
    for s in range(n // 4 + 1):
        ar, ai = groups[s]
        br, bi = groups[n // 2 - s]
        even.append((add(ar, br), sub(ai, bi)))
        odd.append(rotate((sub(ar, br), add(ai, bi)), s, n))
    even[0] = (even[0][0], None)
    odd[0] = (odd[0][0], None)
    even[-1] = (even[-1][0], None)
    odd[-1] = (odd[-1][0], None)
    out = [None] * n
    out[0::2] = real_dft_inverse(even)
    out[1::2] = real_dft_inverse(odd)
    return out


def tables(length):
    pieces = length // LANES
    groups = pieces // 2 + 1
    lane = np.arange(LANES)
    angle = 2.0 * np.pi / LANES * (np.outer(lane, lane) % LANES)
    cos, sin = np.cos(angle), np.sin(angle)
    matrix = np.block([[cos, -sin], [sin, cos]])

    def halves(m):
        m = m.astype(np.float32)
        high = m.astype(BF16)
        return np.stack([high, (m - high.astype(np.float32)).astype(BF16)])

    weights = np.stack([halves(matrix), halves(matrix.T)])
    s = np.arange(groups)[:, None]
    turn = 2.0 * np.pi / length * (s * lane[None, :])
    wavenum = pieces * lane[None, :] + s
    wavenum = np.minimum(wavenum, length - wavenum).astype(np.float64)
    slope = 2.0 * np.sin(2.0 * np.pi / length * (pieces * lane[None, :] + s))
    rows = np.stack([np.cos(turn), np.sin(turn), wavenum, 1.0 / np.maximum(wavenum, 1.0) ** 2, slope])
    return weights, rows.astype(np.float32)


def transform_kernel(plan, full, x_ref, *refs):
    extra_ref = x_ref
    if plan.packed and full:
        extra_ref, refs = refs[0], refs[1:]
    coef_ref, weight_ref, table_ref, result_ref, lhs_ref, spec_ref, work_ref, out_ref, sem = refs
    nl, per, tall, skip, band = plan.nl, plan.per, plan.tall, plan.skip, plan.band
    stacks = len(plan.offsets)
    pieces = nl * per
    groups = pieces // 2 + 1
    rows = stacks * tall
    length = pieces * LANES

    def block(stack, l):
        return plan.offsets[stack] + l % nl * plan.depth

    def tile(stack, l, h):
        return x_ref[block(stack, l), h * tall:(h + 1) * tall]

    def edge_tile(stack, l):
        return unfold(extra_ref[block(stack, l), per * tall + 4:per * tall + 8])

    def product(which, count):
        total = jnp.dot(lhs_ref[0, :count], weight_ref[which, 0], preferred_element_type=F32)
        total += jnp.dot(lhs_ref[1, :count], weight_ref[which, 0], preferred_element_type=F32)
        return total + jnp.dot(lhs_ref[0, :count], weight_ref[which, 1], preferred_element_type=F32)

    def put(row, re, im):
        for half, part in enumerate((re, im)):
            high = part.astype(BF16)
            low = (part - high.astype(F32)).astype(BF16)
            lhs_ref[0, row:row + rows, half * LANES:(half + 1) * LANES] = high
            lhs_ref[1, row:row + rows, half * LANES:(half + 1) * LANES] = low

    chunks = []
    for l in range(nl):
        for h in range(per):
            chunks.append(jnp.concatenate([tile(z, l, h) for z in range(stacks)], axis=0))
    zero = jnp.zeros((rows, LANES), F32)
    for s, (re, im) in enumerate(real_dft(chunks)):
        if s:
            cr, ci = table_ref[0, s:s + 1], table_ref[1, s:s + 1]
            if im is None:
                re, im = re * cr, -re * ci
            else:
                re, im = re * cr + im * ci, im * cr - re * ci
        put(s * rows, re, zero if im is None else im)
    spec_ref[...] = product(0, groups * rows)

    def column(a):
        return jnp.broadcast_to(a, (a.shape[0], LANES))

    if plan.packed:
        limit = column(coef_ref[...])
        place = lax.broadcasted_iota(jnp.int32, (rows, LANES), 0) % (2 * tall)
        has_up = jnp.where(place < 2 * tall - 1, 1.0, 0.0)
        has_down = jnp.where(place > 0, 1.0, 0.0)
        pair = [edge_tile(z, 0) for z in range(2)]
        zonal = jnp.concatenate([column(t[:, 1:2]) for t in pair] * (stacks // 2), axis=0)
        merid = jnp.concatenate([column(t[:, 2:3]) for t in pair] * (stacks // 2), axis=0)
    else:
        limit, has_up, has_down, zonal, merid = (column(coef_ref[:, i:i + 1]) for i in range(5))
    zonal2, merid_up, merid_down = zonal * zonal, merid * has_up, merid * has_down
    limit2 = limit * limit

    def above(a):
        return pltpu.roll(a, rows - 1, 0)

    def below(a):
        return pltpu.roll(a, 1, 0)

    for s in range(groups):
        wavenum, inverse2, slope = (table_ref[i, s:s + 1] for i in (2, 3, 4))
        factor = jnp.where(wavenum > limit, limit2 * inverse2, 1.0)
        parts = [spec_ref[s * rows:(s + 1) * rows, half * LANES:(half + 1) * LANES] for half in (0, 1)]
        spread2 = zonal2 * (slope * slope)
        filtered = [factor * part for part in parts]
        merids, divs = [], []
        for part, filt in zip(parts, filtered):
            across = factor * (has_up * above(part) - has_down * below(part))
            flux = merid * across
            merids.append(across)
            divs.append(spread2 * filt - merid_up * above(flux) + merid_down * below(flux))
        spectra = {"d": divs, "u": (-slope * filtered[1], slope * filtered[0]), "v": merids}
        for field, name in enumerate(plan.fields(full)):
            put((field * groups + s) * rows, *spectra[name])

    count = len(plan.fields(full)) * groups * rows
    work_ref[...] = product(1, count)
    results = []
    for field in range(len(plan.fields(full))):
        spectrum = []
        for s in range(groups):
            base = (field * groups + s) * rows
            re = work_ref[base:base + rows, :LANES]
            im = work_ref[base:base + rows, LANES:]
            if s:
                cr, ci = table_ref[0, s:s + 1], table_ref[1, s:s + 1]
                re, im = re * cr - im * ci, (None if s == groups - 1 else re * ci + im * cr)
            else:
                im = None
            spectrum.append((re, im))
        result = real_dft_inverse(spectrum)
        results.append([piece * (1.0 / length) for piece in result])

    row = lax.broadcasted_iota(jnp.int32, (band, LANES), 0)
    lane = lax.broadcasted_iota(jnp.int32, (band, LANES), 1)
    for z in range(stacks):
        first = z * tall + skip
        last = first + band
        own_zonal = zonal[first:last]
        if plan.packed:
            edges = [edge_tile(z, l) for l in range(nl)]
            spot = per * tall
            side = band - 1 if z % 2 == 0 else 0
            sign = 1.0 if z % 2 == 0 else -1.0
            v_weight = jnp.where(row == side, sign * merid[first:last], 0.0)
            west = jnp.where(lane == 0, -own_zonal, 0.0)
            east = jnp.where(lane == LANES - 1, own_zonal, 0.0)
        for l in range(nl):
            here = block(z, l)
            if plan.packed and full:
                for field in range(2):
                    for h in range(per):
                        at = (field * per + h) * band
                        out_ref[here, at:at + band] = results[field][l * per + h][first:last]
                u, v = results
                before = u[(l * per - 1) % pieces][first:last]
                after = u[(l * per + per) % pieces][first:last]
                before = edges[l - 1] - own_zonal * pltpu.roll(before, 1, 1)
                after = edges[(l + 1) % nl] - own_zonal * pltpu.roll(after, LANES - 1, 1)
                edge = jnp.where(lane == 0, before, jnp.where(lane == LANES - 1, after, 0.0))
                at = 2 * per * band
                out_ref[here, at + 4:at + 8] = fold(edge, row)
                other = (z ^ 1) * tall + (0 if z % 2 == 0 else band - 1)
                for h in range(per):
                    moved = merid[other:other + 1] * v[l * per + h][other:other + 1]
                    out_ref[here, at + h:at + h + 1] = extra_ref[block(z ^ 1, l), spot + h:spot + h + 1] - moved
                if per < 4:
                    out_ref[here, at + per:at + 4] = jnp.zeros((4 - per, LANES), F32)
                continue
            for field in range(len(results)):
                for h in range(per):
                    value = results[field][l * per + h][first:last]
                    if plan.packed:
                        value += v_weight * extra_ref[block(z ^ 1, l), spot + h:spot + h + 1]
                        if h == 0:
                            value += west * edges[l - 1]
                        if h == per - 1:
                            value += east * edges[(l + 1) % nl]
                    out_ref[here, field * band:(field + 1) * band, h * LANES:(h + 1) * LANES] = value
    leave = pltpu.make_async_copy(out_ref, result_ref, sem)
    leave.start()
    leave.wait()


def fold(edge, row):
    edge = jnp.where(row < 4, edge, pltpu.roll(edge, LANES // 2, 1))
    return edge[:4] + edge[4:]


def unfold(part):
    return jnp.concatenate([part, pltpu.roll(part, LANES // 2, 1)], axis=0)


def transform(plan, full, coefs, weights, table, *operands):
    rows = len(plan.offsets) * plan.tall
    fields = len(plan.fields(full))
    groups = table.shape[1]
    count = fields * groups * rows
    blocks, width = operands[0].shape[0], plan.per * LANES
    shape = (blocks, fields * plan.band, width)
    if plan.packed and full:
        shape = (blocks, (2 * plan.per + 1) * plan.band, LANES)
    return pl.pallas_call(
        functools.partial(transform_kernel, plan, full),
        out_specs=pl.BlockSpec(memory_space=pltpu.HBM),
        out_shape=jax.ShapeDtypeStruct(shape, F32),
        scratch_shapes=[
            pltpu.VMEM((2, count, 2 * LANES), BF16),
            pltpu.VMEM((groups * rows, 2 * LANES), F32),
            pltpu.VMEM((count, 2 * LANES), F32),
            pltpu.VMEM(shape, F32),
            pltpu.SemaphoreType.DMA,
        ],
        compiler_params=KERNEL,
        cost_estimate=pl.CostEstimate(flops=6 * 2 * 65536 * count, bytes_accessed=32 * blocks * plan.band * width, transcendentals=0),
        name="transform_all" if full else "transform_div",
    )(*operands, coefs, weights, table)


def pack_kernel(zonal_ref, merid_ref, p_ref, u_ref, v_ref, result_ref, rows_ref, out_ref, u_buf, v_buf, sems):
    levels, band, width = u_buf.shape
    per = width // LANES
    moves = [pltpu.make_async_copy(u_ref, u_buf, sems.at[0]), pltpu.make_async_copy(v_ref, v_buf, sems.at[1])]
    for h in range(per):
        source = p_ref.at[:, :, pl.ds(h * LANES, LANES)]
        moves.append(pltpu.make_async_copy(source, out_ref.at[:, pl.ds(h * band, band)], sems.at[2 + h]))
    for move in moves:
        move.start()
    odd = lax.axis_index("lat") % 2 == 1
    row = lax.broadcasted_iota(jnp.int32, (band, LANES), 0)
    lane = lax.broadcasted_iota(jnp.int32, (band, LANES), 1)
    coefs = jnp.zeros((band, LANES), F32)
    for j in range(band):
        coefs = jnp.where(row == j, jnp.where(lane == 1, zonal_ref[j], jnp.where(lane == 2, merid_ref[j], 0.0)), coefs)
    facing = jnp.where(odd, merid_ref[band - 1], merid_ref[0])
    blank = jnp.zeros((4 - per, LANES), F32)
    for move in moves:
        move.wait()
    for k in range(levels):
        west = pltpu.roll(u_buf[k, :, width - LANES:], 1, 1)
        east = pltpu.roll(u_buf[k, :, :LANES], LANES - 1, 1)
        edge = jnp.where(lane == 0, west, jnp.where(lane == LANES - 1, east, coefs))
        base = per * band
        out_ref[k, base + 4:base + 8] = fold(edge, row)
        for h in range(per):
            lanes = slice(h * LANES, (h + 1) * LANES)
            top, bottom = v_buf[k, :1, lanes], v_buf[k, band - 1:, lanes]
            out_ref[k, base + h:base + h + 1] = jnp.where(odd, top, bottom)
            rows_ref[k, 2:3, lanes] = jnp.where(odd, bottom, top)
            rows_ref[k, :2, lanes] = jnp.where(odd, out_ref[k, h * band + band - 2:h * band + band], out_ref[k, h * band:h * band + 2])
        rows_ref[k, 3:4] = jnp.full((1, width), facing, F32)
        if per < 4:
            out_ref[k, base + per:base + 4] = blank
    leave = pltpu.make_async_copy(out_ref, result_ref, sems.at[0])
    leave.start()
    leave.wait()


def pack(zonal, merid, p, u, v):
    levels, band, width = p.shape
    shape = (levels, (width // LANES + 1) * band, LANES)
    hbm = pl.BlockSpec(memory_space=pltpu.HBM)
    return pl.pallas_call(
        pack_kernel,
        in_specs=[pl.BlockSpec(memory_space=pltpu.SMEM)] * 2 + [hbm] * 3,
        out_specs=[hbm, pl.BlockSpec(memory_space=pltpu.VMEM)],
        out_shape=[jax.ShapeDtypeStruct(shape, F32), jax.ShapeDtypeStruct((levels, 4, width), F32)],
        scratch_shapes=[
            pltpu.VMEM(shape, F32),
            pltpu.VMEM(p.shape, F32),
            pltpu.VMEM(p.shape, F32),
            pltpu.SemaphoreType.DMA((2 + width // LANES,)),
        ],
        compiler_params=ALONE,
        cost_estimate=pl.CostEstimate(flops=p.size, bytes_accessed=16 * p.size, transcendentals=0),
        name="pack_circles",
    )(zonal, merid, p, u, v)


def factor_kernel(level_ref, sound_ref, *refs):
    if len(refs) > 1:
        u_ref, v_ref, own_ref, inv_ref, base_ref = refs
        band, width = u_ref.shape[1:]
        row = lax.broadcasted_iota(jnp.int32, (band, width), 0)
        lane = lax.broadcasted_iota(jnp.int32, (band, width), 1)
        zonal, merid = own_ref[:, 0:1], own_ref[:, 1:2]
        east = jnp.where(lane < width - 1, zonal, 0.0)
        west = jnp.where(lane > 0, zonal, 0.0)
        north = jnp.where(row < band - 1, merid, 0.0)
        south = jnp.where(row > 0, merid, 0.0)
    else:
        (inv_ref,) = refs
    levels = sound_ref.shape[0]
    prev = jnp.zeros(sound_ref.shape[1:], F32)
    for k in range(levels):
        alpha = level_ref[k]
        below = alpha * sound_ref[k]
        above = alpha * sound_ref[k + 1] if k + 1 < levels else jnp.zeros_like(below)
        inv = 1.0 / (1.0 + below + above + below * prev)
        prev = -above * inv
        inv_ref[k] = inv
        if len(refs) > 1:
            u, v = u_ref[k], v_ref[k]
            div = east * pltpu.roll(u, width - 1, 1) - west * pltpu.roll(u, 1, 1)
            base_ref[k] = div + north * pltpu.roll(v, band - 1, 0) - south * pltpu.roll(v, 1, 0)


def factor(level_coef, sound, *winds):
    shape = jax.ShapeDtypeStruct(sound.shape, F32)
    count = 1 + len(winds)
    return pl.pallas_call(
        factor_kernel,
        in_specs=[pl.BlockSpec(memory_space=pltpu.SMEM)] + [pl.BlockSpec(memory_space=pltpu.VMEM)] * count,
        out_shape=[shape] * (2 if winds else 1),
        compiler_params=KERNEL,
        cost_estimate=pl.CostEstimate(flops=10 * sound.size, bytes_accessed=16 * sound.size, transcendentals=0),
        name="factor_columns",
    )(level_coef, sound, *winds)


def border_weights(own_ref, near, nz, shape, first_step):
    band = shape[0]
    me = lax.axis_index("lat")
    low, high = me == nz // 2 - 1, me == nz // 2
    row = lax.broadcasted_iota(jnp.int32, shape, 0)
    merid = jnp.broadcast_to(own_ref[:, 1:2], shape)
    last, first = merid[band - 1:], merid[:1]
    on_v = jnp.where(low & (row == band - 1), merid, jnp.where(high & (row == 0), -merid, 0.0))
    if not first_step:
        v_first = jnp.where(low & (row == band - 1), merid, 0.0)
        v_second = jnp.where(high & (row == 0), -merid, 0.0)
        return v_first, v_second
    inner = jnp.where(low & (row == band - 2), -merid * last, 0.0)
    outer = jnp.where(low & (row == band - 1), -merid * near, 0.0)
    on_first = jnp.where(high & (row == 0), -merid * near, inner)
    on_second = jnp.where(high & (row == 1), -merid * first, outer)
    on_own = -jnp.where(high & (row == 0), -merid * near, outer)
    return on_first, on_second, on_own, on_v


def sweep(level_ref, sound_ref, inv_ref, w_ref, star, w_out, p_out, finish):
    levels = sound_ref.shape[0]
    here = star(0)
    value = None
    for k in range(levels):
        alpha = level_ref[k]
        p_out[k] = here
        if k + 1 < levels:
            upper = star(k + 1)
            rhs = w_ref[k] - alpha * (upper - here)
            here = upper
        else:
            rhs = w_ref[k] + alpha * here
        inv = inv_ref[k]
        scaled = rhs * inv
        value = scaled if value is None else scaled + (alpha * sound_ref[k] * inv) * value
        w_out[k] = value
    upper = w_out[levels - 1]
    for k in range(levels - 1, -1, -1):
        lower = None
        if k:
            lower = w_out[k - 1] + (level_ref[k - 1] * sound_ref[k] * inv_ref[k - 1]) * upper
            w_out[k - 1] = lower
        fresh = p_out[k] - sound_ref[k] * (upper if lower is None else upper - lower)
        p_out[k] = fresh
        finish(k, fresh)
        upper = lower


def column_first_kernel(nz, level_ref, own_ref, sound_ref, inv_ref, base_ref, div_ref, p_ref, w_ref, *refs):
    _, band, width = sound_ref.shape
    per = width // LANES
    if nz:
        edge_ref, w_out, p_out, sum_out, rows_out = refs
        weights = border_weights(own_ref, edge_ref[0, 3:4], nz, (band, width), True)
        odd = lax.axis_index("lat") % 2 == 1
    else:
        w_out, p_out = refs

    def star(k):
        div = base_ref[k] + div_ref[k]
        if nz:
            div += weights[0] * edge_ref[k, 0:1] + weights[1] * edge_ref[k, 1:2]
            div += weights[2] * p_ref[k] + weights[3] * edge_ref[k, 2:3]
        return p_ref[k] - sound_ref[k] * div

    def finish(k, fresh):
        if nz:
            total = p_ref[k] + fresh
            rows_out[k] = jnp.where(odd, total[band - 2:], total[:2])
            for h in range(per):
                sum_out[k, h * band:(h + 1) * band] = total[:, h * LANES:(h + 1) * LANES]

    sweep(level_ref, sound_ref, inv_ref, w_ref, star, w_out, p_out, finish)


def column_last_kernel(nz, level_ref, own_ref, sound_ref, inv_ref, field_ref, p_ref, w_ref, u_ref, v_ref, *refs):
    _, band, width = sound_ref.shape
    per = width // LANES
    zonal = jnp.broadcast_to(own_ref[:, 0:1], (band, width))
    merid = jnp.broadcast_to(own_ref[:, 1:2], (band, width))
    if nz:
        edge_ref, facing_ref, rows_ref, u_out, v_out, w_out, p_out = refs
        near = edge_ref[0, 3:4]
        weights = border_weights(own_ref, near, nz, (band, width), False)
        odd = lax.axis_index("lat") % 2 == 1
        row = lax.broadcasted_iota(jnp.int32, (band, width), 0)
        lane = lax.broadcasted_iota(jnp.int32, (band, width), 1)
    else:
        base_ref, u_out, v_out, w_out, p_out = refs

    def wide(k, at):
        return jnp.concatenate([field_ref[k, at + h * band:at + (h + 1) * band] for h in range(per)], axis=1)

    def star(k):
        if not nz:
            u_out[k] = u_ref[k] - zonal * field_ref[k, band:2 * band]
            v_out[k] = v_ref[k] - merid * field_ref[k, 2 * band:]
            return p_ref[k] - sound_ref[k] * (base_ref[k] + field_ref[k, :band])
        u = u_ref[k] - zonal * wide(k, 0)
        v = v_ref[k] - merid * wide(k, per * band)
        far, mine = facing_ref[k], rows_ref[k]
        v -= weights[0] * far[0:1] + weights[1] * far[1:2]
        u_out[k], v_out[k] = u, v
        at = 2 * per * band
        sides = jnp.concatenate([unfold(field_ref[k, at + 4:at + 8])] * per, axis=1)
        pair = jnp.concatenate([field_ref[k, at + h:at + h + 1] for h in range(per)], axis=1)
        half = edge_ref[k, 2:3] - near * jnp.where(odd, far[1:2] - mine[1:2], mine[0:1] - far[0:1])
        north, south = jnp.where(odd, half, pair), jnp.where(odd, pair, half)
        east = jnp.where(lane == width - 1, sides, pltpu.roll(u, width - 1, 1))
        west = jnp.where(lane == 0, sides, pltpu.roll(u, 1, 1))
        up = jnp.where(row == band - 1, north, pltpu.roll(v, band - 1, 0))
        down = jnp.where(row == 0, south, pltpu.roll(v, 1, 0))
        return p_ref[k] - sound_ref[k] * (zonal * (east - west) + merid * (up - down))

    sweep(level_ref, sound_ref, inv_ref, w_ref, star, w_out, p_out, lambda k, fresh: None)


def column(first, nz, level_coef, own, sound, *operands):
    levels, band, width = sound.shape
    shapes = [jax.ShapeDtypeStruct(sound.shape, F32)] * (2 if first else 4)
    if first and nz:
        shapes.append(jax.ShapeDtypeStruct((levels, width // LANES * band, LANES), F32))
        shapes.append(jax.ShapeDtypeStruct((levels, 2, width), F32))
    return pl.pallas_call(
        functools.partial(column_first_kernel if first else column_last_kernel, nz),
        in_specs=[pl.BlockSpec(memory_space=pltpu.SMEM)] + [pl.BlockSpec(memory_space=pltpu.VMEM)] * (2 + len(operands)),
        out_shape=shapes,
        compiler_params=KERNEL,
        cost_estimate=pl.CostEstimate(flops=20 * sound.size, bytes_accessed=40 * sound.size, transcendentals=0),
        name="column_first" if first else "column_last",
    )(level_coef, own, sound, *operands)


def shifted(block, axis, step):
    count = lax.axis_size(axis)
    return lax.ppermute(block, axis, [(i, (i + step) % count) for i in range(count)])


def exchange(block, halves):
    axes, members = "lon", None
    if halves:
        axes = ("lat", "lon")
        count = lax.axis_size(axes)
        members = np.arange(count).reshape(2, count // 2).tolist()
    return lax.all_to_all(block, axes, split_axis=0, concat_axis=0, axis_index_groups=members, tiled=True)


def swapped(block, first):
    count = lax.axis_size("lat")
    pairs = [(i, i + 1) for i in range(first, count - 1, 2)]
    return lax.ppermute(block, "lat", pairs + [(b, a) for a, b in pairs])


def lat_edges(last, first):
    count = lax.axis_size("lat")
    low = lax.ppermute(last, "lat", [(i, i + 1) for i in range(count - 1)])
    high = lax.ppermute(first, "lat", [(i + 1, i) for i in range(count - 1)])
    return low, high


def program(
    zonal_wind,
    merid_wind,
    vertical_wind,
    pressure,
    zonal_coef,
    merid_coef,
    level_coef,
    sound_coef,
    cutoff,
    filter_mask,
):
    levels, band, width = pressure.shape
    nz, nl = lax.axis_size("lat"), lax.axis_size("lon")
    length = width * nl
    lats = band * nz
    me = lax.axis_index("lat")
    weights, table = tables(length)
    own = jnp.stack([zonal_coef, merid_coef], axis=1)
    limit = jnp.where(filter_mask > 0, cutoff, length).astype(F32)
    per = width // LANES

    if nz == 4 and band == 8 and per <= 4 and levels % (2 * nl) == 0:
        depth = levels // (2 * nl)
        offsets = tuple(z * nl * depth + c for c in range(depth) for z in range(2))
        plan = Plan(True, offsets, depth, nl, per, band, 0, band)
        sent, rows = pack(zonal_coef, merid_coef, pressure, zonal_wind, merid_wind)
        circles = exchange(sent, True)
        edges = swapped(rows, 1)
        limits = lax.dynamic_slice_in_dim(limit, me // 2 * 2 * band, 2 * band)
        limits = jnp.tile(limits, depth)[:, None]
        inv, base = factor(level_coef, sound_coef, zonal_wind, merid_wind, own)
        div = transform(plan, False, limits, weights, table, circles)
        div = exchange(div, True)
        w, p, total, rows = column(True, nz, level_coef, own, sound_coef, inv, base, div, pressure, vertical_wind, edges)
        facing = swapped(rows, 1)
        fields = transform(plan, True, limits, weights, table, exchange(total, True), circles)
        fields = exchange(fields, True)
        return column(False, nz, level_coef, own, sound_coef, inv, fields, p, w, zonal_wind, merid_wind, edges, facing, rows)

    depth, halo = levels // nl, 2
    tall = -(-(band + 2 * halo) // 8) * 8
    plan = Plan(False, tuple(range(depth)), depth, nl, per, tall, halo, band)

    def spread(field):
        low, high = lat_edges(field[:, -halo:], field[:, :halo])
        field = jnp.concatenate([low, field, high], axis=1)
        field = jnp.pad(field, ((0, 0), (0, tall - band - 2 * halo), (0, 0)))
        field = field.reshape(levels, tall, per, LANES).swapaxes(1, 2)
        return exchange(field.reshape(levels, per * tall, LANES), False)

    circles = spread(pressure)
    low, high = lat_edges(own[-halo:], own[:halo])
    v_low, v_high = lat_edges(merid_wind[:, -1:], merid_wind[:, :1])
    row = jnp.arange(lats + 2 * halo) - halo
    limit = jnp.pad(limit, (halo, halo), constant_values=1.0)
    known = jnp.stack([limit, (row < lats - 1).astype(F32), (row > 0).astype(F32)], axis=1)
    known = lax.dynamic_slice_in_dim(known, me * band, band + 2 * halo, 0)
    coefs = jnp.concatenate([known, jnp.concatenate([low, own, high])], axis=1)
    coefs = jnp.tile(jnp.pad(coefs, ((0, tall - band - 2 * halo), (0, 0))), (depth, 1))

    u_low = shifted(zonal_wind[:, :, -1:], "lon", 1)
    u_high = shifted(zonal_wind[:, :, :1], "lon", -1)
    u_diff = jnp.concatenate([zonal_wind[:, :, 1:], u_high], 2) - jnp.concatenate([u_low, zonal_wind[:, :, :-1]], 2)
    v_diff = jnp.concatenate([merid_wind[:, 1:], v_high], 1) - jnp.concatenate([v_low, merid_wind[:, :-1]], 1)
    base = zonal_coef[None, :, None] * u_diff + merid_coef[None, :, None] * v_diff

    (inv,) = factor(level_coef, sound_coef)
    div = transform(plan, False, coefs, weights, table, circles)
    div = exchange(div, False)
    w, p = column(True, 0, level_coef, own, sound_coef, inv, base, div, pressure, vertical_wind)
    fields = transform(plan, True, coefs, weights, table, spread(pressure + p))
    fields = exchange(fields, False)
    return column(False, 0, level_coef, own, sound_coef, inv, fields, p, w, zonal_wind, merid_wind, base)


def solution(mesh):
    spec = P(None, "lat", "lon")
    in_specs = (spec, spec, spec, spec, P("lat"), P("lat"), P(), spec, P(), P())
    return jax.shard_map(program, mesh=mesh, in_specs=in_specs, out_specs=(spec,) * 4, check_vma=False)
```

time: 79.4 us -> 66.9 us (0.84)
  starting transfers between devices: 24.6 us -> 15.2 us
  waiting for transfers between devices: 29.6 us -> 24.2 us
  Pallas kernels: 7.08 us -> 10.9 us
  other arithmetic: 1.35 us -> 0.01 us
    ppermute x7 -> x2, starting transfers between devices: 14.8 us -> 1.33 us  [swapped(): return lax.ppermute(block, 'lat', pairs + [(b, a) for a, b in pairs])]
    all_to_all x3, waiting for transfers between devices: 29.5 us -> 24.2 us  [exchange(): lax.all_to_all(block, axes, split_axis=0, concat_axis=0, axis_index_group...]
    all_to_all x3, starting transfers between devices: 9.81 us -> 13.9 us  [exchange(): lax.all_to_all(block, axes, split_axis=0, concat_axis=0, axis_index_group...]
    pallas_call x4 -> x5, Pallas kernels: 6.26 us -> 10 us  [the longest x2 3.75 us: transform(): pl.pallas_call(functools.partial(transform_kernel, plan, full), out_specs...]
    add x1 -> x0, other arithmetic: 1.22 us -> none  [program(): base = zonal_rows * u_diff + merid_rows * v_diff]
    unnamed x28 -> x30, local copies, waits for them, and re-layouts: 2.16 us -> 2.62 us
  transfers between devices with their start and end apart: 10 -> 5, of which waited for: 3 -> 3; matrix products, arithmetic and copies ran while one was open for 2% -> 0% of each run, Pallas kernels for 3% -> 1%
where the time goes in v3:
time: 66.9 us; the launch traced here: 66.4 us
  waiting for transfers between devices  24.2 us (36%)
  starting transfers between devices  15.2 us (23%)
  blocking collectives  12.3 us (18%)
  Pallas kernels  10.9 us (16%)
  local copies, waits for them, and re-layouts  2.86 us (4%)
  between operations  0.85 us (1%)
    all_to_all x3, waiting for transfers between devices, exchange(): lax.all_to_all(block, axes, split_axis=0, concat_axis=0, axis_index_group...  24.2 us
    all_to_all x3, starting transfers between devices, exchange(): lax.all_to_all(block, axes, split_axis=0, concat_axis=0, axis_index_group...  13.9 us
    all_to_all x1, blocking collectives, exchange(): lax.all_to_all(block, axes, split_axis=0, concat_axis=0, axis_index_group...  12.3 us
    pallas_call x2, Pallas kernels, transform(): pl.pallas_call(functools.partial(transform_kernel, plan, full), out_specs...  3.75 us
    pallas_call x1, Pallas kernels, pack(): pl.pallas_call(pack_kernel, in_specs=[pl.BlockSpec(memory_space=pltpu.SME...  3.47 us
    pallas_call x2, Pallas kernels, column(): pl.pallas_call(functools.partial(column_first_kernel if first else column...  2.8 us
    unnamed x30, local copies, waits for them, and re-layouts  2.62 us
  transfers between devices with their start and end apart: 5, of which 3 were waited for; matrix products, arithmetic and copies ran while one was open for 0% of the time, Pallas kernels for 1%

profile of v3, /device:TPU:0, one launch (start us, length us, event | category | flops | bytes accessed | tf_op | source)
XLA Modules:
  0.0 66.4 jit_solution(16643851077453410495)
XLA Ops:
  0.6 3.5 %pack_circles.1 = (f32[32,24,128]{2,1,0:T(8,128)}, f32[32,4,256]{2,1,0:T(4,128)}) custom-call(f32[8]{0:T(128)} %zonal_ref.1, f32[8]{0:T(128)} %merid_ref.1, f32[32,8,256]{2,1,0:T(8,128)} %p_ref.3, f32[32,8,256]{2,1,0:T(8,128)} %u_ref.3, f32[32,8,256]{2,1,0:T(8,128)} %v_ref.3), custom_call_target="tpu_custom_call" | custom-call | flops 65536 | bytes 1048576 | tf_op jit(solution)/shard_map/pack_circles/pallas_call | solution.py:373
  4.1 0.0 copy-start.3
  4.1 6.5 %all-to-all-start = ((f32[32,24,128]{2,1,0:T(8,128)}), f32[32,24,128]{2,1,0:T(8,128)S(1)}, u32[]{:S(2)}, u32[]{:S(2)}) async-start(f32[32,24,128]{2,1,0:T(8,128)} %get-tuple-element.14), calls=%async_computation | async-start | bytes 786432 | tf_op jit(solution)/shard_map/all_to_all | solution.py:576
  10.6 0.0 copy-start.8
  10.6 0.0 copy-start.13
  10.6 0.0 copy-start.14
  10.6 0.6 copy-done.13
  11.3 0.0 copy-done.14
  11.3 0.1 dynamic_slice.3
  11.4 0.1 broadcast_in_dim_tile.4.refs_0_.refs_1_
  11.5 8.2 %all-to-all-done.x_ref.refs_0_ = f32[32,24,128]{2,1,0:T(8,128)S(1)} async-done(((f32[32,24,128]{2,1,0:T(8,128)}), f32[32,24,128]{2,1,0:T(8,128)S(1)}, u32[]{:S(2)}, u32[]{:S(2)}) %all-to-all-start) | async-done | bytes 393248 | tf_op jit(solution)/shard_map/all_to_all | solution.py:576
  19.7 0.0 copy-done.3
  19.7 0.0 copy-done.8
  19.7 0.0 copy-start.12
  19.7 0.0 copy-start.2
  19.7 1.7 %transform_div.1 = f32[32,8,256]{2,1,0:T(8,128)} custom-call(f32[32,24,128]{2,1,0:T(8,128)S(1)} %all-to-all-done.x_ref.refs_0_, f32[32,1]{1,0:T(8,128)S(1)} %broadcast_in_dim_tile.4.refs_0_.refs_1_, bf16[2,2,256,256]{3,2,1,0:T(8,128)(2,1)S(1)} %copy-done.3, f32[5,9,128]{2,1,0:T(8,128)S(1)} %copy-done.8), custom_call_target="tpu_custom_call" | custom-call | flops 226492416 | bytes 2097152 | tf_op jit(solution)/shard_map/transform_div/pallas_call | solution.py:313
  21.4 0.0 copy-start
  21.4 0.0 copy-start.1
  21.4 3.7 %all-to-all-start.1 = ((f32[32,8,256]{2,1,0:T(8,128)}), f32[32,8,256]{2,1,0:T(8,128)S(1)}, u32[]{:S(2)}, u32[]{:S(2)}) async-start(f32[32,8,256]{2,1,0:T(8,128)} %transform_div.1), calls=%async_computation.1 | async-start | bytes 524288 | tf_op jit(solution)/shard_map/all_to_all | solution.py:576
  25.1 0.0 copy-done.12
  25.1 0.7 %collective-permute-start = (f32[32,4,256]{2,1,0:T(4,128)S(1)}, f32[32,4,256]{2,1,0:T(4,128)S(1)}, u32[]{:S(2)}, u32[]{:S(2)}) collective-permute-start(f32[32,4,256]{2,1,0:T(4,128)S(1)} %copy-done.12), channel_id=1, source_target_pairs={{8,16},{16,8},{9,17},{17,9},{10,18},{18,10},{11,19},{19,11},{12,20... | collective-permute-start | bytes 393224 | tf_op jit(solution)/shard_map/ppermute | solution.py:582
  25.8 0.0 copy-start.10
  25.8 0.0 copy-start.11
  25.8 0.6 copy-done.10
  26.4 0.0 copy-done.11
  26.5 0.0 copy-start.9
  26.5 0.1 copy.24.refs_2_.own_ref
  26.6 0.0 copy-done.2
  26.6 0.0 copy-done
  26.6 0.0 copy-done.1
  26.6 0.6 copy-done.9
  27.1 0.0 copy-start.4
  27.1 0.0 copy-start.5
  27.1 0.9 %factor_columns.1 = (f32[32,8,256]{2,1,0:T(8,128)S(1)}, f32[32,8,256]{2,1,0:T(8,128)S(1)}) custom-call(f32[32]{0:T(128)S(1)} %copy-done.9, f32[32,8,256]{2,1,0:T(8,128)S(1)} %copy-done, f32[32,8,256]{2,1,0:T(8,128)S(1)} %copy-done.1, f32[32,8,256]{2,1,0:T(8,128)S(1)} %copy-done.2, f32[8,2]{1,0:T(8,128)S(1)} %copy.24.refs_2_.own_ref), custom_call_target="tpu_custom_call" | custom-call | flops 655360 | bytes 1048576 | tf_op jit(solution)/shard_map/factor_columns/pallas_call | solution.py:421
  28.0 0.0 collective-permute-done.refs_0_
  28.0 4.8 %all-to-all-done.1.div_ref = f32[32,8,256]{2,1,0:T(8,128)S(1)} async-done(((f32[32,8,256]{2,1,0:T(8,128)}), f32[32,8,256]{2,1,0:T(8,128)S(1)}, u32[]{:S(2)}, u32[]{:S(2)}) %all-to-all-start.1) | async-done | bytes 262176 | tf_op jit(solution)/shard_map/all_to_all | solution.py:576
  32.8 0.0 copy-done.4
  32.8 0.0 copy-done.5
  32.8 0.9 %column_first.1 = (f32[32,8,256]{2,1,0:T(8,128)S(1)}, f32[32,8,256]{2,1,0:T(8,128)S(1)}, f32[32,16,128]{2,1,0:T(8,128)S(1)}, f32[32,2,256]{2,1,0:T(2,128)S(1)}) custom-call(f32[32]{0:T(128)S(1)} %copy-done.9, f32[8,2]{1,0:T(8,128)S(1)} %copy.24.refs_2_.own_ref, f32[32,8,256]{2,1,0:T(8,128)S(1)} %copy-done, f32[32,8,256]{2,1,0:T(8,128)S(1)} %get-tuple-element.12.inv_ref, ...), custom_call_target="tpu_custom_call" | custom-call | flops 1310720 | bytes 2621440 | tf_op jit(solution)/shard_map/column_first/pallas_call | solution.py:555
  33.7 0.0 copy-start.6
  33.7 0.7 %copy-done.6 = f32[32,8,256]{2,1,0:T(8,128)} copy-done((f32[32,8,256]{2,1,0:T(8,128)}, f32[32,8,256]{2,1,0:T(8,128)S(1)}, u32[]{:S(2)}) %copy-start.6) | copy-done | bytes 262168
  34.4 12.3 %all_to_all.20.x_ref = f32[32,16,128]{2,1,0:T(8,128)S(1)} all-to-all(f32[32,16,128]{2,1,0:T(8,128)S(1)} %get-tuple-element.16), channel_id=1, replica_groups={{0,1,2,3,4,5,6,7,8,9,10,11,12,13,14,15},{16,17,18,19,20,21,22,23,24,25,..., dimensions={0} | all-to-all | bytes 524288 | tf_op jit(solution)/shard_map/all_to_all | solution.py:576
  46.7 2.1 %transform_all.1 = f32[32,40,128]{2,1,0:T(8,128)} custom-call(f32[32,16,128]{2,1,0:T(8,128)S(1)} %all_to_all.20.x_ref, f32[32,24,128]{2,1,0:T(8,128)S(1)} %all-to-all-done.x_ref.refs_0_, f32[32,1]{1,0:T(8,128)S(1)} %broadcast_in_dim_tile.4.refs_0_.refs_1_, bf16[2,2,256,256]{3,2,1,0:T(8,128)(2,1)S(1)} %copy-done.3, f32[5,9,128]{2,1,0:T(8,128)S(1)} %copy-done.8), custom_call_target="tpu_custom_call" | custom-call | flops 452984832 | bytes 2097152 | tf_op jit(solution)/shard_map/transform_all/pallas_call | solution.py:313
  48.8 0.0 copy-start.7
  48.9 3.7 %all-to-all-start.3 = ((f32[32,40,128]{2,1,0:T(8,128)}), f32[32,40,128]{2,1,0:T(8,128)S(1)}, u32[]{:S(2)}, u32[]{:S(2)}) async-start(f32[32,40,128]{2,1,0:T(8,128)} %transform_all.1), calls=%async_computation.3 | async-start | bytes 1310720 | tf_op jit(solution)/shard_map/all_to_all | solution.py:576
  52.6 0.7 %collective-permute-start.1 = (f32[32,2,256]{2,1,0:T(2,128)S(1)}, f32[32,2,256]{2,1,0:T(2,128)S(1)}, u32[]{:S(2)}, u32[]{:S(2)}) collective-permute-start(f32[32,2,256]{2,1,0:T(2,128)S(1)} %get-tuple-element.19.refs_2_), channel_id=1, source_target_pairs={{8,16},{16,8},{9,17},{17,9},{10,18},{18,10},{11,19},{19,11},{12,20... | collective-permute-start | bytes 196616 | tf_op jit(solution)/shard_map/ppermute | solution.py:582
  53.3 0.0 collective-permute-done.1.refs_1_
  53.3 11.2 %all-to-all-done.3.field_ref = f32[32,40,128]{2,1,0:T(8,128)S(1)} async-done(((f32[32,40,128]{2,1,0:T(8,128)}), f32[32,40,128]{2,1,0:T(8,128)S(1)}, u32[]{:S(2)}, u32[]{:S(2)}) %all-to-all-start.3) | async-done | bytes 655392 | tf_op jit(solution)/shard_map/all_to_all | solution.py:576
  64.5 0.0 copy-done.7
  64.5 1.9 %column_last.1 = (f32[32,8,256]{2,1,0:T(8,128)}, f32[32,8,256]{2,1,0:T(8,128)}, f32[32,8,256]{2,1,0:T(8,128)}, f32[32,8,256]{2,1,0:T(8,128)}) custom-call(f32[32]{0:T(128)S(1)} %copy-done.9, f32[8,2]{1,0:T(8,128)S(1)} %copy.24.refs_2_.own_ref, f32[32,8,256]{2,1,0:T(8,128)S(1)} %copy-done, f32[32,8,256]{2,1,0:T(8,128)S(1)} %get-tuple-element.12.inv_ref, ...), custom_call_target="tpu_custom_call" | custom-call | flops 1310720 | bytes 2621440 | tf_op jit(solution)/shard_map/column_last/pallas_call | solution.py:555
  (3 shorter events, 0.0 us)
Async XLA Ops:
  4.1 15.6 %copy-start.3 = (bf16[2,2,256,256]{3,2,1,0:T(8,128)(2,1)S(1)}, bf16[2,2,256,256]{3,2,1,0:T(8,128)(2,1)}, u32[]{:S(2)}) copy-start(bf16[2,2,256,256]{3,2,1,0:T(8,128)(2,1)} %constant.32.clone.refs_1_.refs_2_) | copy-start | bytes 1572868
  4.1 15.6 %all-to-all-start = ((f32[32,24,128]{2,1,0:T(8,128)}), f32[32,24,128]{2,1,0:T(8,128)S(1)}, u32[]{:S(2)}, u32[]{:S(2)}) async-start(f32[32,24,128]{2,1,0:T(8,128)} %get-tuple-element.14), calls=%async_computation | async-start | bytes 786432 | tf_op jit(solution)/shard_map/all_to_all | solution.py:576
  10.6 9.1 %copy-start.8 = (f32[5,9,128]{2,1,0:T(8,128)S(1)}, f32[5,9,128]{2,1,0:T(8,128)}, u32[]{:S(2)}) copy-start(f32[5,9,128]{2,1,0:T(8,128)} %constant.33.clone.refs_2_.refs_3_) | copy-start | bytes 69124
  10.6 0.7 copy-start.13
  10.6 0.7 copy-start.14
  19.7 5.4 %copy-start.12 = (f32[32,4,256]{2,1,0:T(4,128)S(1)}, f32[32,4,256]{2,1,0:T(4,128)}, u32[]{:S(2)}) copy-start(f32[32,4,256]{2,1,0:T(4,128)} %get-tuple-element.15) | copy-start | bytes 393220
  19.7 6.9 %copy-start.2 = (f32[32,8,256]{2,1,0:T(8,128)S(1)}, f32[32,8,256]{2,1,0:T(8,128)}, u32[]{:S(2)}) copy-start(f32[32,8,256]{2,1,0:T(8,128)} %v_ref.3) | copy-start | bytes 786436
  21.4 5.2 %copy-start = (f32[32,8,256]{2,1,0:T(8,128)S(1)}, f32[32,8,256]{2,1,0:T(8,128)}, u32[]{:S(2)}) copy-start(f32[32,8,256]{2,1,0:T(8,128)} %sound_ref.5) | copy-start | bytes 786436
  21.4 5.2 %copy-start.1 = (f32[32,8,256]{2,1,0:T(8,128)S(1)}, f32[32,8,256]{2,1,0:T(8,128)}, u32[]{:S(2)}) copy-start(f32[32,8,256]{2,1,0:T(8,128)} %u_ref.3) | copy-start | bytes 786436
  21.4 11.4 %all-to-all-start.1 = ((f32[32,8,256]{2,1,0:T(8,128)}), f32[32,8,256]{2,1,0:T(8,128)S(1)}, u32[]{:S(2)}, u32[]{:S(2)}) async-start(f32[32,8,256]{2,1,0:T(8,128)} %transform_div.1), calls=%async_computation.1 | async-start | bytes 524288 | tf_op jit(solution)/shard_map/all_to_all | solution.py:576
  25.1 2.9 %collective-permute-start = (f32[32,4,256]{2,1,0:T(4,128)S(1)}, f32[32,4,256]{2,1,0:T(4,128)S(1)}, u32[]{:S(2)}, u32[]{:S(2)}) collective-permute-start(f32[32,4,256]{2,1,0:T(4,128)S(1)} %copy-done.12), channel_id=1, source_target_pairs={{8,16},{16,8},{9,17},{17,9},{10,18},{18,10},{11,19},{19,11},{12,20... | collective-permute-start | bytes 393224 | tf_op jit(solution)/shard_map/ppermute | solution.py:582
  25.8 0.7 copy-start.10
  25.8 0.7 copy-start.11
  26.5 0.7 copy-start.9
  27.1 5.7 %copy-start.4 = (f32[32,8,256]{2,1,0:T(8,128)S(1)}, f32[32,8,256]{2,1,0:T(8,128)}, u32[]{:S(2)}) copy-start(f32[32,8,256]{2,1,0:T(8,128)} %p_ref.3) | copy-start | bytes 786436
  27.1 5.7 %copy-start.5 = (f32[32,8,256]{2,1,0:T(8,128)S(1)}, f32[32,8,256]{2,1,0:T(8,128)}, u32[]{:S(2)}) copy-start(f32[32,8,256]{2,1,0:T(8,128)} %w_ref.1) | copy-start | bytes 786436
  33.7 0.7 %copy-start.6 = (f32[32,8,256]{2,1,0:T(8,128)}, f32[32,8,256]{2,1,0:T(8,128)S(1)}, u32[]{:S(2)}) copy-start(f32[32,8,256]{2,1,0:T(8,128)S(1)} %get-tuple-element.17.p_ref) | copy-start | bytes 786436
  48.8 15.6 %copy-start.7 = (f32[32,8,256]{2,1,0:T(8,128)S(1)}, f32[32,8,256]{2,1,0:T(8,128)}, u32[]{:S(2)}) copy-start(f32[32,8,256]{2,1,0:T(8,128)} %copy-done.6) | copy-start | bytes 786436
  48.9 15.6 %all-to-all-start.3 = ((f32[32,40,128]{2,1,0:T(8,128)}), f32[32,40,128]{2,1,0:T(8,128)S(1)}, u32[]{:S(2)}, u32[]{:S(2)}) async-start(f32[32,40,128]{2,1,0:T(8,128)} %transform_all.1), calls=%async_computation.3 | async-start | bytes 1310720 | tf_op jit(solution)/shard_map/all_to_all | solution.py:576
  52.6 0.7 %collective-permute-start.1 = (f32[32,2,256]{2,1,0:T(2,128)S(1)}, f32[32,2,256]{2,1,0:T(2,128)S(1)}, u32[]{:S(2)}, u32[]{:S(2)}) collective-permute-start(f32[32,2,256]{2,1,0:T(2,128)S(1)} %get-tuple-element.19.refs_2_), channel_id=1, source_target_pairs={{8,16},{16,8},{9,17},{17,9},{10,18},{18,10},{11,19},{19,11},{12,20... | collective-permute-start | bytes 196616 | tf_op jit(solution)/shard_map/ppermute | solution.py:582

commit v4 on v3

v4 whole, which is shorter than its diff:
```python
import functools
import math
from typing import NamedTuple

import jax
import jax.numpy as jnp
import numpy as np
from jax import lax
from jax.experimental import pallas as pl
from jax.experimental.pallas import tpu as pltpu
from jax.sharding import PartitionSpec as P


LANES = 128
F32 = jnp.float32
BF16 = jnp.bfloat16
KERNEL = pltpu.CompilerParams(vmem_limit_bytes=8 << 20)
ALONE = pltpu.CompilerParams(vmem_limit_bytes=60 << 20)


class Plan(NamedTuple):
    packed: bool
    bands: int
    nl: int
    depth: int
    per: int
    tall: int
    skip: int
    band: int

    def fields(self, full):
        if not full:
            return "d"
        return "uv" if self.packed else "duv"


def cmul_const(re, im, cr, ci):
    if im is None:
        return (re * cr if cr != 0.0 else None, re * ci if ci != 0.0 else None)
    return (re * cr - im * ci, re * ci + im * cr)


def add(a, b):
    if a is None:
        return b
    return a if b is None else a + b


def sub(a, b):
    if b is None:
        return a
    return -b if a is None else a - b


def neg(a):
    return None if a is None else -a


def unit(num, den):
    turn = num % den
    table = {0: (1.0, 0.0), den / 4: (0.0, 1.0), den / 2: (-1.0, 0.0), 3 * den / 4: (0.0, -1.0)}
    if turn in table:
        return table[turn]
    angle = 2.0 * math.pi * turn / den
    return math.cos(angle), math.sin(angle)


def rotate(z, num, den):
    cr, ci = unit(num, den)
    re, im = z
    if (cr, ci) == (1.0, 0.0):
        return z
    if (cr, ci) == (0.0, 1.0):
        return (neg(im), re)
    if (cr, ci) == (0.0, -1.0):
        return (im, neg(re))
    return cmul_const(re, im, cr, ci)


def real_dft(pieces):
    n = len(pieces)
    if n == 1:
        return [(pieces[0], None)]
    even, odd = real_dft(pieces[0::2]), real_dft(pieces[1::2])
    out = [None] * (n // 2 + 1)
    for s in range(n // 4 + 1 if n > 2 else 1):
        er, ei = even[s]
        tr, ti = rotate(odd[s], -s, n)
        out[n // 2 - s] = (sub(er, tr), sub(ti, ei))
        out[s] = (add(er, tr), add(ei, ti))
    return out


def real_dft_inverse(groups):
    n = 2 * (len(groups) - 1)
    if n == 0:
        return [groups[0][0]]
    if n == 2:
        a, b = groups[0][0], groups[1][0]
        return [a + b, a - b]
    even, odd = [], []
    for s in range(n // 4 + 1):
        ar, ai = groups[s]
        br, bi = groups[n // 2 - s]
        even.append((add(ar, br), sub(ai, bi)))
        odd.append(rotate((sub(ar, br), add(ai, bi)), s, n))
    even[0] = (even[0][0], None)
    odd[0] = (odd[0][0], None)
    even[-1] = (even[-1][0], None)
    odd[-1] = (odd[-1][0], None)
    out = [None] * n
    out[0::2] = real_dft_inverse(even)
    out[1::2] = real_dft_inverse(odd)
    return out


def tables(length):
    pieces = length // LANES
    groups = pieces // 2 + 1
    lane = np.arange(LANES)
    angle = 2.0 * np.pi / LANES * (np.outer(lane, lane) % LANES)
    cos, sin = np.cos(angle), np.sin(angle)
    matrix = np.block([[cos, -sin], [sin, cos]])

    def halves(m):
        m = m.astype(np.float32)
        high = m.astype(BF16)
        return np.stack([high, (m - high.astype(np.float32)).astype(BF16)])

    weights = np.stack([halves(matrix), halves(matrix.T)])
    s = np.arange(groups)[:, None]
    turn = 2.0 * np.pi / length * (s * lane[None, :])
    wavenum = pieces * lane[None, :] + s
    wavenum = np.minimum(wavenum, length - wavenum).astype(np.float64)
    slope = 2.0 * np.sin(2.0 * np.pi / length * (pieces * lane[None, :] + s))
    rows = np.stack([np.cos(turn), np.sin(turn), wavenum, 1.0 / np.maximum(wavenum, 1.0) ** 2, slope])
    return weights, rows.astype(np.float32)


def transform_kernel(plan, full, x_ref, *refs):
    extra_ref = x_ref
    if plan.packed and full:
        extra_ref, refs = refs[0], refs[1:]
    coef_ref, weight_ref, table_ref, result_ref, lhs_ref, spec_ref, work_ref, out_ref, sems = refs
    bands, nl, depth, per = plan.bands, plan.nl, plan.depth, plan.per
    tall, skip, band = plan.tall, plan.skip, plan.band
    stacks = depth * bands
    pieces = nl * per
    groups = pieces // 2 + 1
    rows = stacks * tall
    length = pieces * LANES
    spot = depth * per * tall

    def tile(c, z, l, h):
        at = (c * per + h) * tall
        return x_ref[z * nl + l, at:at + tall]

    def edge_tile(c, z, l):
        return unfold(extra_ref[z * nl + l % nl, spot + 4:spot + 8], c)

    def product(which, start):
        high, low = (lhs_ref[i, start:start + groups * rows] for i in range(2))
        total = jnp.dot(high, weight_ref[which, 0], preferred_element_type=F32)
        total += jnp.dot(low, weight_ref[which, 0], preferred_element_type=F32)
        return total + jnp.dot(high, weight_ref[which, 1], preferred_element_type=F32)

    def put(row, re, im):
        for half, part in enumerate((re, im)):
            high = part.astype(BF16)
            low = (part - high.astype(F32)).astype(BF16)
            lhs_ref[0, row:row + rows, half * LANES:(half + 1) * LANES] = high
            lhs_ref[1, row:row + rows, half * LANES:(half + 1) * LANES] = low

    chunks = []
    for l in range(nl):
        for h in range(per):
            chunks.append(jnp.concatenate([tile(c, z, l, h) for c in range(depth) for z in range(bands)], axis=0))
    zero = jnp.zeros((rows, LANES), F32)
    for s, (re, im) in enumerate(real_dft(chunks)):
        if s:
            cr, ci = table_ref[0, s:s + 1], table_ref[1, s:s + 1]
            if im is None:
                re, im = re * cr, -re * ci
            else:
                re, im = re * cr + im * ci, im * cr - re * ci
        put(s * rows, re, zero if im is None else im)
    spec_ref[...] = product(0, 0)

    def column(a):
        return jnp.broadcast_to(a, (a.shape[0], LANES))

    if plan.packed:
        limit = column(coef_ref[...])
        place = lax.broadcasted_iota(jnp.int32, (rows, LANES), 0) % (bands * tall)
        has_up = jnp.where(place < bands * tall - 1, 1.0, 0.0)
        has_down = jnp.where(place > 0, 1.0, 0.0)
        pair = [edge_tile(0, z, 0) for z in range(bands)]
        zonal = jnp.concatenate([column(t[:, 1:2]) for t in pair] * depth, axis=0)
        merid = jnp.concatenate([column(t[:, 2:3]) for t in pair] * depth, axis=0)
    else:
        limit, has_up, has_down, zonal, merid = (column(coef_ref[:, i:i + 1]) for i in range(5))
    zonal2, merid_up, merid_down = zonal * zonal, merid * has_up, merid * has_down
    limit2 = limit * limit

    def above(a):
        return pltpu.roll(a, rows - 1, 0)

    def below(a):
        return pltpu.roll(a, 1, 0)

    for s in range(groups):
        wavenum, inverse2, slope = (table_ref[i, s:s + 1] for i in (2, 3, 4))
        factor = jnp.where(wavenum > limit, limit2 * inverse2, 1.0)
        parts = [spec_ref[s * rows:(s + 1) * rows, half * LANES:(half + 1) * LANES] for half in (0, 1)]
        spread2 = zonal2 * (slope * slope)
        filtered = [factor * part for part in parts]
        merids, divs = [], []
        for part, filt in zip(parts, filtered):
            across = factor * (has_up * above(part) - has_down * below(part))
            flux = merid * across
            merids.append(across)
            divs.append(spread2 * filt - merid_up * above(flux) + merid_down * below(flux))
        spectra = {"d": divs, "u": (-slope * filtered[1], slope * filtered[0]), "v": merids}
        for field, name in enumerate(plan.fields(full)):
            put((field * groups + s) * rows, *spectra[name])

    row = lax.broadcasted_iota(jnp.int32, (band, LANES), 0)
    lane = lax.broadcasted_iota(jnp.int32, (band, LANES), 1)
    cells = [(c, z, l) for c in range(depth) for z in range(bands) for l in range(nl)]

    def latitudes(c, z):
        first = (c * bands + z) * tall + skip
        return slice(first, first + band)

    leaving = []

    def leave(start, size):
        part = (slice(None), pl.ds(start, size))
        move = pltpu.make_async_copy(out_ref.at[part], result_ref.at[part], sems.at[len(leaving)])
        move.start()
        leaving.append(move)

    results = []
    for field in range(len(plan.fields(full))):
        base = field * groups * rows
        work_ref[...] = product(1, base)
        spectrum = []
        for s in range(groups):
            re = work_ref[s * rows:(s + 1) * rows, :LANES]
            im = work_ref[s * rows:(s + 1) * rows, LANES:]
            if s:
                cr, ci = table_ref[0, s:s + 1], table_ref[1, s:s + 1]
                re, im = re * cr - im * ci, (None if s == groups - 1 else re * ci + im * cr)
            else:
                im = None
            spectrum.append((re, im))
        result = [piece * (1.0 / length) for piece in real_dft_inverse(spectrum)]
        results.append(result)
        for c, z, l in cells:
            own = latitudes(c, z)
            if plan.packed and not full:
                side = band - 1 if z % 2 == 0 else 0
                v_weight = jnp.where(row == side, merid[own] if z % 2 == 0 else -merid[own], 0.0)
                at = spot + c * per
            for h in range(per):
                value = result[l * per + h][own]
                if plan.packed and full:
                    start = ((field * depth + c) * per + h) * band
                    out_ref[z * nl + l, start:start + band] = value
                    continue
                if plan.packed:
                    value += v_weight * extra_ref[(z ^ 1) * nl + l, at + h:at + h + 1]
                    if h == 0:
                        value += jnp.where(lane == 0, -zonal[own], 0.0) * edge_tile(c, z, l - 1)
                    if h == per - 1:
                        value += jnp.where(lane == LANES - 1, zonal[own], 0.0) * edge_tile(c, z, l + 1)
                start = (c * len(plan.fields(full)) + field) * band
                out_ref[z * nl + l, start:start + band, h * LANES:(h + 1) * LANES] = value
        if plan.packed and full:
            leave(field * depth * per * band, depth * per * band)
    if plan.packed and full:
        u, v = results
        base = 2 * depth * per * band
        for z in range(bands):
            for l in range(nl):
                edge = None
                for c in range(depth):
                    own = latitudes(c, z)
                    before = u[(l * per - 1) % pieces][own]
                    after = u[(l * per + per) % pieces][own]
                    before = edge_tile(c, z, l - 1) - zonal[own] * pltpu.roll(before, 1, 1)
                    after = edge_tile(c, z, l + 1) - zonal[own] * pltpu.roll(after, LANES - 1, 1)
                    sides = jnp.where(lane == 0, before, jnp.where(lane == LANES - 1, after, 0.0))
                    edge = sides if c == 0 else edge + pltpu.roll(sides, c * (LANES // 4), 1)
                    other = latitudes(c, z ^ 1)
                    other = other.start if z % 2 == 0 else other.stop - 1
                    at = c * per
                    for h in range(per):
                        moved = merid[other:other + 1] * v[l * per + h][other:other + 1]
                        known = extra_ref[(z ^ 1) * nl + l, spot + at + h:spot + at + h + 1]
                        out_ref[z * nl + l, base + at + h:base + at + h + 1] = known - moved
                out_ref[z * nl + l, base + 4:base + 8] = fold(edge, row)
                if depth * per < 4:
                    out_ref[z * nl + l, base + depth * per:base + 4] = jnp.zeros((4 - depth * per, LANES), F32)
        leave(base, 8)
    else:
        leave(0, out_ref.shape[1])
    for move in leaving:
        move.wait()


def fold(edge, row):
    edge = jnp.where(row < 4, edge, pltpu.roll(edge, LANES // 2, 1))
    return edge[:4] + edge[4:]


def unfold(part, c):
    tile = jnp.concatenate([part, pltpu.roll(part, LANES // 2, 1)], axis=0)
    return pltpu.roll(tile, LANES - c * (LANES // 4), 1) if c else tile


def transform(plan, full, coefs, weights, table, *operands):
    rows = plan.depth * plan.bands * plan.tall
    fields = len(plan.fields(full))
    groups = table.shape[1]
    count = fields * groups * rows
    blocks, width = operands[0].shape[0], plan.per * LANES
    shape = (blocks, plan.depth * fields * plan.band, width)
    if plan.packed and full:
        shape = (blocks, (2 * plan.depth * plan.per + 1) * plan.band, LANES)
    return pl.pallas_call(
        functools.partial(transform_kernel, plan, full),
        out_specs=pl.BlockSpec(memory_space=pltpu.HBM),
        out_shape=jax.ShapeDtypeStruct(shape, F32),
        scratch_shapes=[
            pltpu.VMEM((2, count, 2 * LANES), BF16),
            pltpu.VMEM((groups * rows, 2 * LANES), F32),
            pltpu.VMEM((groups * rows, 2 * LANES), F32),
            pltpu.VMEM(shape, F32),
            pltpu.SemaphoreType.DMA((3,)),
        ],
        compiler_params=KERNEL,
        cost_estimate=pl.CostEstimate(flops=6 * 2 * 65536 * count, bytes_accessed=32 * blocks * plan.depth * plan.band * width, transcendentals=0),
        name="transform_all" if full else "transform_div",
    )(*operands, coefs, weights, table)


def pack_kernel(zonal_ref, merid_ref, p_ref, u_ref, v_ref, result_ref, far_ref, zonal_s, merid_s, out_ref, rows_ref, u_buf, v_buf, in_sems, out_sems):
    blocks, depth, band, width = p_ref.shape
    per = width // LANES
    parts = in_sems.shape[0] - 1
    size = blocks // parts
    spot = depth * per * band

    def chunk(n):
        at = pl.ds(n * size, size)
        moves = [pltpu.make_async_copy(u_ref.at[at], u_buf.at[at], in_sems.at[n, 0]), pltpu.make_async_copy(v_ref.at[at], v_buf.at[at], in_sems.at[n, 1])]
        for c in range(depth):
            for h in range(per):
                source = p_ref.at[at, c, :, pl.ds(h * LANES, LANES)]
                target = out_ref.at[at, pl.ds((c * per + h) * band, band)]
                moves.append(pltpu.make_async_copy(source, target, in_sems.at[n, len(moves)]))
        return moves

    small = [pltpu.make_async_copy(zonal_ref, zonal_s, in_sems.at[parts, 0]), pltpu.make_async_copy(merid_ref, merid_s, in_sems.at[parts, 1])]
    entering = [chunk(n) for n in range(parts)]
    for move in small + sum(entering, []):
        move.start()
    odd = lax.axis_index("lat") % 2 == 1
    row = lax.broadcasted_iota(jnp.int32, (band, LANES), 0)
    lane = lax.broadcasted_iota(jnp.int32, (band, LANES), 1)
    for move in small:
        move.wait()
    coefs = jnp.zeros((band, LANES), F32)
    for j in range(band):
        coefs = jnp.where(row == j, jnp.where(lane == 1, zonal_s[j], jnp.where(lane == 2, merid_s[j], 0.0)), coefs)
    facing = jnp.full((1, width), jnp.where(odd, merid_s[band - 1], merid_s[0]), F32)
    leaving = []
    for n in range(parts):
        for move in entering[n]:
            move.wait()
        for b in range(n * size, (n + 1) * size):
            edge = coefs
            for c in range(depth):
                west = pltpu.roll(u_buf[b, c, :, width - LANES:], 1, 1)
                east = pltpu.roll(u_buf[b, c, :, :LANES], LANES - 1, 1)
                sides = jnp.where(lane == 0, west, jnp.where(lane == LANES - 1, east, 0.0))
                edge = edge + (pltpu.roll(sides, c * (LANES // 4), 1) if c else sides)
                k = b * depth + c
                for h in range(per):
                    lanes = slice(h * LANES, (h + 1) * LANES)
                    at = (c * per + h) * band
                    top, bottom = v_buf[b, c, :1, lanes], v_buf[b, c, band - 1:, lanes]
                    out_ref[b, spot + c * per + h:spot + c * per + h + 1] = jnp.where(odd, top, bottom)
                    rows_ref[k, 2:3, lanes] = jnp.where(odd, bottom, top)
                    rows_ref[k, :2, lanes] = jnp.where(odd, out_ref[b, at + band - 2:at + band], out_ref[b, at:at + 2])
                rows_ref[k, 3:4] = facing
            out_ref[b, spot + 4:spot + 8] = fold(edge, row)
            if depth * per < 4:
                out_ref[b, spot + depth * per:spot + 4] = jnp.zeros((4 - depth * per, LANES), F32)
        at = pl.ds(n * size, size)
        leaving.append(pltpu.make_async_copy(out_ref.at[at], result_ref.at[at], out_sems.at[n]))
        leaving[-1].start()
    leaving.append(pltpu.make_async_copy(rows_ref, far_ref, out_sems.at[parts]))
    leaving[-1].start()
    for move in leaving:
        move.wait()


def pack(zonal, merid, p, u, v):
    blocks, depth, band, width = p.shape
    per = width // LANES
    shape = (blocks, (depth * per + 1) * band, LANES)
    rows = (blocks * depth, 4, width)
    parts = 4 if blocks % 4 == 0 else 1
    hbm = pl.BlockSpec(memory_space=pltpu.HBM)
    return pl.pallas_call(
        pack_kernel,
        in_specs=[hbm] * 5,
        out_specs=[hbm, hbm],
        out_shape=[jax.ShapeDtypeStruct(shape, F32), jax.ShapeDtypeStruct(rows, F32)],
        scratch_shapes=[
            pltpu.SMEM((band,), F32),
            pltpu.SMEM((band,), F32),
            pltpu.VMEM(shape, F32),
            pltpu.VMEM(rows, F32),
            pltpu.VMEM(p.shape, F32),
            pltpu.VMEM(p.shape, F32),
            pltpu.SemaphoreType.DMA((parts + 1, 2 + depth * per)),
            pltpu.SemaphoreType.DMA((parts + 1,)),
        ],
        compiler_params=ALONE,
        cost_estimate=pl.CostEstimate(flops=p.size, bytes_accessed=16 * p.size, transcendentals=0),
        name="pack_circles",
    )(zonal, merid, p, u, v)


def factor_kernel(level_ref, sound_ref, *refs):
    if len(refs) > 1:
        u_ref, v_ref, own_ref, inv_ref, base_ref = refs
        band, width = u_ref.shape[1:]
        row = lax.broadcasted_iota(jnp.int32, (band, width), 0)
        lane = lax.broadcasted_iota(jnp.int32, (band, width), 1)
        zonal, merid = own_ref[:, 0:1], own_ref[:, 1:2]
        east = jnp.where(lane < width - 1, zonal, 0.0)
        west = jnp.where(lane > 0, zonal, 0.0)
        north = jnp.where(row < band - 1, merid, 0.0)
        south = jnp.where(row > 0, merid, 0.0)
    else:
        (inv_ref,) = refs
    levels = sound_ref.shape[0]
    prev = jnp.zeros(sound_ref.shape[1:], F32)
    for k in range(levels):
        alpha = level_ref[k:k + 1]
        below = alpha * sound_ref[k]
        above = alpha * sound_ref[k + 1] if k + 1 < levels else jnp.zeros_like(below)
        inv = 1.0 / (1.0 + below + above + below * prev)
        prev = -above * inv
        inv_ref[k] = inv
        if len(refs) > 1:
            u, v = u_ref[k], v_ref[k]
            div = east * pltpu.roll(u, width - 1, 1) - west * pltpu.roll(u, 1, 1)
            base_ref[k] = div + north * pltpu.roll(v, band - 1, 0) - south * pltpu.roll(v, 1, 0)


def factor(level_coef, sound, *winds):
    shape = jax.ShapeDtypeStruct(sound.shape, F32)
    count = 1 + len(winds)
    return pl.pallas_call(
        factor_kernel,
        in_specs=[pl.BlockSpec(memory_space=pltpu.VMEM)] * (1 + count),
        out_shape=[shape] * (2 if winds else 1),
        compiler_params=KERNEL,
        cost_estimate=pl.CostEstimate(flops=10 * sound.size, bytes_accessed=16 * sound.size, transcendentals=0),
        name="factor_columns",
    )(level_coef, sound, *winds)


def border_weights(own_ref, near, nz, shape, first_step):
    band = shape[0]
    me = lax.axis_index("lat")
    low, high = me == nz // 2 - 1, me == nz // 2
    row = lax.broadcasted_iota(jnp.int32, shape, 0)
    merid = jnp.broadcast_to(own_ref[:, 1:2], shape)
    last, first = merid[band - 1:], merid[:1]
    on_v = jnp.where(low & (row == band - 1), merid, jnp.where(high & (row == 0), -merid, 0.0))
    if not first_step:
        v_first = jnp.where(low & (row == band - 1), merid, 0.0)
        v_second = jnp.where(high & (row == 0), -merid, 0.0)
        return v_first, v_second
    inner = jnp.where(low & (row == band - 2), -merid * last, 0.0)
    outer = jnp.where(low & (row == band - 1), -merid * near, 0.0)
    on_first = jnp.where(high & (row == 0), -merid * near, inner)
    on_second = jnp.where(high & (row == 1), -merid * first, outer)
    on_own = -jnp.where(high & (row == 0), -merid * near, outer)
    return on_first, on_second, on_own, on_v


def sweep(level_ref, sound_ref, inv_ref, w_ref, star, w_out, p_out, finish):
    levels = sound_ref.shape[0]
    here = star(0)
    value = None
    for k in range(levels):
        alpha = level_ref[k:k + 1]
        p_out[k] = here
        if k + 1 < levels:
            upper = star(k + 1)
            rhs = w_ref[k] - alpha * (upper - here)
            here = upper
        else:
            rhs = w_ref[k] + alpha * here
        inv = inv_ref[k]
        scaled = rhs * inv
        value = scaled if value is None else scaled + (alpha * sound_ref[k] * inv) * value
        w_out[k] = value
    upper = w_out[levels - 1]
    for k in range(levels - 1, -1, -1):
        lower = None
        if k:
            lower = w_out[k - 1] + (level_ref[k - 1:k] * sound_ref[k] * inv_ref[k - 1]) * upper
            w_out[k - 1] = lower
        fresh = p_out[k] - sound_ref[k] * (upper if lower is None else upper - lower)
        p_out[k] = fresh
        finish(k, fresh)
        upper = lower


def column_first_kernel(nz, level_ref, own_ref, sound_ref, inv_ref, base_ref, div_ref, p_ref, w_ref, *refs):
    levels, band, width = sound_ref.shape
    per = width // LANES
    if nz:
        edge_ref, w_out, p_out, sum_out, rows_out = refs
        depth = levels // sum_out.shape[0]
        weights = border_weights(own_ref, edge_ref[0, 3:4], nz, (band, width), True)
        odd = lax.axis_index("lat") % 2 == 1
    else:
        w_out, p_out = refs

    def star(k):
        div = base_ref[k] + div_ref[k]
        if nz:
            div += weights[0] * edge_ref[k, 0:1] + weights[1] * edge_ref[k, 1:2]
            div += weights[2] * p_ref[k] + weights[3] * edge_ref[k, 2:3]
        return p_ref[k] - sound_ref[k] * div

    def finish(k, fresh):
        if nz:
            total = p_ref[k] + fresh
            rows_out[k] = jnp.where(odd, total[band - 2:], total[:2])
            for h in range(per):
                at = (k % depth * per + h) * band
                sum_out[k // depth, at:at + band] = total[:, h * LANES:(h + 1) * LANES]

    sweep(level_ref, sound_ref, inv_ref, w_ref, star, w_out, p_out, finish)


def column_last_kernel(nz, level_ref, own_ref, sound_ref, inv_ref, field_ref, p_ref, w_ref, u_ref, v_ref, *refs):
    levels, band, width = sound_ref.shape
    per = width // LANES
    zonal = jnp.broadcast_to(own_ref[:, 0:1], (band, width))
    merid = jnp.broadcast_to(own_ref[:, 1:2], (band, width))
    if nz:
        edge_ref, facing_ref, rows_ref, refs = refs[0], refs[1], refs[2], refs[3:]
        depth = levels // field_ref.shape[0]
        near = edge_ref[0, 3:4]
        weights = border_weights(own_ref, near, nz, (band, width), False)
        odd = lax.axis_index("lat") % 2 == 1
        row = lax.broadcasted_iota(jnp.int32, (band, width), 0)
        lane = lax.broadcasted_iota(jnp.int32, (band, width), 1)
    else:
        base_ref, refs = refs[0], refs[1:]
    u_out, v_out, w_out, p_out = refs[4:8]
    sems = refs[8]
    leaving = []
    size = levels // 4

    def leave(out, start):
        part = pl.ds(start, size)
        move = pltpu.make_async_copy(refs[4 + out].at[part], refs[out].at[part], sems.at[len(leaving)])
        move.start()
        leaving.append(move)

    def wide(k, field):
        at = (field * depth + k % depth) * per * band
        return jnp.concatenate([field_ref[k // depth, at + h * band:at + (h + 1) * band] for h in range(per)], axis=1)

    def star(k):
        result = new_star(k)
        if (k + 1) % size == 0:
            leave(0, k + 1 - size)
            leave(1, k + 1 - size)
        return result

    def finish(k, fresh):
        if k % size == 0:
            leave(2, k)
            leave(3, k)

    def new_star(k):
        if not nz:
            u_out[k] = u_ref[k] - zonal * field_ref[k, band:2 * band]
            v_out[k] = v_ref[k] - merid * field_ref[k, 2 * band:]
            return p_ref[k] - sound_ref[k] * (base_ref[k] + field_ref[k, :band])
        u = u_ref[k] - zonal * wide(k, 0)
        v = v_ref[k] - merid * wide(k, 1)
        far, mine = facing_ref[k], rows_ref[k]
        v -= weights[0] * far[0:1] + weights[1] * far[1:2]
        u_out[k], v_out[k] = u, v
        b, c, at = k // depth, k % depth, 2 * depth * per * band
        sides = jnp.concatenate([unfold(field_ref[b, at + 4:at + 8], c)] * per, axis=1)
        at += c * per
        pair = jnp.concatenate([field_ref[b, at + h:at + h + 1] for h in range(per)], axis=1)
        half = edge_ref[k, 2:3] - near * jnp.where(odd, far[1:2] - mine[1:2], mine[0:1] - far[0:1])
        north, south = jnp.where(odd, half, pair), jnp.where(odd, pair, half)
        east = jnp.where(lane == width - 1, sides, pltpu.roll(u, width - 1, 1))
        west = jnp.where(lane == 0, sides, pltpu.roll(u, 1, 1))
        up = jnp.where(row == band - 1, north, pltpu.roll(v, band - 1, 0))
        down = jnp.where(row == 0, south, pltpu.roll(v, 1, 0))
        return p_ref[k] - sound_ref[k] * (zonal * (east - west) + merid * (up - down))

    sweep(level_ref, sound_ref, inv_ref, w_ref, star, w_out, p_out, finish)
    for move in leaving:
        move.wait()


def column(first, nz, depth, level_coef, own, sound, *operands):
    levels, band, width = sound.shape
    shapes = [jax.ShapeDtypeStruct(sound.shape, F32)] * (2 if first else 4)
    if first and nz:
        shapes.append(jax.ShapeDtypeStruct((levels // depth, depth * (width // LANES) * band, LANES), F32))
        shapes.append(jax.ShapeDtypeStruct((levels, 2, width), F32))
    extra = {}
    if not first:
        extra["scratch_shapes"] = [pltpu.VMEM(sound.shape, F32)] * 4 + [pltpu.SemaphoreType.DMA((16,))]
    return pl.pallas_call(
        functools.partial(column_first_kernel if first else column_last_kernel, nz),
        in_specs=[pl.BlockSpec(memory_space=pltpu.VMEM)] * (3 + len(operands)),
        out_specs=[pl.BlockSpec(memory_space=pltpu.VMEM if first else pltpu.HBM)] * len(shapes),
        out_shape=shapes,
        compiler_params=KERNEL,
        cost_estimate=pl.CostEstimate(flops=20 * sound.size, bytes_accessed=40 * sound.size, transcendentals=0),
        name="column_first" if first else "column_last",
        **extra,
    )(level_coef, own, sound, *operands)


def shifted(block, axis, step):
    count = lax.axis_size(axis)
    return lax.ppermute(block, axis, [(i, (i + step) % count) for i in range(count)])


def exchange(block, halves):
    axes, members = "lon", None
    if halves:
        axes = ("lat", "lon")
        count = lax.axis_size(axes)
        members = np.arange(count).reshape(2, count // 2).tolist()
    return lax.all_to_all(block, axes, split_axis=0, concat_axis=0, axis_index_groups=members, tiled=True)


def swapped(block, first):
    count = lax.axis_size("lat")
    pairs = [(i, i + 1) for i in range(first, count - 1, 2)]
    return lax.ppermute(block, "lat", pairs + [(b, a) for a, b in pairs])


def lat_edges(last, first):
    count = lax.axis_size("lat")
    low = lax.ppermute(last, "lat", [(i, i + 1) for i in range(count - 1)])
    high = lax.ppermute(first, "lat", [(i + 1, i) for i in range(count - 1)])
    return low, high


def program(
    zonal_wind,
    merid_wind,
    vertical_wind,
    pressure,
    zonal_coef,
    merid_coef,
    level_coef,
    sound_coef,
    cutoff,
    filter_mask,
):
    levels, band, width = pressure.shape
    nz, nl = lax.axis_size("lat"), lax.axis_size("lon")
    length = width * nl
    lats = band * nz
    me = lax.axis_index("lat")
    weights, table = tables(length)
    level_rows = jnp.broadcast_to(level_coef[:, None], (levels, width))
    own = jnp.stack([zonal_coef, merid_coef], axis=1)
    limit = jnp.where(filter_mask > 0, cutoff, length).astype(F32)
    per = width // LANES

    depth = levels // (2 * nl)
    if nz == 4 and band == 8 and 1 <= depth <= 2 and depth * per <= 4 and levels == 2 * nl * depth:
        plan = Plan(True, 2, nl, depth, per, band, 0, band)
        blocked = [a.reshape(levels // depth, depth, band, width) for a in (pressure, zonal_wind, merid_wind)]
        sent, rows = pack(zonal_coef, merid_coef, *blocked)
        circles = exchange(sent, True)
        edges = swapped(rows, 1)
        limits = lax.dynamic_slice_in_dim(limit, me // 2 * 2 * band, 2 * band)
        limits = jnp.tile(limits, depth)[:, None]
        inv, base = factor(level_rows, sound_coef, zonal_wind, merid_wind, own)
        div = transform(plan, False, limits, weights, table, circles)
        div = exchange(div, True).reshape(levels, band, width)
        w, p, total, rows = column(True, nz, depth, level_rows, own, sound_coef, inv, base, div, pressure, vertical_wind, edges)
        facing = swapped(rows, 1)
        fields = transform(plan, True, limits, weights, table, exchange(total, True), circles)
        fields = exchange(fields, True)
        return column(False, nz, depth, level_rows, own, sound_coef, inv, fields, p, w, zonal_wind, merid_wind, edges, facing, rows)

    depth, halo = levels // nl, 2
    tall = -(-(band + 2 * halo) // 8) * 8
    plan = Plan(False, 1, nl, depth, per, tall, halo, band)

    def spread(field):
        low, high = lat_edges(field[:, -halo:], field[:, :halo])
        field = jnp.concatenate([low, field, high], axis=1)
        field = jnp.pad(field, ((0, 0), (0, tall - band - 2 * halo), (0, 0)))
        field = field.reshape(levels, tall, per, LANES).swapaxes(1, 2)
        return exchange(field.reshape(nl, depth * per * tall, LANES), False)

    circles = spread(pressure)
    low, high = lat_edges(own[-halo:], own[:halo])
    v_low, v_high = lat_edges(merid_wind[:, -1:], merid_wind[:, :1])
    row = jnp.arange(lats + 2 * halo) - halo
    limit = jnp.pad(limit, (halo, halo), constant_values=1.0)
    known = jnp.stack([limit, (row < lats - 1).astype(F32), (row > 0).astype(F32)], axis=1)
    known = lax.dynamic_slice_in_dim(known, me * band, band + 2 * halo, 0)
    coefs = jnp.concatenate([known, jnp.concatenate([low, own, high])], axis=1)
    coefs = jnp.tile(jnp.pad(coefs, ((0, tall - band - 2 * halo), (0, 0))), (depth, 1))

    u_low = shifted(zonal_wind[:, :, -1:], "lon", 1)
    u_high = shifted(zonal_wind[:, :, :1], "lon", -1)
    u_diff = jnp.concatenate([zonal_wind[:, :, 1:], u_high], 2) - jnp.concatenate([u_low, zonal_wind[:, :, :-1]], 2)
    v_diff = jnp.concatenate([merid_wind[:, 1:], v_high], 1) - jnp.concatenate([v_low, merid_wind[:, :-1]], 1)
    base = zonal_coef[None, :, None] * u_diff + merid_coef[None, :, None] * v_diff

    (inv,) = factor(level_rows, sound_coef)
    div = transform(plan, False, coefs, weights, table, circles)
    div = exchange(div, False).reshape(levels, band, width)
    w, p = column(True, 0, depth, level_rows, own, sound_coef, inv, base, div, pressure, vertical_wind)
    fields = transform(plan, True, coefs, weights, table, spread(pressure + p))
    fields = exchange(fields, False).reshape(levels, 3 * band, width)
    return column(False, 0, depth, level_rows, own, sound_coef, inv, fields, p, w, zonal_wind, merid_wind, base)


def solution(mesh):
    spec = P(None, "lat", "lon")
    in_specs = (spec, spec, spec, spec, P("lat"), P("lat"), P(), spec, P(), P())
    return jax.shard_map(program, mesh=mesh, in_specs=in_specs, out_specs=(spec,) * 4, check_vma=False)
```

time: 66.9 us -> 63.8 us (0.954)
  Pallas kernels: 10.9 us -> 8.51 us
  waiting for transfers between devices: 24.2 us -> 22.5 us
  local copies, waits for them, and re-layouts: 2.86 us -> 3.9 us
    all_to_all x3, waiting for transfers between devices: 24.2 us -> 22.5 us  [exchange(): lax.all_to_all(block, axes, split_axis=0, concat_axis=0, axis_index_group...]
    pallas_call x2, Pallas kernels: 4.34 us -> 3.12 us  [the longest x1 2.79 us: pack(): pl.pallas_call(pack_kernel, in_specs=[hbm] * 5, out_specs=[hbm, hbm], out...]
    unnamed x30, local copies, waits for them, and re-layouts: 2.62 us -> 3.59 us
    pallas_call x2, Pallas kernels: 2.8 us -> 1.84 us  [column(): pl.pallas_call(functools.partial(column_first_kernel if first else column...]
  transfers between devices with their start and end apart: 5 -> 5, of which waited for: 3 -> 3; matrix products, arithmetic and copies ran while one was open for 0% -> 1% of each run, Pallas kernels for 1% -> 1%
where the time goes in v4:
time: 63.8 us; the launch traced here: 63.2 us
  waiting for transfers between devices  22.5 us (35%)
  starting transfers between devices  15.1 us (24%)
  blocking collectives  12.3 us (19%)
  Pallas kernels  8.51 us (13%)
  local copies, waits for them, and re-layouts  3.9 us (6%)
  between operations  0.85 us (1%)
    all_to_all x3, waiting for transfers between devices, exchange(): lax.all_to_all(block, axes, split_axis=0, concat_axis=0, axis_index_group...  22.5 us
    all_to_all x3, starting transfers between devices, exchange(): lax.all_to_all(block, axes, split_axis=0, concat_axis=0, axis_index_group...  13.7 us
    all_to_all x1, blocking collectives, exchange(): lax.all_to_all(block, axes, split_axis=0, concat_axis=0, axis_index_group...  12.3 us
    unnamed x30, local copies, waits for them, and re-layouts  3.59 us
    pallas_call x2, Pallas kernels, transform(): pl.pallas_call(functools.partial(transform_kernel, plan, full), out_specs...  3.55 us
    pallas_call x1, Pallas kernels, pack(): pl.pallas_call(pack_kernel, in_specs=[hbm] * 5, out_specs=[hbm, hbm], out...  2.79 us
    pallas_call x2, Pallas kernels, column(): pl.pallas_call(functools.partial(column_first_kernel if first else column...  1.84 us
    ppermute x2, starting transfers between devices, swapped(): return lax.ppermute(block, 'lat', pairs + [(b, a) for a, b in pairs])  1.33 us
  transfers between devices with their start and end apart: 5, of which 3 were waited for; matrix products, arithmetic and copies ran while one was open for 1% of the time, Pallas kernels for 1%

profile of v4, /device:TPU:0, one launch (start us, length us, event | category | flops | bytes accessed | tf_op | source)
XLA Modules:
  0.0 63.2 jit_solution(15012926239932715110)
XLA Ops:
  0.6 2.8 %pack_circles.1 = (f32[16,40,128]{2,1,0:T(8,128)}, f32[32,4,256]{2,1,0:T(4,128)}) custom-call(f32[8]{0:T(128)} %zonal_ref.1, f32[8]{0:T(128)} %merid_ref.1, f32[16,2,8,256]{3,2,1,0:T(8,128)} %bitcast.8, f32[16,2,8,256]{3,2,1,0:T(8,128)} %bitcast.6, f32[16,2,8,256]{3,2,1,0:T(8,128)} %bitcast.7), custom_call_target="tpu_custom_call" | custom-call | flops 65536 | bytes 1048576 | tf_op jit(solution)/shard_map/pack_circles/pallas_call | solution.py:417
  3.4 0.0 copy-start.3
  3.4 6.5 %all-to-all-start = ((f32[16,40,128]{2,1,0:T(8,128)}), f32[16,40,128]{2,1,0:T(8,128)S(1)}, u32[]{:S(2)}, u32[]{:S(2)}) async-start(f32[16,40,128]{2,1,0:T(8,128)} %get-tuple-element.14), calls=%async_computation | async-start | bytes 655360 | tf_op jit(solution)/shard_map/all_to_all | solution.py:658
  9.9 0.0 copy-start.8
  9.9 0.0 copy-start.13
  9.9 0.0 copy-start.14
  10.0 0.6 copy-done.13
  10.6 0.0 copy-done.14
  10.6 0.1 dynamic_slice.3
  10.7 0.1 broadcast_in_dim_tile.4.refs_0_.refs_1_
  10.8 7.5 %all-to-all-done.x_ref.refs_0_ = f32[16,40,128]{2,1,0:T(8,128)S(1)} async-done(((f32[16,40,128]{2,1,0:T(8,128)}), f32[16,40,128]{2,1,0:T(8,128)S(1)}, u32[]{:S(2)}, u32[]{:S(2)}) %all-to-all-start) | async-done | bytes 327712 | tf_op jit(solution)/shard_map/all_to_all | solution.py:658
  18.3 0.0 copy-done.3
  18.3 0.0 copy-done.8
  18.3 0.0 copy-start.12
  18.3 0.0 copy-start.2
  18.3 1.7 %transform_div.1 = f32[16,16,256]{2,1,0:T(8,128)} custom-call(f32[16,40,128]{2,1,0:T(8,128)S(1)} %all-to-all-done.x_ref.refs_0_, f32[32,1]{1,0:T(8,128)S(1)} %broadcast_in_dim_tile.4.refs_0_.refs_1_, bf16[2,2,256,256]{3,2,1,0:T(8,128)(2,1)S(1)} %copy-done.3, f32[5,9,128]{2,1,0:T(8,128)S(1)} %copy-done.8), custom_call_target="tpu_custom_call" | custom-call | flops 226492416 | bytes 2097152 | tf_op jit(solution)/shard_map/transform_div/pallas_call | solution.py:331
  20.0 0.0 copy-start
  20.0 0.0 copy-start.1
  20.0 3.7 %all-to-all-start.1 = ((f32[16,16,256]{2,1,0:T(8,128)}), f32[16,16,256]{2,1,0:T(8,128)S(1)}, u32[]{:S(2)}, u32[]{:S(2)}) async-start(f32[16,16,256]{2,1,0:T(8,128)} %transform_div.1), calls=%async_computation.1 | async-start | bytes 524288 | tf_op jit(solution)/shard_map/all_to_all | solution.py:658
  23.7 0.0 copy-done.12
  23.7 0.7 %collective-permute-start = (f32[32,4,256]{2,1,0:T(4,128)S(1)}, f32[32,4,256]{2,1,0:T(4,128)S(1)}, u32[]{:S(2)}, u32[]{:S(2)}) collective-permute-start(f32[32,4,256]{2,1,0:T(4,128)S(1)} %copy-done.12), channel_id=1, source_target_pairs={{8,16},{16,8},{9,17},{17,9},{10,18},{18,10},{11,19},{19,11},{12,20... | collective-permute-start | bytes 393224 | tf_op jit(solution)/shard_map/ppermute | solution.py:664
  24.4 0.0 copy-start.9
  24.4 0.0 copy-start.10
  24.4 0.6 %copy-done.9 = f32[8]{0:T(128)S(1)} copy-done((f32[8]{0:T(128)S(1)}, f32[8]{0:T(128)}, u32[]{:S(2)}) %copy-start.9) | copy-done | bytes 56
  25.1 0.0 copy-done.10
  25.1 0.0 copy-start.11
  25.1 0.1 copy.24.refs_2_.own_ref
  25.2 0.6 copy-done.11
  25.8 0.1 broadcast_in_dim.10.level_ref
  25.8 0.0 copy-done.2
  25.8 0.0 copy-done
  25.8 0.0 copy-done.1
  25.8 0.0 copy-start.4
  25.9 0.0 copy-start.5
  25.9 0.3 factor_columns.1
  26.2 0.0 copy-start.6
  26.2 0.7 %copy-done.6 = f32[32,8,256]{2,1,0:T(8,128)} copy-done((f32[32,8,256]{2,1,0:T(8,128)}, f32[32,8,256]{2,1,0:T(8,128)S(1)}, u32[]{:S(2)}) %copy-start.6) | copy-done | bytes 262168
  26.9 0.0 collective-permute-done.refs_0_
  26.9 4.5 %all-to-all-done.1 = f32[16,16,256]{2,1,0:T(8,128)S(1)} async-done(((f32[16,16,256]{2,1,0:T(8,128)}), f32[16,16,256]{2,1,0:T(8,128)S(1)}, u32[]{:S(2)}, u32[]{:S(2)}) %all-to-all-start.1) | async-done | bytes 262176 | tf_op jit(solution)/shard_map/all_to_all | solution.py:658
  31.4 0.0 copy-done.4
  31.4 0.0 copy-done.5
  31.4 0.0 copy-start.7
  31.4 0.9 %copy-done.7 = f32[32,8,256]{2,1,0:T(8,128)S(1)} copy-done((f32[32,8,256]{2,1,0:T(8,128)S(1)}, f32[32,8,256]{2,1,0:T(8,128)}, u32[]{:S(2)}) %copy-start.7) | copy-done | bytes 262168
  32.4 0.4 column_first.1
  32.8 12.3 %all_to_all.20.x_ref = f32[16,32,128]{2,1,0:T(8,128)S(1)} all-to-all(f32[16,32,128]{2,1,0:T(8,128)S(1)} %get-tuple-element.16), channel_id=1, replica_groups={{0,1,2,3,4,5,6,7,8,9,10,11,12,13,14,15},{16,17,18,19,20,21,22,23,24,25,..., dimensions={0} | all-to-all | bytes 524288 | tf_op jit(solution)/shard_map/all_to_all | solution.py:658
  45.1 1.9 %transform_all.1 = f32[16,72,128]{2,1,0:T(8,128)} custom-call(f32[16,32,128]{2,1,0:T(8,128)S(1)} %all_to_all.20.x_ref, f32[16,40,128]{2,1,0:T(8,128)S(1)} %all-to-all-done.x_ref.refs_0_, f32[32,1]{1,0:T(8,128)S(1)} %broadcast_in_dim_tile.4.refs_0_.refs_1_, bf16[2,2,256,256]{3,2,1,0:T(8,128)(2,1)S(1)} %copy-done.3, f32[5,9,128]{2,1,0:T(8,128)S(1)} %copy-done.8), custom_call_target="tpu_custom_call" | custom-call | flops 452984832 | bytes 2097152 | tf_op jit(solution)/shard_map/transform_all/pallas_call | solution.py:331
  47.0 3.6 %all-to-all-start.3 = ((f32[16,72,128]{2,1,0:T(8,128)}), f32[16,72,128]{2,1,0:T(8,128)S(1)}, u32[]{:S(2)}, u32[]{:S(2)}) async-start(f32[16,72,128]{2,1,0:T(8,128)} %transform_all.1), calls=%async_computation.3 | async-start | bytes 1179648 | tf_op jit(solution)/shard_map/all_to_all | solution.py:658
  50.6 0.7 %collective-permute-start.1 = (f32[32,2,256]{2,1,0:T(2,128)S(1)}, f32[32,2,256]{2,1,0:T(2,128)S(1)}, u32[]{:S(2)}, u32[]{:S(2)}) collective-permute-start(f32[32,2,256]{2,1,0:T(2,128)S(1)} %get-tuple-element.19.refs_2_), channel_id=1, source_target_pairs={{8,16},{16,8},{9,17},{17,9},{10,18},{18,10},{11,19},{19,11},{12,20... | collective-permute-start | bytes 196616 | tf_op jit(solution)/shard_map/ppermute | solution.py:664
  51.3 0.0 collective-permute-done.1.refs_1_
  51.3 10.5 %all-to-all-done.3.field_ref = f32[16,72,128]{2,1,0:T(8,128)S(1)} async-done(((f32[16,72,128]{2,1,0:T(8,128)}), f32[16,72,128]{2,1,0:T(8,128)S(1)}, u32[]{:S(2)}, u32[]{:S(2)}) %all-to-all-start.3) | async-done | bytes 589856 | tf_op jit(solution)/shard_map/all_to_all | solution.py:658
  61.8 1.4 %column_last.1 = (f32[32,8,256]{2,1,0:T(8,128)}, f32[32,8,256]{2,1,0:T(8,128)}, f32[32,8,256]{2,1,0:T(8,128)}, f32[32,8,256]{2,1,0:T(8,128)}) custom-call(f32[32,256]{1,0:T(8,128)S(1)} %broadcast_in_dim.10.level_ref, f32[8,2]{1,0:T(8,128)S(1)} %copy.24.refs_2_.own_ref, f32[32,8,256]{2,1,0:T(8,128)S(1)} %copy-done.2, ...), custom_call_target="tpu_custom_call" | custom-call | flops 1310720 | bytes 2621440 | tf_op jit(solution)/shard_map/column_last/pallas_call | solution.py:635
  (3 shorter events, 0.0 us)
Async XLA Ops:
  3.4 14.9 %copy-start.3 = (bf16[2,2,256,256]{3,2,1,0:T(8,128)(2,1)S(1)}, bf16[2,2,256,256]{3,2,1,0:T(8,128)(2,1)}, u32[]{:S(2)}) copy-start(bf16[2,2,256,256]{3,2,1,0:T(8,128)(2,1)} %constant.32.clone.refs_1_.refs_2_) | copy-start | bytes 1572868
  3.4 14.9 %all-to-all-start = ((f32[16,40,128]{2,1,0:T(8,128)}), f32[16,40,128]{2,1,0:T(8,128)S(1)}, u32[]{:S(2)}, u32[]{:S(2)}) async-start(f32[16,40,128]{2,1,0:T(8,128)} %get-tuple-element.14), calls=%async_computation | async-start | bytes 655360 | tf_op jit(solution)/shard_map/all_to_all | solution.py:658
  9.9 8.4 %copy-start.8 = (f32[5,9,128]{2,1,0:T(8,128)S(1)}, f32[5,9,128]{2,1,0:T(8,128)}, u32[]{:S(2)}) copy-start(f32[5,9,128]{2,1,0:T(8,128)} %constant.33.clone.refs_2_.refs_3_) | copy-start | bytes 69124
  9.9 0.7 %copy-start.13 = (s32[32]{0:T(128)S(1)}, s32[32]{0:T(128)}, u32[]{:S(2)}) copy-start(s32[32]{0:T(128)} %param.20) | copy-start | bytes 388
  9.9 0.7 %copy-start.14 = (s32[32]{0:T(128)S(1)}, s32[32]{0:T(128)}, u32[]{:S(2)}) copy-start(s32[32]{0:T(128)} %param.21) | copy-start | bytes 388
  18.3 5.4 %copy-start.12 = (f32[32,4,256]{2,1,0:T(4,128)S(1)}, f32[32,4,256]{2,1,0:T(4,128)}, u32[]{:S(2)}) copy-start(f32[32,4,256]{2,1,0:T(4,128)} %get-tuple-element.15) | copy-start | bytes 393220
  18.3 7.5 %copy-start.2 = (f32[32,8,256]{2,1,0:T(8,128)S(1)}, f32[32,8,256]{2,1,0:T(8,128)}, u32[]{:S(2)}) copy-start(f32[32,8,256]{2,1,0:T(8,128)} %sound_ref.5) | copy-start | bytes 786436
  20.0 5.8 %copy-start = (f32[32,8,256]{2,1,0:T(8,128)S(1)}, f32[32,8,256]{2,1,0:T(8,128)}, u32[]{:S(2)}) copy-start(f32[32,8,256]{2,1,0:T(8,128)} %u_ref.1) | copy-start | bytes 786436
  20.0 5.8 %copy-start.1 = (f32[32,8,256]{2,1,0:T(8,128)S(1)}, f32[32,8,256]{2,1,0:T(8,128)}, u32[]{:S(2)}) copy-start(f32[32,8,256]{2,1,0:T(8,128)} %v_ref.1) | copy-start | bytes 786436
  20.0 11.4 %all-to-all-start.1 = ((f32[16,16,256]{2,1,0:T(8,128)}), f32[16,16,256]{2,1,0:T(8,128)S(1)}, u32[]{:S(2)}, u32[]{:S(2)}) async-start(f32[16,16,256]{2,1,0:T(8,128)} %transform_div.1), calls=%async_computation.1 | async-start | bytes 524288 | tf_op jit(solution)/shard_map/all_to_all | solution.py:658
  23.7 3.2 %collective-permute-start = (f32[32,4,256]{2,1,0:T(4,128)S(1)}, f32[32,4,256]{2,1,0:T(4,128)S(1)}, u32[]{:S(2)}, u32[]{:S(2)}) collective-permute-start(f32[32,4,256]{2,1,0:T(4,128)S(1)} %copy-done.12), channel_id=1, source_target_pairs={{8,16},{16,8},{9,17},{17,9},{10,18},{18,10},{11,19},{19,11},{12,20... | collective-permute-start | bytes 393224 | tf_op jit(solution)/shard_map/ppermute | solution.py:664
  24.4 0.7 %copy-start.9 = (f32[8]{0:T(128)S(1)}, f32[8]{0:T(128)}, u32[]{:S(2)}) copy-start(f32[8]{0:T(128)} %merid_ref.1) | copy-start | bytes 100
  24.4 0.7 %copy-start.10 = (f32[8]{0:T(128)S(1)}, f32[8]{0:T(128)}, u32[]{:S(2)}) copy-start(f32[8]{0:T(128)} %zonal_ref.1) | copy-start | bytes 100
  25.1 0.7 %copy-start.11 = (f32[32]{0:T(128)S(1)}, f32[32]{0:T(128)}, u32[]{:S(2)}) copy-start(f32[32]{0:T(128)} %param.18) | copy-start | bytes 388
  25.8 5.6 %copy-start.4 = (f32[32,8,256]{2,1,0:T(8,128)S(1)}, f32[32,8,256]{2,1,0:T(8,128)}, u32[]{:S(2)}) copy-start(f32[32,8,256]{2,1,0:T(8,128)} %p_ref.1) | copy-start | bytes 786436
  25.9 5.6 %copy-start.5 = (f32[32,8,256]{2,1,0:T(8,128)S(1)}, f32[32,8,256]{2,1,0:T(8,128)}, u32[]{:S(2)}) copy-start(f32[32,8,256]{2,1,0:T(8,128)} %w_ref.1) | copy-start | bytes 786436
  26.2 0.7 %copy-start.6 = (f32[32,8,256]{2,1,0:T(8,128)}, f32[32,8,256]{2,1,0:T(8,128)S(1)}, u32[]{:S(2)}) copy-start(f32[32,8,256]{2,1,0:T(8,128)S(1)} %get-tuple-element.13.base_ref) | copy-start | bytes 786436
  31.4 1.0 %copy-start.7 = (f32[32,8,256]{2,1,0:T(8,128)S(1)}, f32[32,8,256]{2,1,0:T(8,128)}, u32[]{:S(2)}) copy-start(f32[32,8,256]{2,1,0:T(8,128)} %copy-done.6) | copy-start | bytes 786436
  47.0 14.8 %all-to-all-start.3 = ((f32[16,72,128]{2,1,0:T(8,128)}), f32[16,72,128]{2,1,0:T(8,128)S(1)}, u32[]{:S(2)}, u32[]{:S(2)}) async-start(f32[16,72,128]{2,1,0:T(8,128)} %transform_all.1), calls=%async_computation.3 | async-start | bytes 1179648 | tf_op jit(solution)/shard_map/all_to_all | solution.py:658
  50.6 0.7 %collective-permute-start.1 = (f32[32,2,256]{2,1,0:T(2,128)S(1)}, f32[32,2,256]{2,1,0:T(2,128)S(1)}, u32[]{:S(2)}, u32[]{:S(2)}) collective-permute-start(f32[32,2,256]{2,1,0:T(2,128)S(1)} %get-tuple-element.19.refs_2_), channel_id=1, source_target_pairs={{8,16},{16,8},{9,17},{17,9},{10,18},{18,10},{11,19},{19,11},{12,20... | collective-permute-start | bytes 196616 | tf_op jit(solution)/shard_map/ppermute | solution.py:664

commit v5 on v4

--- a/solution.py
+++ b/solution.py
@@ -15,7 +15,6 @@
 F32 = jnp.float32
 BF16 = jnp.bfloat16
 KERNEL = pltpu.CompilerParams(vmem_limit_bytes=8 << 20)
-ALONE = pltpu.CompilerParams(vmem_limit_bytes=60 << 20)
 
 
 class Plan(NamedTuple):
@@ -138,9 +137,8 @@
 
 
 def transform_kernel(plan, full, x_ref, *refs):
-    extra_ref = x_ref
-    if plan.packed and full:
-        extra_ref, refs = refs[0], refs[1:]
+    if plan.packed:
+        own_ref, near_ref, refs = refs[0], refs[1], refs[2:]
     coef_ref, weight_ref, table_ref, result_ref, lhs_ref, spec_ref, work_ref, out_ref, sems = refs
     bands, nl, depth, per = plan.bands, plan.nl, plan.depth, plan.per
     tall, skip, band = plan.tall, plan.skip, plan.band
@@ -149,14 +147,9 @@
     groups = pieces // 2 + 1
     rows = stacks * tall
     length = pieces * LANES
-    spot = depth * per * tall
 
     def tile(c, z, l, h):
-        at = (c * per + h) * tall
-        return x_ref[z * nl + l, at:at + tall]
-
-    def edge_tile(c, z, l):
-        return unfold(extra_ref[z * nl + l % nl, spot + 4:spot + 8], c)
+        return x_ref[z * nl + l, c * tall:(c + 1) * tall, h * LANES:(h + 1) * LANES]
 
     def product(which, start):
         high, low = (lhs_ref[i, start:start + groups * rows] for i in range(2))
@@ -190,13 +183,15 @@
         return jnp.broadcast_to(a, (a.shape[0], LANES))
 
     if plan.packed:
-        limit = column(coef_ref[...])
+        limit = coef_ref[...]
         place = lax.broadcasted_iota(jnp.int32, (rows, LANES), 0) % (bands * tall)
         has_up = jnp.where(place < bands * tall - 1, 1.0, 0.0)
         has_down = jnp.where(place > 0, 1.0, 0.0)
-        pair = [edge_tile(0, z, 0) for z in range(bands)]
-        zonal = jnp.concatenate([column(t[:, 1:2]) for t in pair] * depth, axis=0)
-        merid = jnp.concatenate([column(t[:, 2:3]) for t in pair] * depth, axis=0)
+        odd = lax.axis_index("lat") % 2 == 1
+        own_rows, near_rows = own_ref[...], near_ref[-tall:, :LANES]
+        pair = [jnp.where(odd, near_rows, own_rows), jnp.where(odd, own_rows, near_rows)]
+        zonal = jnp.concatenate([column(t[:, 0:1]) for t in pair] * depth, axis=0)
+        merid = jnp.concatenate([column(t[:, 1:2]) for t in pair] * depth, axis=0)
     else:
         limit, has_up, has_down, zonal, merid = (column(coef_ref[:, i:i + 1]) for i in range(5))
     zonal2, merid_up, merid_down = zonal * zonal, merid * has_up, merid * has_down
@@ -258,22 +253,12 @@
         results.append(result)
         for c, z, l in cells:
             own = latitudes(c, z)
-            if plan.packed and not full:
-                side = band - 1 if z % 2 == 0 else 0
-                v_weight = jnp.where(row == side, merid[own] if z % 2 == 0 else -merid[own], 0.0)
-                at = spot + c * per
             for h in range(per):
                 value = result[l * per + h][own]
                 if plan.packed and full:
                     start = ((field * depth + c) * per + h) * band
                     out_ref[z * nl + l, start:start + band] = value
                     continue
-                if plan.packed:
-                    value += v_weight * extra_ref[(z ^ 1) * nl + l, at + h:at + h + 1]
-                    if h == 0:
-                        value += jnp.where(lane == 0, -zonal[own], 0.0) * edge_tile(c, z, l - 1)
-                    if h == per - 1:
-                        value += jnp.where(lane == LANES - 1, zonal[own], 0.0) * edge_tile(c, z, l + 1)
                 start = (c * len(plan.fields(full)) + field) * band
                 out_ref[z * nl + l, start:start + band, h * LANES:(h + 1) * LANES] = value
         if plan.packed and full:
@@ -288,8 +273,8 @@
                     own = latitudes(c, z)
                     before = u[(l * per - 1) % pieces][own]
                     after = u[(l * per + per) % pieces][own]
-                    before = edge_tile(c, z, l - 1) - zonal[own] * pltpu.roll(before, 1, 1)
-                    after = edge_tile(c, z, l + 1) - zonal[own] * pltpu.roll(after, LANES - 1, 1)
+                    before = -zonal[own] * pltpu.roll(before, 1, 1)
+                    after = -zonal[own] * pltpu.roll(after, LANES - 1, 1)
                     sides = jnp.where(lane == 0, before, jnp.where(lane == LANES - 1, after, 0.0))
                     edge = sides if c == 0 else edge + pltpu.roll(sides, c * (LANES // 4), 1)
                     other = latitudes(c, z ^ 1)
@@ -297,8 +282,7 @@
                     at = c * per
                     for h in range(per):
                         moved = merid[other:other + 1] * v[l * per + h][other:other + 1]
-                        known = extra_ref[(z ^ 1) * nl + l, spot + at + h:spot + at + h + 1]
-                        out_ref[z * nl + l, base + at + h:base + at + h + 1] = known - moved
+                        out_ref[z * nl + l, base + at + h:base + at + h + 1] = -moved
                 out_ref[z * nl + l, base + 4:base + 8] = fold(edge, row)
                 if depth * per < 4:
                     out_ref[z * nl + l, base + depth * per:base + 4] = jnp.zeros((4 - depth * per, LANES), F32)
@@ -345,100 +329,11 @@
     )(*operands, coefs, weights, table)
 
 
-def pack_kernel(zonal_ref, merid_ref, p_ref, u_ref, v_ref, result_ref, far_ref, zonal_s, merid_s, out_ref, rows_ref, u_buf, v_buf, in_sems, out_sems):
-    blocks, depth, band, width = p_ref.shape
-    per = width // LANES
-    parts = in_sems.shape[0] - 1
-    size = blocks // parts
-    spot = depth * per * band
-
-    def chunk(n):
-        at = pl.ds(n * size, size)
-        moves = [pltpu.make_async_copy(u_ref.at[at], u_buf.at[at], in_sems.at[n, 0]), pltpu.make_async_copy(v_ref.at[at], v_buf.at[at], in_sems.at[n, 1])]
-        for c in range(depth):
-            for h in range(per):
-                source = p_ref.at[at, c, :, pl.ds(h * LANES, LANES)]
-                target = out_ref.at[at, pl.ds((c * per + h) * band, band)]
-                moves.append(pltpu.make_async_copy(source, target, in_sems.at[n, len(moves)]))
-        return moves
-
-    small = [pltpu.make_async_copy(zonal_ref, zonal_s, in_sems.at[parts, 0]), pltpu.make_async_copy(merid_ref, merid_s, in_sems.at[parts, 1])]
-    entering = [chunk(n) for n in range(parts)]
-    for move in small + sum(entering, []):
-        move.start()
-    odd = lax.axis_index("lat") % 2 == 1
-    row = lax.broadcasted_iota(jnp.int32, (band, LANES), 0)
-    lane = lax.broadcasted_iota(jnp.int32, (band, LANES), 1)
-    for move in small:
-        move.wait()
-    coefs = jnp.zeros((band, LANES), F32)
-    for j in range(band):
-        coefs = jnp.where(row == j, jnp.where(lane == 1, zonal_s[j], jnp.where(lane == 2, merid_s[j], 0.0)), coefs)
-    facing = jnp.full((1, width), jnp.where(odd, merid_s[band - 1], merid_s[0]), F32)
-    leaving = []
-    for n in range(parts):
-        for move in entering[n]:
-            move.wait()
-        for b in range(n * size, (n + 1) * size):
-            edge = coefs
-            for c in range(depth):
-                west = pltpu.roll(u_buf[b, c, :, width - LANES:], 1, 1)
-                east = pltpu.roll(u_buf[b, c, :, :LANES], LANES - 1, 1)
-                sides = jnp.where(lane == 0, west, jnp.where(lane == LANES - 1, east, 0.0))
-                edge = edge + (pltpu.roll(sides, c * (LANES // 4), 1) if c else sides)
-                k = b * depth + c
-                for h in range(per):
-                    lanes = slice(h * LANES, (h + 1) * LANES)
-                    at = (c * per + h) * band
-                    top, bottom = v_buf[b, c, :1, lanes], v_buf[b, c, band - 1:, lanes]
-                    out_ref[b, spot + c * per + h:spot + c * per + h + 1] = jnp.where(odd, top, bottom)
-                    rows_ref[k, 2:3, lanes] = jnp.where(odd, bottom, top)
-                    rows_ref[k, :2, lanes] = jnp.where(odd, out_ref[b, at + band - 2:at + band], out_ref[b, at:at + 2])
-                rows_ref[k, 3:4] = facing
-            out_ref[b, spot + 4:spot + 8] = fold(edge, row)
-            if depth * per < 4:
-                out_ref[b, spot + depth * per:spot + 4] = jnp.zeros((4 - depth * per, LANES), F32)
-        at = pl.ds(n * size, size)
-        leaving.append(pltpu.make_async_copy(out_ref.at[at], result_ref.at[at], out_sems.at[n]))
-        leaving[-1].start()
-    leaving.append(pltpu.make_async_copy(rows_ref, far_ref, out_sems.at[parts]))
-    leaving[-1].start()
-    for move in leaving:
-        move.wait()
-
-
-def pack(zonal, merid, p, u, v):
-    blocks, depth, band, width = p.shape
-    per = width // LANES
-    shape = (blocks, (depth * per + 1) * band, LANES)
-    rows = (blocks * depth, 4, width)
-    parts = 4 if blocks % 4 == 0 else 1
-    hbm = pl.BlockSpec(memory_space=pltpu.HBM)
-    return pl.pallas_call(
-        pack_kernel,
-        in_specs=[hbm] * 5,
-        out_specs=[hbm, hbm],
-        out_shape=[jax.ShapeDtypeStruct(shape, F32), jax.ShapeDtypeStruct(rows, F32)],
-        scratch_shapes=[
-            pltpu.SMEM((band,), F32),
-            pltpu.SMEM((band,), F32),
-            pltpu.VMEM(shape, F32),
-            pltpu.VMEM(rows, F32),
-            pltpu.VMEM(p.shape, F32),
-            pltpu.VMEM(p.shape, F32),
-            pltpu.SemaphoreType.DMA((parts + 1, 2 + depth * per)),
-            pltpu.SemaphoreType.DMA((parts + 1,)),
-        ],
-        compiler_params=ALONE,
-        cost_estimate=pl.CostEstimate(flops=p.size, bytes_accessed=16 * p.size, transcendentals=0),
-        name="pack_circles",
-    )(zonal, merid, p, u, v)
-
-
 def factor_kernel(level_ref, sound_ref, *refs):
-    if len(refs) > 1:
+    levels, band, width = sound_ref.shape
+    full = len(refs) > 1
+    if full:
         u_ref, v_ref, own_ref, inv_ref, base_ref = refs
-        band, width = u_ref.shape[1:]
         row = lax.broadcasted_iota(jnp.int32, (band, width), 0)
         lane = lax.broadcasted_iota(jnp.int32, (band, width), 1)
         zonal, merid = own_ref[:, 0:1], own_ref[:, 1:2]
@@ -448,8 +343,7 @@
         south = jnp.where(row > 0, merid, 0.0)
     else:
         (inv_ref,) = refs
-    levels = sound_ref.shape[0]
-    prev = jnp.zeros(sound_ref.shape[1:], F32)
+    prev = jnp.zeros((band, width), F32)
     for k in range(levels):
         alpha = level_ref[k:k + 1]
         below = alpha * sound_ref[k]
@@ -457,23 +351,97 @@
         inv = 1.0 / (1.0 + below + above + below * prev)
         prev = -above * inv
         inv_ref[k] = inv
-        if len(refs) > 1:
+        if full:
             u, v = u_ref[k], v_ref[k]
             div = east * pltpu.roll(u, width - 1, 1) - west * pltpu.roll(u, 1, 1)
             base_ref[k] = div + north * pltpu.roll(v, band - 1, 0) - south * pltpu.roll(v, 1, 0)
 
 
-def factor(level_coef, sound, *winds):
-    shape = jax.ShapeDtypeStruct(sound.shape, F32)
-    count = 1 + len(winds)
+def edges_kernel(depth, bands, zonal_ref, merid_ref, level_ref, cutoff_ref, mask_ref, p_ref, u_ref, v_ref, *refs):
+    pair_ref, half_ref, side_ref, own_ref, rows_ref, limit_ref = refs[:6]
+    smalls, (p_buf, u_buf, v_buf), sems = refs[6:11], refs[11:14], refs[14]
+    levels, band, width = u_buf.shape
+    moves = []
+    for source, target in zip((zonal_ref, merid_ref, level_ref, cutoff_ref, mask_ref, p_ref, u_ref, v_ref), (*smalls, p_buf, u_buf, v_buf)):
+        moves.append(pltpu.make_async_copy(source, target, sems.at[len(moves)]))
+        moves[-1].start()
+    for move in moves[:5]:
+        move.wait()
+    zonal_s, merid_s, level_s, cutoff_s, mask_s = smalls
+    me = lax.axis_index("lat")
+    odd = me % 2 == 1
+    row = lax.broadcasted_iota(jnp.int32, (band, LANES), 0)
+    lane = lax.broadcasted_iota(jnp.int32, (band, LANES), 1)
+    own = jnp.zeros((band, LANES), F32)
+    for j in range(band):
+        own = jnp.where(row == j, jnp.where(lane == 0, zonal_s[j], jnp.where(lane == 1, merid_s[j], 0.0)), own)
+    own_ref[...] = own
+    pair_ref[levels:, :LANES] = own
+    if width > LANES:
+        pair_ref[levels:, LANES:] = jnp.zeros((band, width - LANES), F32)
+    for k in range(levels):
+        rows_ref[k:k + 1] = jnp.full((1, width), level_s[k], F32)
+    start = me // bands * bands * band
+    for z in range(bands):
+        limit = jnp.zeros((band, LANES), F32)
+        for j in range(band):
+            at = start + z * band + j
+            known = jnp.where(mask_s[at] > 0, cutoff_s[at], 1 << 20).astype(F32)
+            limit = jnp.where(row == j, known, limit)
+        for c in range(depth):
+            at = (c * bands + z) * band
+            limit_ref[at:at + band] = limit
+    facing = jnp.full((1, width), jnp.where(odd, merid_s[band - 1], merid_s[0]), F32)
+    for move in moves[5:]:
+        move.wait()
+    sides = jnp.zeros((band, LANES), F32)
+    for k in range(levels):
+        v = v_buf[k]
+        pair_ref[k:k + 1] = jnp.where(odd, v[:1], v[band - 1:])
+        half_ref[k, :2] = jnp.where(odd, p_buf[k, band - 2:], p_buf[k, :2])
+        half_ref[k, 2:3] = jnp.where(odd, v[band - 1:], v[:1])
+        half_ref[k, 3:4] = facing
+        sides = jnp.where(lane == k, pltpu.roll(u_buf[k, :, width - LANES:], (k + 1) % LANES, 1), sides)
+        sides = jnp.where(lane == levels + k, pltpu.roll(u_buf[k, :, :LANES], levels + k, 1), sides)
+    side_ref[...] = sides
+
+
+def edges(depth, bands, zonal, merid, level, cutoff, mask, p, u, v):
+    levels, band, width = p.shape
+    shapes = [(levels + band, width), (levels, 4, width), (band, LANES), (band, LANES), (levels, width), (depth * bands * band, LANES)]
+    hbm = pl.BlockSpec(memory_space=pltpu.HBM)
+    return pl.pallas_call(
+        functools.partial(edges_kernel, depth, bands),
+        in_specs=[hbm] * 8,
+        out_shape=[jax.ShapeDtypeStruct(shape, F32) for shape in shapes],
+        scratch_shapes=[pltpu.SMEM(a.shape, a.dtype) for a in (zonal, merid, level, cutoff, mask)]
+        + [pltpu.VMEM(p.shape, F32)] * 3
+        + [pltpu.SemaphoreType.DMA((8,))],
+        compiler_params=KERNEL,
+        cost_estimate=pl.CostEstimate(flops=4 * p.size, bytes_accessed=16 * p.size, transcendentals=0),
+        name="edges",
+    )(zonal, merid, level, cutoff, mask, p, u, v)
+
+
+def factor(level_rows, sound, *fields):
+    shapes = [sound.shape]
+    if fields:
+        shapes += [sound.shape]
     return pl.pallas_call(
         factor_kernel,
-        in_specs=[pl.BlockSpec(memory_space=pltpu.VMEM)] * (1 + count),
-        out_shape=[shape] * (2 if winds else 1),
+        in_specs=[pl.BlockSpec(memory_space=pltpu.VMEM)] * (2 + len(fields)),
+        out_shape=[jax.ShapeDtypeStruct(shape, F32) for shape in shapes],
         compiler_params=KERNEL,
         cost_estimate=pl.CostEstimate(flops=10 * sound.size, bytes_accessed=16 * sound.size, transcendentals=0),
         name="factor_columns",
-    )(level_coef, sound, *winds)
+    )(level_rows, sound, *fields)
+
+
+def beside(west_ref, east_ref, k, levels):
+    lane = lax.broadcasted_iota(jnp.int32, west_ref.shape, 1)
+    west = pltpu.roll(west_ref[...], (LANES - k) % LANES, 1)
+    east = pltpu.roll(east_ref[...], LANES - 1 - levels - k, 1)
+    return jnp.where(lane == 0, west, jnp.where(lane == LANES - 1, east, 0.0))
 
 
 def border_weights(own_ref, near, nz, shape, first_step):
@@ -529,10 +497,15 @@
     levels, band, width = sound_ref.shape
     per = width // LANES
     if nz:
-        edge_ref, w_out, p_out, sum_out, rows_out = refs
-        depth = levels // sum_out.shape[0]
+        edge_ref, pair_ref, west_ref, east_ref, w_out, p_out, sum_out, rows_out = refs
         weights = border_weights(own_ref, edge_ref[0, 3:4], nz, (band, width), True)
         odd = lax.axis_index("lat") % 2 == 1
+        row = lax.broadcasted_iota(jnp.int32, (band, width), 0)
+        lane = lax.broadcasted_iota(jnp.int32, (band, width), 1)
+        zonal, merid = own_ref[:, 0:1], own_ref[:, 1:2]
+        on_sides = jnp.where(lane == 0, -zonal, jnp.where(lane == width - 1, zonal, 0.0))
+        on_pair = jnp.where(odd & (row == 0), -merid, 0.0)
+        on_pair = jnp.where(jnp.logical_not(odd) & (row == band - 1), merid, on_pair)
     else:
         w_out, p_out = refs
 
@@ -541,15 +514,15 @@
         if nz:
             div += weights[0] * edge_ref[k, 0:1] + weights[1] * edge_ref[k, 1:2]
             div += weights[2] * p_ref[k] + weights[3] * edge_ref[k, 2:3]
+            sides = jnp.concatenate([beside(west_ref, east_ref, k, levels)] * per, axis=1)
+            div += on_sides * sides + on_pair * pair_ref[k:k + 1]
         return p_ref[k] - sound_ref[k] * div
 
     def finish(k, fresh):
         if nz:
             total = p_ref[k] + fresh
             rows_out[k] = jnp.where(odd, total[band - 2:], total[:2])
-            for h in range(per):
-                at = (k % depth * per + h) * band
-                sum_out[k // depth, at:at + band] = total[:, h * LANES:(h + 1) * LANES]
+            sum_out[k] = total
 
     sweep(level_ref, sound_ref, inv_ref, w_ref, star, w_out, p_out, finish)
 
@@ -560,7 +533,8 @@
     zonal = jnp.broadcast_to(own_ref[:, 0:1], (band, width))
     merid = jnp.broadcast_to(own_ref[:, 1:2], (band, width))
     if nz:
-        edge_ref, facing_ref, rows_ref, refs = refs[0], refs[1], refs[2], refs[3:]
+        edge_ref, facing_ref, rows_ref, pair_ref, west_ref, east_ref = refs[:6]
+        refs = refs[6:]
         depth = levels // field_ref.shape[0]
         near = edge_ref[0, 3:4]
         weights = border_weights(own_ref, near, nz, (band, width), False)
@@ -607,9 +581,10 @@
         v -= weights[0] * far[0:1] + weights[1] * far[1:2]
         u_out[k], v_out[k] = u, v
         b, c, at = k // depth, k % depth, 2 * depth * per * band
-        sides = jnp.concatenate([unfold(field_ref[b, at + 4:at + 8], c)] * per, axis=1)
+        sides = unfold(field_ref[b, at + 4:at + 8], c) + beside(west_ref, east_ref, k, levels)
+        sides = jnp.concatenate([sides] * per, axis=1)
         at += c * per
-        pair = jnp.concatenate([field_ref[b, at + h:at + h + 1] for h in range(per)], axis=1)
+        pair = pair_ref[k:k + 1] + jnp.concatenate([field_ref[b, at + h:at + h + 1] for h in range(per)], axis=1)
         half = edge_ref[k, 2:3] - near * jnp.where(odd, far[1:2] - mine[1:2], mine[0:1] - far[0:1])
         north, south = jnp.where(odd, half, pair), jnp.where(odd, pair, half)
         east = jnp.where(lane == width - 1, sides, pltpu.roll(u, width - 1, 1))
@@ -623,11 +598,11 @@
         move.wait()
 
 
-def column(first, nz, depth, level_coef, own, sound, *operands):
-    levels, band, width = sound.shape
+def column(first, nz, level_rows, own, sound, *operands):
+    levels, _, width = sound.shape
     shapes = [jax.ShapeDtypeStruct(sound.shape, F32)] * (2 if first else 4)
     if first and nz:
-        shapes.append(jax.ShapeDtypeStruct((levels // depth, depth * (width // LANES) * band, LANES), F32))
+        shapes.append(jax.ShapeDtypeStruct(sound.shape, F32))
         shapes.append(jax.ShapeDtypeStruct((levels, 2, width), F32))
     extra = {}
     if not first:
@@ -641,7 +616,7 @@
         cost_estimate=pl.CostEstimate(flops=20 * sound.size, bytes_accessed=40 * sound.size, transcendentals=0),
         name="column_first" if first else "column_last",
         **extra,
-    )(level_coef, own, sound, *operands)
+    )(level_rows, own, sound, *operands)
 
 
 def shifted(block, axis, step):
@@ -695,22 +670,25 @@
     per = width // LANES
 
     depth = levels // (2 * nl)
-    if nz == 4 and band == 8 and 1 <= depth <= 2 and depth * per <= 4 and levels == 2 * nl * depth:
+    if nz == 4 and band == 8 and 1 <= depth <= 2 and depth * per <= 4 and levels == 2 * nl * depth and levels <= LANES // 2:
         plan = Plan(True, 2, nl, depth, per, band, 0, band)
-        blocked = [a.reshape(levels // depth, depth, band, width) for a in (pressure, zonal_wind, merid_wind)]
-        sent, rows = pack(zonal_coef, merid_coef, *blocked)
-        circles = exchange(sent, True)
-        edges = swapped(rows, 1)
-        limits = lax.dynamic_slice_in_dim(limit, me // 2 * 2 * band, 2 * band)
-        limits = jnp.tile(limits, depth)[:, None]
+        blocks = (levels // depth, depth * band, width)
+        circles = exchange(pressure.reshape(blocks), True)
+        inputs = (zonal_coef, merid_coef, level_coef, cutoff, filter_mask, pressure, zonal_wind, merid_wind)
+        inputs = [pltpu.with_memory_space_constraint(a, pltpu.HBM) for a in inputs]
+        pair, half, sides, own, level_rows, limits = edges(depth, 2, *inputs)
+        pair = swapped(pair, 0)
+        half = swapped(half, 1)
+        west, east = shifted(sides, "lon", 1), shifted(sides, "lon", -1)
         inv, base = factor(level_rows, sound_coef, zonal_wind, merid_wind, own)
-        div = transform(plan, False, limits, weights, table, circles)
+        div = transform(plan, False, limits, weights, table, circles, own, pair)
         div = exchange(div, True).reshape(levels, band, width)
-        w, p, total, rows = column(True, nz, depth, level_rows, own, sound_coef, inv, base, div, pressure, vertical_wind, edges)
+        w, p, total, rows = column(True, nz, level_rows, own, sound_coef, inv, base, div, pressure, vertical_wind, half, pair, west, east)
         facing = swapped(rows, 1)
-        fields = transform(plan, True, limits, weights, table, exchange(total, True), circles)
+        circles = exchange(total.reshape(blocks), True)
+        fields = transform(plan, True, limits, weights, table, circles, own, pair)
         fields = exchange(fields, True)
-        return column(False, nz, depth, level_rows, own, sound_coef, inv, fields, p, w, zonal_wind, merid_wind, edges, facing, rows)
+        return column(False, nz, level_rows, own, sound_coef, inv, fields, p, w, zonal_wind, merid_wind, half, facing, rows, pair, west, east)
 
     depth, halo = levels // nl, 2
     tall = -(-(band + 2 * halo) // 8) * 8
@@ -720,8 +698,7 @@
         low, high = lat_edges(field[:, -halo:], field[:, :halo])
         field = jnp.concatenate([low, field, high], axis=1)
         field = jnp.pad(field, ((0, 0), (0, tall - band - 2 * halo), (0, 0)))
-        field = field.reshape(levels, tall, per, LANES).swapaxes(1, 2)
-        return exchange(field.reshape(nl, depth * per * tall, LANES), False)
+        return exchange(field.reshape(nl, depth * tall, width), False)
 
     circles = spread(pressure)
     low, high = lat_edges(own[-halo:], own[:halo])
@@ -742,10 +719,10 @@
     (inv,) = factor(level_rows, sound_coef)
     div = transform(plan, False, coefs, weights, table, circles)
     div = exchange(div, False).reshape(levels, band, width)
-    w, p = column(True, 0, depth, level_rows, own, sound_coef, inv, base, div, pressure, vertical_wind)
+    w, p = column(True, 0, level_rows, own, sound_coef, inv, base, div, pressure, vertical_wind)
     fields = transform(plan, True, coefs, weights, table, spread(pressure + p))
     fields = exchange(fields, False).reshape(levels, 3 * band, width)
-    return column(False, 0, depth, level_rows, own, sound_coef, inv, fields, p, w, zonal_wind, merid_wind, base)
+    return column(False, 0, level_rows, own, sound_coef, inv, fields, p, w, zonal_wind, merid_wind, base)
 
 
 def solution(mesh):

time: 63.8 us -> 59.7 us (0.936)
  starting transfers between devices: 15.1 us -> 19.4 us
  local copies, waits for them, and re-layouts: 3.9 us -> 0.04 us
  waiting for transfers between devices: 22.5 us -> 19.3 us
  Pallas kernels: 8.51 us -> 7.15 us
    all_to_all x3, waiting for transfers between devices: 22.5 us -> 12.4 us  [exchange(): lax.all_to_all(block, axes, split_axis=0, concat_axis=0, axis_index_group...]
    ppermute x0 -> x2, waiting for transfers between devices: none -> 3.56 us  [shifted(): lax.ppermute(block, axis, [(i, (i + step) % count) for i in range(count)])]
    unnamed x30 -> x14, local copies, waits for them, and re-layouts: 3.59 us -> 0.04 us
    ppermute x2 -> x3, waiting for transfers between devices: 0.01 us -> 3.34 us  [swapped(): return lax.ppermute(block, 'lat', pairs + [(b, a) for a, b in pairs])]
    ppermute x0 -> x2, starting transfers between devices: none -> 2.51 us  [shifted(): lax.ppermute(block, axis, [(i, (i + step) % count) for i in range(count)])]
    ppermute x2 -> x3, starting transfers between devices: 1.33 us -> 3.32 us  [swapped(): return lax.ppermute(block, 'lat', pairs + [(b, a) for a, b in pairs])]
    pallas_call x1, Pallas kernels: 2.79 us -> 1.42 us  [edges(): pl.pallas_call(functools.partial(edges_kernel, depth, bands), in_specs=[h...]
  transfers between devices with their start and end apart: 5 -> 8, of which waited for: 3 -> 6; matrix products, arithmetic and copies ran while one was open for 1% -> 0% of each run, Pallas kernels for 1% -> 3%
where the time goes in v5:
time: 59.7 us; the launch traced here: 59.2 us
  starting transfers between devices  19.4 us (32%)
  waiting for transfers between devices  19.3 us (32%)
  blocking collectives  12.5 us (21%)
  Pallas kernels  7.15 us (12%)
  between operations  0.78 us (1%)
    all_to_all x3, starting transfers between devices, exchange(): lax.all_to_all(block, axes, split_axis=0, concat_axis=0, axis_index_group...  13.6 us
    all_to_all x1, blocking collectives, exchange(): lax.all_to_all(block, axes, split_axis=0, concat_axis=0, axis_index_group...  12.5 us
    all_to_all x3, waiting for transfers between devices, exchange(): lax.all_to_all(block, axes, split_axis=0, concat_axis=0, axis_index_group...  12.4 us
    ppermute x2, waiting for transfers between devices, shifted(): lax.ppermute(block, axis, [(i, (i + step) % count) for i in range(count)])  3.56 us
    pallas_call x2, Pallas kernels, transform(): pl.pallas_call(functools.partial(transform_kernel, plan, full), out_specs...  3.52 us
    ppermute x3, waiting for transfers between devices, swapped(): return lax.ppermute(block, 'lat', pairs + [(b, a) for a, b in pairs])  3.34 us
    ppermute x3, starting transfers between devices, swapped(): return lax.ppermute(block, 'lat', pairs + [(b, a) for a, b in pairs])  3.32 us
    ppermute x2, starting transfers between devices, shifted(): lax.ppermute(block, axis, [(i, (i + step) % count) for i in range(count)])  2.51 us
  transfers between devices with their start and end apart: 8, of which 6 were waited for; matrix products, arithmetic and copies ran while one was open for 0% of the time, Pallas kernels for 3%

profile of v5, /device:TPU:0, one launch (start us, length us, event | category | flops | bytes accessed | tf_op | source)
XLA Modules:
  0.0 59.2 jit_solution(7802002435403395235)
XLA Ops:
  0.6 6.3 %all-to-all-start = ((f32[16,16,256]{2,1,0:T(8,128)}), f32[16,16,256]{2,1,0:T(8,128)S(1)}, u32[]{:S(2)}, u32[]{:S(2)}) async-start(f32[16,16,256]{2,1,0:T(8,128)} %bitcast.3), calls=%async_computation | async-start | bytes 524288 | tf_op jit(solution)/shard_map/all_to_all | solution.py:633
  7.0 0.0 copy-start.4
  7.0 0.0 copy-start.6
  7.0 1.4 %edges.1 = (f32[40,256]{1,0:T(8,128)S(1)}, f32[32,4,256]{2,1,0:T(4,128)S(1)}, f32[8,128]{1,0:T(8,128)S(1)}, f32[8,128]{1,0:T(8,128)S(1)}, f32[32,256]{1,0:T(8,128)S(1)}, /*index=5*/f32[32,128]{1,0:T(8,128)S(1)}) custom-call(f32[8]{0:T(128)} %zonal_ref.1, f32[8]{0:T(128)} %merid_ref.1, f32[32]{0:T(128)} %level_ref.1, s32[32]{0:T(128)} %cutoff_ref.1, ...), custom_call_target="tpu_custom_call" | custom-call | flops 262144 | bytes 1048576 | tf_op jit(solution)/shard_map/edges/pallas_call | solution.py:413
  8.4 2.0 %collective-permute-start = (f32[40,256]{1,0:T(8,128)S(1)}, f32[40,256]{1,0:T(8,128)S(1)}, u32[]{:S(2)}, u32[]{:S(2)}) collective-permute-start(f32[40,256]{1,0:T(8,128)S(1)} %get-tuple-element.20), channel_id=1, source_target_pairs={{0,8},{16,24},{8,0},{24,16},{1,9},{17,25},{9,1},{25,17},{2,10},{18... | collective-permute-start | bytes 122888 | tf_op jit(solution)/shard_map/ppermute | solution.py:639
  10.4 3.3 %collective-permute-done.refs_1_.refs_3_ = f32[40,256]{1,0:T(8,128)S(1)} collective-permute-done((f32[40,256]{1,0:T(8,128)S(1)}, f32[40,256]{1,0:T(8,128)S(1)}, u32[]{:S(2)}, u32[]{:S(2)}) %collective-permute-start) | collective-permute-done | bytes 40992 | tf_op jit(solution)/shard_map/ppermute | solution.py:639
  13.7 1.4 %all-to-all-done.x_ref = f32[16,16,256]{2,1,0:T(8,128)S(1)} async-done(((f32[16,16,256]{2,1,0:T(8,128)}), f32[16,16,256]{2,1,0:T(8,128)S(1)}, u32[]{:S(2)}, u32[]{:S(2)}) %all-to-all-start) | async-done | bytes 262176 | tf_op jit(solution)/shard_map/all_to_all | solution.py:633
  15.1 0.0 copy-done.4
  15.1 0.0 copy-done.6
  15.1 0.0 copy-start.2
  15.1 1.7 %transform_div.1 = f32[16,16,256]{2,1,0:T(8,128)} custom-call(f32[16,16,256]{2,1,0:T(8,128)S(1)} %all-to-all-done.x_ref, f32[8,128]{1,0:T(8,128)S(1)} %get-tuple-element.17.refs_2_.refs_0_.own_ref, f32[40,256]{1,0:T(8,128)S(1)} %collective-permute-done.refs_1_.refs_3_, f32[32,128]{1,0:T(8,128)S(1)} %get-tuple-element.21.refs_2_, ...), custom_call_target="tpu_custom_call" | custom-call | flops 226492416 | bytes 2097152 | tf_op jit(solution)/shard_map/transform_div/pallas_call | solution.py:315
  16.8 0.0 copy-start
  16.8 0.0 copy-start.1
  16.8 3.7 %all-to-all-start.1 = ((f32[16,16,256]{2,1,0:T(8,128)}), f32[16,16,256]{2,1,0:T(8,128)S(1)}, u32[]{:S(2)}, u32[]{:S(2)}) async-start(f32[16,16,256]{2,1,0:T(8,128)} %transform_div.1), calls=%async_computation.1 | async-start | bytes 524288 | tf_op jit(solution)/shard_map/all_to_all | solution.py:633
  20.5 0.7 %collective-permute-start.1 = (f32[32,4,256]{2,1,0:T(4,128)S(1)}, f32[32,4,256]{2,1,0:T(4,128)S(1)}, u32[]{:S(2)}, u32[]{:S(2)}) collective-permute-start(f32[32,4,256]{2,1,0:T(4,128)S(1)} %get-tuple-element.22), channel_id=1, source_target_pairs={{8,16},{16,8},{9,17},{17,9},{10,18},{18,10},{11,19},{19,11},{12,20... | collective-permute-start | bytes 393224 | tf_op jit(solution)/shard_map/ppermute | solution.py:639
  21.2 2.5 %collective-permute-start.3 = (f32[8,128]{1,0:T(8,128)S(1)}, f32[8,128]{1,0:T(8,128)S(1)}, u32[]{:S(2)}, u32[]{:S(2)}) collective-permute-start(f32[8,128]{1,0:T(8,128)S(1)} %get-tuple-element.23), channel_id=1, source_target_pairs={{0,7},{1,0},{2,1},{3,2},{4,3},{5,4},{6,5},{7,6},{8,15},{9,8},{10,9... | collective-permute-start | bytes 12296 | tf_op jit(solution)/shard_map/ppermute | solution.py:624
  23.7 0.0 collective-permute-start.2
  23.7 0.0 copy-done.2
  23.7 0.0 copy-done
  23.7 0.0 copy-done.1
  23.7 0.0 copy-start.3
  23.7 0.0 copy-start.5
  23.7 0.3 factor_columns.1
  24.1 0.9 %collective-permute-done.3.refs_3_.refs_5_ = f32[8,128]{1,0:T(8,128)S(1)} collective-permute-done((f32[8,128]{1,0:T(8,128)S(1)}, f32[8,128]{1,0:T(8,128)S(1)}, u32[]{:S(2)}, u32[]{:S(2)}) %collective-permute-start.3) | collective-permute-done | bytes 4128 | tf_op jit(solution)/shard_map/ppermute | solution.py:624
  25.0 2.6 %collective-permute-done.2.refs_2_.refs_4_ = f32[8,128]{1,0:T(8,128)S(1)} collective-permute-done((f32[8,128]{1,0:T(8,128)S(1)}, f32[8,128]{1,0:T(8,128)S(1)}, u32[]{:S(2)}, u32[]{:S(2)}) %collective-permute-start.2) | collective-permute-done | bytes 4128 | tf_op jit(solution)/shard_map/ppermute | solution.py:624
  27.6 0.0 collective-permute-done.1.refs_0_
  27.6 0.5 all-to-all-done.1
  28.2 0.0 copy-done.3
  28.2 0.0 copy-done.5
  28.2 0.4 column_first.1
  28.6 12.5 %all_to_all.20.x_ref = f32[16,16,256]{2,1,0:T(8,128)S(1)} all-to-all(f32[16,16,256]{2,1,0:T(8,128)S(1)} %bitcast.5), channel_id=1, replica_groups={{0,1,2,3,4,5,6,7,8,9,10,11,12,13,14,15},{16,17,18,19,20,21,22,23,24,25,..., dimensions={0} | all-to-all | bytes 524288 | tf_op jit(solution)/shard_map/all_to_all | solution.py:633
  41.1 1.9 %transform_all.1 = f32[16,72,128]{2,1,0:T(8,128)} custom-call(f32[16,16,256]{2,1,0:T(8,128)S(1)} %all_to_all.20.x_ref, f32[8,128]{1,0:T(8,128)S(1)} %get-tuple-element.17.refs_2_.refs_0_.own_ref, f32[40,256]{1,0:T(8,128)S(1)} %collective-permute-done.refs_1_.refs_3_, f32[32,128]{1,0:T(8,128)S(1)} %get-tuple-element.21.refs_2_, ...), custom_call_target="tpu_custom_call" | custom-call | flops 452984832 | bytes 2097152 | tf_op jit(solution)/shard_map/transform_all/pallas_call | solution.py:315
  42.9 3.6 %all-to-all-start.3 = ((f32[16,72,128]{2,1,0:T(8,128)}), f32[16,72,128]{2,1,0:T(8,128)S(1)}, u32[]{:S(2)}, u32[]{:S(2)}) async-start(f32[16,72,128]{2,1,0:T(8,128)} %transform_all.1), calls=%async_computation.3 | async-start | bytes 1179648 | tf_op jit(solution)/shard_map/all_to_all | solution.py:633
  46.5 0.7 %collective-permute-start.4 = (f32[32,2,256]{2,1,0:T(2,128)S(1)}, f32[32,2,256]{2,1,0:T(2,128)S(1)}, u32[]{:S(2)}, u32[]{:S(2)}) collective-permute-start(f32[32,2,256]{2,1,0:T(2,128)S(1)} %get-tuple-element.27.refs_2_), channel_id=1, source_target_pairs={{8,16},{16,8},{9,17},{17,9},{10,18},{18,10},{11,19},{19,11},{12,20... | collective-permute-start | bytes 196616 | tf_op jit(solution)/shard_map/ppermute | solution.py:639
  47.2 0.0 collective-permute-done.4.refs_1_
  47.2 10.5 %all-to-all-done.3.field_ref = f32[16,72,128]{2,1,0:T(8,128)S(1)} async-done(((f32[16,72,128]{2,1,0:T(8,128)}), f32[16,72,128]{2,1,0:T(8,128)S(1)}, u32[]{:S(2)}, u32[]{:S(2)}) %all-to-all-start.3) | async-done | bytes 589856 | tf_op jit(solution)/shard_map/all_to_all | solution.py:633
  57.7 1.4 %column_last.1 = (f32[32,8,256]{2,1,0:T(8,128)}, f32[32,8,256]{2,1,0:T(8,128)}, f32[32,8,256]{2,1,0:T(8,128)}, f32[32,8,256]{2,1,0:T(8,128)}) custom-call(f32[32,256]{1,0:T(8,128)S(1)} %get-tuple-element.16.level_ref, f32[8,128]{1,0:T(8,128)S(1)} %get-tuple-element.17.refs_2_.refs_0_.own_ref, f32[32,8,256]{2,1,0:T(8,128)S(1)} %copy-done, ...), custom_call_target="tpu_custom_call" | custom-call | flops 1310720 | bytes 2621440 | tf_op jit(solution)/shard_map/column_last/pallas_call | solution.py:610
Async XLA Ops:
  0.6 14.5 %all-to-all-start = ((f32[16,16,256]{2,1,0:T(8,128)}), f32[16,16,256]{2,1,0:T(8,128)S(1)}, u32[]{:S(2)}, u32[]{:S(2)}) async-start(f32[16,16,256]{2,1,0:T(8,128)} %bitcast.3), calls=%async_computation | async-start | bytes 524288 | tf_op jit(solution)/shard_map/all_to_all | solution.py:633
  7.0 8.1 %copy-start.4 = (bf16[2,2,256,256]{3,2,1,0:T(8,128)(2,1)S(1)}, bf16[2,2,256,256]{3,2,1,0:T(8,128)(2,1)}, u32[]{:S(2)}) copy-start(bf16[2,2,256,256]{3,2,1,0:T(8,128)(2,1)} %constant.4.clone.refs_3_) | copy-start | bytes 1572868
  7.0 8.1 %copy-start.6 = (f32[5,9,128]{2,1,0:T(8,128)S(1)}, f32[5,9,128]{2,1,0:T(8,128)}, u32[]{:S(2)}) copy-start(f32[5,9,128]{2,1,0:T(8,128)} %constant.5.clone.refs_4_) | copy-start | bytes 69124
  8.4 5.3 %collective-permute-start = (f32[40,256]{1,0:T(8,128)S(1)}, f32[40,256]{1,0:T(8,128)S(1)}, u32[]{:S(2)}, u32[]{:S(2)}) collective-permute-start(f32[40,256]{1,0:T(8,128)S(1)} %get-tuple-element.20), channel_id=1, source_target_pairs={{0,8},{16,24},{8,0},{24,16},{1,9},{17,25},{9,1},{25,17},{2,10},{18... | collective-permute-start | bytes 122888 | tf_op jit(solution)/shard_map/ppermute | solution.py:639
  15.1 8.6 %copy-start.2 = (f32[32,8,256]{2,1,0:T(8,128)S(1)}, f32[32,8,256]{2,1,0:T(8,128)}, u32[]{:S(2)}) copy-start(f32[32,8,256]{2,1,0:T(8,128)} %v_ref.3) | copy-start | bytes 786436
  16.8 6.9 %copy-start = (f32[32,8,256]{2,1,0:T(8,128)S(1)}, f32[32,8,256]{2,1,0:T(8,128)}, u32[]{:S(2)}) copy-start(f32[32,8,256]{2,1,0:T(8,128)} %sound_ref.5) | copy-start | bytes 786436
  16.8 6.9 %copy-start.1 = (f32[32,8,256]{2,1,0:T(8,128)S(1)}, f32[32,8,256]{2,1,0:T(8,128)}, u32[]{:S(2)}) copy-start(f32[32,8,256]{2,1,0:T(8,128)} %u_ref.3) | copy-start | bytes 786436
  16.8 11.4 %all-to-all-start.1 = ((f32[16,16,256]{2,1,0:T(8,128)}), f32[16,16,256]{2,1,0:T(8,128)S(1)}, u32[]{:S(2)}, u32[]{:S(2)}) async-start(f32[16,16,256]{2,1,0:T(8,128)} %transform_div.1), calls=%async_computation.1 | async-start | bytes 524288 | tf_op jit(solution)/shard_map/all_to_all | solution.py:633
  20.5 7.1 %collective-permute-start.1 = (f32[32,4,256]{2,1,0:T(4,128)S(1)}, f32[32,4,256]{2,1,0:T(4,128)S(1)}, u32[]{:S(2)}, u32[]{:S(2)}) collective-permute-start(f32[32,4,256]{2,1,0:T(4,128)S(1)} %get-tuple-element.22), channel_id=1, source_target_pairs={{8,16},{16,8},{9,17},{17,9},{10,18},{18,10},{11,19},{19,11},{12,20... | collective-permute-start | bytes 393224 | tf_op jit(solution)/shard_map/ppermute | solution.py:639
  21.2 3.8 %collective-permute-start.3 = (f32[8,128]{1,0:T(8,128)S(1)}, f32[8,128]{1,0:T(8,128)S(1)}, u32[]{:S(2)}, u32[]{:S(2)}) collective-permute-start(f32[8,128]{1,0:T(8,128)S(1)} %get-tuple-element.23), channel_id=1, source_target_pairs={{0,7},{1,0},{2,1},{3,2},{4,3},{5,4},{6,5},{7,6},{8,15},{9,8},{10,9... | collective-permute-start | bytes 12296 | tf_op jit(solution)/shard_map/ppermute | solution.py:624
  23.7 3.9 %collective-permute-start.2 = (f32[8,128]{1,0:T(8,128)S(1)}, f32[8,128]{1,0:T(8,128)S(1)}, u32[]{:S(2)}, u32[]{:S(2)}) collective-permute-start(f32[8,128]{1,0:T(8,128)S(1)} %get-tuple-element.23), channel_id=1, source_target_pairs={{0,1},{1,2},{2,3},{3,4},{4,5},{5,6},{6,7},{7,0},{8,9},{9,10},{10,1... | collective-permute-start | bytes 12296 | tf_op jit(solution)/shard_map/ppermute | solution.py:624
  23.7 4.5 %copy-start.3 = (f32[32,8,256]{2,1,0:T(8,128)S(1)}, f32[32,8,256]{2,1,0:T(8,128)}, u32[]{:S(2)}) copy-start(f32[32,8,256]{2,1,0:T(8,128)} %p_ref.3) | copy-start | bytes 786436
  23.7 4.5 %copy-start.5 = (f32[32,8,256]{2,1,0:T(8,128)S(1)}, f32[32,8,256]{2,1,0:T(8,128)}, u32[]{:S(2)}) copy-start(f32[32,8,256]{2,1,0:T(8,128)} %w_ref.1) | copy-start | bytes 786436
  42.9 14.8 %all-to-all-start.3 = ((f32[16,72,128]{2,1,0:T(8,128)}), f32[16,72,128]{2,1,0:T(8,128)S(1)}, u32[]{:S(2)}, u32[]{:S(2)}) async-start(f32[16,72,128]{2,1,0:T(8,128)} %transform_all.1), calls=%async_computation.3 | async-start | bytes 1179648 | tf_op jit(solution)/shard_map/all_to_all | solution.py:633
  46.5 0.7 %collective-permute-start.4 = (f32[32,2,256]{2,1,0:T(2,128)S(1)}, f32[32,2,256]{2,1,0:T(2,128)S(1)}, u32[]{:S(2)}, u32[]{:S(2)}) collective-permute-start(f32[32,2,256]{2,1,0:T(2,128)S(1)} %get-tuple-element.27.refs_2_), channel_id=1, source_target_pairs={{8,16},{16,8},{9,17},{17,9},{10,18},{18,10},{11,19},{19,11},{12,20... | collective-permute-start | bytes 196616 | tf_op jit(solution)/shard_map/ppermute | solution.py:639

commit v6 on v5

--- a/solution.py
+++ b/solution.py
@@ -136,23 +136,9 @@
     return weights, rows.astype(np.float32)
 
 
-def transform_kernel(plan, full, x_ref, *refs):
-    if plan.packed:
-        own_ref, near_ref, refs = refs[0], refs[1], refs[2:]
-    coef_ref, weight_ref, table_ref, result_ref, lhs_ref, spec_ref, work_ref, out_ref, sems = refs
-    bands, nl, depth, per = plan.bands, plan.nl, plan.depth, plan.per
-    tall, skip, band = plan.tall, plan.skip, plan.band
-    stacks = depth * bands
-    pieces = nl * per
-    groups = pieces // 2 + 1
-    rows = stacks * tall
-    length = pieces * LANES
-
-    def tile(c, z, l, h):
-        return x_ref[z * nl + l, c * tall:(c + 1) * tall, h * LANES:(h + 1) * LANES]
-
+def matmul(weight_ref, lhs_ref, size, rows):
     def product(which, start):
-        high, low = (lhs_ref[i, start:start + groups * rows] for i in range(2))
+        high, low = (lhs_ref[i, start:start + size] for i in range(2))
         total = jnp.dot(high, weight_ref[which, 0], preferred_element_type=F32)
         total += jnp.dot(low, weight_ref[which, 0], preferred_element_type=F32)
         return total + jnp.dot(high, weight_ref[which, 1], preferred_element_type=F32)
@@ -163,6 +149,18 @@
             low = (part - high.astype(F32)).astype(BF16)
             lhs_ref[0, row:row + rows, half * LANES:(half + 1) * LANES] = high
             lhs_ref[1, row:row + rows, half * LANES:(half + 1) * LANES] = low
+
+    return product, put
+
+
+def forward(plan, x_ref, weight_ref, table_ref, spec_ref, lhs_ref):
+    bands, nl, depth, per, tall = plan.bands, plan.nl, plan.depth, plan.per, plan.tall
+    rows = depth * bands * tall
+    groups = nl * per // 2 + 1
+    product, put = matmul(weight_ref, lhs_ref, groups * rows, rows)
+
+    def tile(c, z, l, h):
+        return x_ref[z * nl + l, c * tall:(c + 1) * tall, h * LANES:(h + 1) * LANES]
 
     chunks = []
     for l in range(nl):
@@ -178,6 +176,37 @@
                 re, im = re * cr + im * ci, im * cr - re * ci
         put(s * rows, re, zero if im is None else im)
     spec_ref[...] = product(0, 0)
+
+
+def spectra_of(plan, x, weights, table):
+    size = table.shape[1] * plan.depth * plan.bands * plan.tall
+    return pl.pallas_call(
+        functools.partial(forward, plan),
+        out_shape=jax.ShapeDtypeStruct((size, 2 * LANES), F32),
+        scratch_shapes=[pltpu.VMEM((2, size, 2 * LANES), BF16)],
+        compiler_params=KERNEL,
+        cost_estimate=pl.CostEstimate(flops=3 * 2 * 65536 * size, bytes_accessed=8 * x.size, transcendentals=0),
+        name="transform_forward",
+    )(x, weights, table)
+
+
+def transform_kernel(plan, full, x_ref, *refs):
+    if plan.packed:
+        own_ref, near_ref, refs = refs[0], refs[1], refs[2:]
+    coef_ref, weight_ref, table_ref, result_ref, lhs_ref, spec_ref, work_ref, out_ref, sems = refs
+    bands, nl, depth, per = plan.bands, plan.nl, plan.depth, plan.per
+    tall, skip, band = plan.tall, plan.skip, plan.band
+    stacks = depth * bands
+    pieces = nl * per
+    groups = pieces // 2 + 1
+    rows = stacks * tall
+    length = pieces * LANES
+
+    if len(x_ref.shape) == 3:
+        forward(plan, x_ref, weight_ref, table_ref, spec_ref, lhs_ref)
+    else:
+        spec_ref = x_ref
+    product, put = matmul(weight_ref, lhs_ref, groups * rows, rows)
 
     def column(a):
         return jnp.broadcast_to(a, (a.shape[0], LANES))
@@ -308,7 +337,7 @@
     fields = len(plan.fields(full))
     groups = table.shape[1]
     count = fields * groups * rows
-    blocks, width = operands[0].shape[0], plan.per * LANES
+    blocks, width = plan.bands * plan.nl, plan.per * LANES
     shape = (blocks, plan.depth * fields * plan.band, width)
     if plan.packed and full:
         shape = (blocks, (2 * plan.depth * plan.per + 1) * plan.band, LANES)
@@ -546,7 +575,7 @@
     u_out, v_out, w_out, p_out = refs[4:8]
     sems = refs[8]
     leaving = []
-    size = levels // 4
+    size = levels // 8
 
     def leave(out, start):
         part = pl.ds(start, size)
@@ -606,7 +635,7 @@
         shapes.append(jax.ShapeDtypeStruct((levels, 2, width), F32))
     extra = {}
     if not first:
-        extra["scratch_shapes"] = [pltpu.VMEM(sound.shape, F32)] * 4 + [pltpu.SemaphoreType.DMA((16,))]
+        extra["scratch_shapes"] = [pltpu.VMEM(sound.shape, F32)] * 4 + [pltpu.SemaphoreType.DMA((32,))]
     return pl.pallas_call(
         functools.partial(column_first_kernel if first else column_last_kernel, nz),
         in_specs=[pl.BlockSpec(memory_space=pltpu.VMEM)] * (3 + len(operands)),
@@ -681,6 +710,7 @@
         half = swapped(half, 1)
         west, east = shifted(sides, "lon", 1), shifted(sides, "lon", -1)
         inv, base = factor(level_rows, sound_coef, zonal_wind, merid_wind, own)
+        circles = spectra_of(plan, circles, weights, table)
         div = transform(plan, False, limits, weights, table, circles, own, pair)
         div = exchange(div, True).reshape(levels, band, width)
         w, p, total, rows = column(True, nz, level_rows, own, sound_coef, inv, base, div, pressure, vertical_wind, half, pair, west, east)

time: 59.7 us -> 59.7 us (level)
    all_to_all x3, waiting for transfers between devices: 12.4 us -> 15.7 us  [exchange(): lax.all_to_all(block, axes, split_axis=0, concat_axis=0, axis_index_group...]
    ppermute x3, waiting for transfers between devices: 3.34 us -> 0.01 us  [swapped(): return lax.ppermute(block, 'lat', pairs + [(b, a) for a, b in pairs])]
  transfers between devices with their start and end apart: 8 -> 8, of which waited for: 6 -> 5; matrix products, arithmetic and copies ran while one was open for 0% -> 0% of each run, Pallas kernels for 3% -> 4%
where the time goes in v6:
time: 59.7 us; the launch traced here: 59.2 us
  starting transfers between devices  19.4 us (32%)
  waiting for transfers between devices  19.3 us (32%)
  blocking collectives  12.5 us (21%)
  Pallas kernels  7.2 us (12%)
  between operations  0.8 us (1%)
    all_to_all x3, waiting for transfers between devices, exchange(): lax.all_to_all(block, axes, split_axis=0, concat_axis=0, axis_index_group...  15.7 us
    all_to_all x3, starting transfers between devices, exchange(): lax.all_to_all(block, axes, split_axis=0, concat_axis=0, axis_index_group...  13.6 us
    all_to_all x1, blocking collectives, exchange(): lax.all_to_all(block, axes, split_axis=0, concat_axis=0, axis_index_group...  12.5 us
    ppermute x2, waiting for transfers between devices, shifted(): lax.ppermute(block, axis, [(i, (i + step) % count) for i in range(count)])  3.56 us
    ppermute x3, starting transfers between devices, swapped(): return lax.ppermute(block, 'lat', pairs + [(b, a) for a, b in pairs])  3.32 us
    pallas_call x2, Pallas kernels, transform(): pl.pallas_call(functools.partial(transform_kernel, plan, full), out_specs...  3.12 us
    ppermute x2, starting transfers between devices, shifted(): lax.ppermute(block, axis, [(i, (i + step) % count) for i in range(count)])  2.51 us
    pallas_call x2, Pallas kernels, column(): pl.pallas_call(functools.partial(column_first_kernel if first else column...  2.01 us
  transfers between devices with their start and end apart: 8, of which 5 were waited for; matrix products, arithmetic and copies ran while one was open for 0% of the time, Pallas kernels for 4%

profile of v6, /device:TPU:0, one launch (start us, length us, event | category | flops | bytes accessed | tf_op | source)
XLA Modules:
  0.0 59.2 jit_solution(3524798754767646404)
XLA Ops:
  0.6 6.3 %all-to-all-start = ((f32[16,16,256]{2,1,0:T(8,128)}), f32[16,16,256]{2,1,0:T(8,128)S(1)}, u32[]{:S(2)}, u32[]{:S(2)}) async-start(f32[16,16,256]{2,1,0:T(8,128)} %bitcast.3), calls=%async_computation | async-start | bytes 524288 | tf_op jit(solution)/shard_map/all_to_all | solution.py:662
  7.0 0.0 copy-start.4
  7.0 0.0 copy-start.6
  7.0 1.4 %edges.1 = (f32[40,256]{1,0:T(8,128)S(1)}, f32[32,4,256]{2,1,0:T(4,128)S(1)}, f32[8,128]{1,0:T(8,128)S(1)}, f32[8,128]{1,0:T(8,128)S(1)}, f32[32,256]{1,0:T(8,128)S(1)}, /*index=5*/f32[32,128]{1,0:T(8,128)S(1)}) custom-call(f32[8]{0:T(128)} %zonal_ref.1, f32[8]{0:T(128)} %merid_ref.1, f32[32]{0:T(128)} %level_ref.1, s32[32]{0:T(128)} %cutoff_ref.1, ...), custom_call_target="tpu_custom_call" | custom-call | flops 262144 | bytes 1048576 | tf_op jit(solution)/shard_map/edges/pallas_call | solution.py:442
  8.4 2.0 %collective-permute-start = (f32[40,256]{1,0:T(8,128)S(1)}, f32[40,256]{1,0:T(8,128)S(1)}, u32[]{:S(2)}, u32[]{:S(2)}) collective-permute-start(f32[40,256]{1,0:T(8,128)S(1)} %get-tuple-element.20), channel_id=1, source_target_pairs={{0,8},{16,24},{8,0},{24,16},{1,9},{17,25},{9,1},{25,17},{2,10},{18... | collective-permute-start | bytes 122888 | tf_op jit(solution)/shard_map/ppermute | solution.py:668
  10.4 4.7 %all-to-all-done.x_ref = f32[16,16,256]{2,1,0:T(8,128)S(1)} async-done(((f32[16,16,256]{2,1,0:T(8,128)}), f32[16,16,256]{2,1,0:T(8,128)S(1)}, u32[]{:S(2)}, u32[]{:S(2)}) %all-to-all-start) | async-done | bytes 262176 | tf_op jit(solution)/shard_map/all_to_all | solution.py:662
  15.1 0.0 copy-done.4
  15.1 0.0 copy-done.6
  15.1 0.3 transform_forward.1.x_ref
  15.4 0.0 collective-permute-done.refs_1_.refs_3_
  15.5 0.0 copy-start.2
  15.5 1.3 %transform_div.1 = f32[16,16,256]{2,1,0:T(8,128)} custom-call(f32[288,256]{1,0:T(8,128)S(1)} %transform_forward.1.x_ref, f32[8,128]{1,0:T(8,128)S(1)} %get-tuple-element.17.refs_2_.refs_0_.own_ref, f32[40,256]{1,0:T(8,128)S(1)} %collective-permute-done.refs_1_.refs_3_, f32[32,128]{1,0:T(8,128)S(1)} %get-tuple-element.21.refs_2_, ...), custom_call_target="tpu_custom_call" | custom-call | flops 226492416 | bytes 2097152 | tf_op jit(solution)/shard_map/transform_div/pallas_call | solution.py:344
  16.7 0.0 copy-start
  16.8 0.0 copy-start.1
  16.8 3.7 %all-to-all-start.1 = ((f32[16,16,256]{2,1,0:T(8,128)}), f32[16,16,256]{2,1,0:T(8,128)S(1)}, u32[]{:S(2)}, u32[]{:S(2)}) async-start(f32[16,16,256]{2,1,0:T(8,128)} %transform_div.1), calls=%async_computation.1 | async-start | bytes 524288 | tf_op jit(solution)/shard_map/all_to_all | solution.py:662
  20.4 0.7 %collective-permute-start.1 = (f32[32,4,256]{2,1,0:T(4,128)S(1)}, f32[32,4,256]{2,1,0:T(4,128)S(1)}, u32[]{:S(2)}, u32[]{:S(2)}) collective-permute-start(f32[32,4,256]{2,1,0:T(4,128)S(1)} %get-tuple-element.22), channel_id=1, source_target_pairs={{8,16},{16,8},{9,17},{17,9},{10,18},{18,10},{11,19},{19,11},{12,20... | collective-permute-start | bytes 393224 | tf_op jit(solution)/shard_map/ppermute | solution.py:668
  21.1 2.5 %collective-permute-start.3 = (f32[8,128]{1,0:T(8,128)S(1)}, f32[8,128]{1,0:T(8,128)S(1)}, u32[]{:S(2)}, u32[]{:S(2)}) collective-permute-start(f32[8,128]{1,0:T(8,128)S(1)} %get-tuple-element.23), channel_id=1, source_target_pairs={{0,7},{1,0},{2,1},{3,2},{4,3},{5,4},{6,5},{7,6},{8,15},{9,8},{10,9... | collective-permute-start | bytes 12296 | tf_op jit(solution)/shard_map/ppermute | solution.py:653
  23.6 0.0 collective-permute-start.2
  23.6 0.0 copy-done.2
  23.6 0.0 copy-done
  23.6 0.0 copy-done.1
  23.7 0.0 copy-start.3
  23.7 0.0 copy-start.5
  23.7 0.3 factor_columns.1
  24.0 0.9 %collective-permute-done.3.refs_3_.refs_5_ = f32[8,128]{1,0:T(8,128)S(1)} collective-permute-done((f32[8,128]{1,0:T(8,128)S(1)}, f32[8,128]{1,0:T(8,128)S(1)}, u32[]{:S(2)}, u32[]{:S(2)}) %collective-permute-start.3) | collective-permute-done | bytes 4128 | tf_op jit(solution)/shard_map/ppermute | solution.py:653
  25.0 2.6 %collective-permute-done.2.refs_2_.refs_4_ = f32[8,128]{1,0:T(8,128)S(1)} collective-permute-done((f32[8,128]{1,0:T(8,128)S(1)}, f32[8,128]{1,0:T(8,128)S(1)}, u32[]{:S(2)}, u32[]{:S(2)}) %collective-permute-start.2) | collective-permute-done | bytes 4128 | tf_op jit(solution)/shard_map/ppermute | solution.py:653
  27.6 0.0 collective-permute-done.1.refs_0_
  27.6 0.5 all-to-all-done.1
  28.1 0.0 copy-done.3
  28.1 0.0 copy-done.5
  28.1 0.4 column_first.1
  28.6 12.5 %all_to_all.20.x_ref = f32[16,16,256]{2,1,0:T(8,128)S(1)} all-to-all(f32[16,16,256]{2,1,0:T(8,128)S(1)} %bitcast.5), channel_id=1, replica_groups={{0,1,2,3,4,5,6,7,8,9,10,11,12,13,14,15},{16,17,18,19,20,21,22,23,24,25,..., dimensions={0} | all-to-all | bytes 524288 | tf_op jit(solution)/shard_map/all_to_all | solution.py:662
  41.0 1.9 %transform_all.1 = f32[16,72,128]{2,1,0:T(8,128)} custom-call(f32[16,16,256]{2,1,0:T(8,128)S(1)} %all_to_all.20.x_ref, f32[8,128]{1,0:T(8,128)S(1)} %get-tuple-element.17.refs_2_.refs_0_.own_ref, f32[40,256]{1,0:T(8,128)S(1)} %collective-permute-done.refs_1_.refs_3_, f32[32,128]{1,0:T(8,128)S(1)} %get-tuple-element.21.refs_2_, ...), custom_call_target="tpu_custom_call" | custom-call | flops 452984832 | bytes 2097152 | tf_op jit(solution)/shard_map/transform_all/pallas_call | solution.py:344
  42.9 3.6 %all-to-all-start.3 = ((f32[16,72,128]{2,1,0:T(8,128)}), f32[16,72,128]{2,1,0:T(8,128)S(1)}, u32[]{:S(2)}, u32[]{:S(2)}) async-start(f32[16,72,128]{2,1,0:T(8,128)} %transform_all.1), calls=%async_computation.3 | async-start | bytes 1179648 | tf_op jit(solution)/shard_map/all_to_all | solution.py:662
  46.5 0.7 %collective-permute-start.4 = (f32[32,2,256]{2,1,0:T(2,128)S(1)}, f32[32,2,256]{2,1,0:T(2,128)S(1)}, u32[]{:S(2)}, u32[]{:S(2)}) collective-permute-start(f32[32,2,256]{2,1,0:T(2,128)S(1)} %get-tuple-element.27.refs_2_), channel_id=1, source_target_pairs={{8,16},{16,8},{9,17},{17,9},{10,18},{18,10},{11,19},{19,11},{12,20... | collective-permute-start | bytes 196616 | tf_op jit(solution)/shard_map/ppermute | solution.py:668
  47.2 0.0 collective-permute-done.4.refs_1_
  47.2 10.5 %all-to-all-done.3.field_ref = f32[16,72,128]{2,1,0:T(8,128)S(1)} async-done(((f32[16,72,128]{2,1,0:T(8,128)}), f32[16,72,128]{2,1,0:T(8,128)S(1)}, u32[]{:S(2)}, u32[]{:S(2)}) %all-to-all-start.3) | async-done | bytes 589856 | tf_op jit(solution)/shard_map/all_to_all | solution.py:662
  57.7 1.6 %column_last.1 = (f32[32,8,256]{2,1,0:T(8,128)}, f32[32,8,256]{2,1,0:T(8,128)}, f32[32,8,256]{2,1,0:T(8,128)}, f32[32,8,256]{2,1,0:T(8,128)}) custom-call(f32[32,256]{1,0:T(8,128)S(1)} %get-tuple-element.16.level_ref, f32[8,128]{1,0:T(8,128)S(1)} %get-tuple-element.17.refs_2_.refs_0_.own_ref, f32[32,8,256]{2,1,0:T(8,128)S(1)} %copy-done, ...), custom_call_target="tpu_custom_call" | custom-call | flops 1310720 | bytes 2621440 | tf_op jit(solution)/shard_map/column_last/pallas_call | solution.py:639
Async XLA Ops:
  0.6 14.5 %all-to-all-start = ((f32[16,16,256]{2,1,0:T(8,128)}), f32[16,16,256]{2,1,0:T(8,128)S(1)}, u32[]{:S(2)}, u32[]{:S(2)}) async-start(f32[16,16,256]{2,1,0:T(8,128)} %bitcast.3), calls=%async_computation | async-start | bytes 524288 | tf_op jit(solution)/shard_map/all_to_all | solution.py:662
  7.0 8.1 %copy-start.4 = (bf16[2,2,256,256]{3,2,1,0:T(8,128)(2,1)S(1)}, bf16[2,2,256,256]{3,2,1,0:T(8,128)(2,1)}, u32[]{:S(2)}) copy-start(bf16[2,2,256,256]{3,2,1,0:T(8,128)(2,1)} %constant.4.clone.weight_ref.refs_3_) | copy-start | bytes 1572868
  7.0 8.1 %copy-start.6 = (f32[5,9,128]{2,1,0:T(8,128)S(1)}, f32[5,9,128]{2,1,0:T(8,128)}, u32[]{:S(2)}) copy-start(f32[5,9,128]{2,1,0:T(8,128)} %constant.5.clone.table_ref.refs_4_) | copy-start | bytes 69124
  8.4 7.0 %collective-permute-start = (f32[40,256]{1,0:T(8,128)S(1)}, f32[40,256]{1,0:T(8,128)S(1)}, u32[]{:S(2)}, u32[]{:S(2)}) collective-permute-start(f32[40,256]{1,0:T(8,128)S(1)} %get-tuple-element.20), channel_id=1, source_target_pairs={{0,8},{16,24},{8,0},{24,16},{1,9},{17,25},{9,1},{25,17},{2,10},{18... | collective-permute-start | bytes 122888 | tf_op jit(solution)/shard_map/ppermute | solution.py:668
  15.5 8.2 %copy-start.2 = (f32[32,8,256]{2,1,0:T(8,128)S(1)}, f32[32,8,256]{2,1,0:T(8,128)}, u32[]{:S(2)}) copy-start(f32[32,8,256]{2,1,0:T(8,128)} %v_ref.3) | copy-start | bytes 786436
  16.7 6.9 %copy-start = (f32[32,8,256]{2,1,0:T(8,128)S(1)}, f32[32,8,256]{2,1,0:T(8,128)}, u32[]{:S(2)}) copy-start(f32[32,8,256]{2,1,0:T(8,128)} %sound_ref.5) | copy-start | bytes 786436
  16.8 6.9 %copy-start.1 = (f32[32,8,256]{2,1,0:T(8,128)S(1)}, f32[32,8,256]{2,1,0:T(8,128)}, u32[]{:S(2)}) copy-start(f32[32,8,256]{2,1,0:T(8,128)} %u_ref.3) | copy-start | bytes 786436
  16.8 11.4 %all-to-all-start.1 = ((f32[16,16,256]{2,1,0:T(8,128)}), f32[16,16,256]{2,1,0:T(8,128)S(1)}, u32[]{:S(2)}, u32[]{:S(2)}) async-start(f32[16,16,256]{2,1,0:T(8,128)} %transform_div.1), calls=%async_computation.1 | async-start | bytes 524288 | tf_op jit(solution)/shard_map/all_to_all | solution.py:662
  20.4 7.1 %collective-permute-start.1 = (f32[32,4,256]{2,1,0:T(4,128)S(1)}, f32[32,4,256]{2,1,0:T(4,128)S(1)}, u32[]{:S(2)}, u32[]{:S(2)}) collective-permute-start(f32[32,4,256]{2,1,0:T(4,128)S(1)} %get-tuple-element.22), channel_id=1, source_target_pairs={{8,16},{16,8},{9,17},{17,9},{10,18},{18,10},{11,19},{19,11},{12,20... | collective-permute-start | bytes 393224 | tf_op jit(solution)/shard_map/ppermute | solution.py:668
  21.1 3.8 %collective-permute-start.3 = (f32[8,128]{1,0:T(8,128)S(1)}, f32[8,128]{1,0:T(8,128)S(1)}, u32[]{:S(2)}, u32[]{:S(2)}) collective-permute-start(f32[8,128]{1,0:T(8,128)S(1)} %get-tuple-element.23), channel_id=1, source_target_pairs={{0,7},{1,0},{2,1},{3,2},{4,3},{5,4},{6,5},{7,6},{8,15},{9,8},{10,9... | collective-permute-start | bytes 12296 | tf_op jit(solution)/shard_map/ppermute | solution.py:653
  23.6 3.9 %collective-permute-start.2 = (f32[8,128]{1,0:T(8,128)S(1)}, f32[8,128]{1,0:T(8,128)S(1)}, u32[]{:S(2)}, u32[]{:S(2)}) collective-permute-start(f32[8,128]{1,0:T(8,128)S(1)} %get-tuple-element.23), channel_id=1, source_target_pairs={{0,1},{1,2},{2,3},{3,4},{4,5},{5,6},{6,7},{7,0},{8,9},{9,10},{10,1... | collective-permute-start | bytes 12296 | tf_op jit(solution)/shard_map/ppermute | solution.py:653
  23.7 4.5 %copy-start.3 = (f32[32,8,256]{2,1,0:T(8,128)S(1)}, f32[32,8,256]{2,1,0:T(8,128)}, u32[]{:S(2)}) copy-start(f32[32,8,256]{2,1,0:T(8,128)} %p_ref.3) | copy-start | bytes 786436
  23.7 4.5 %copy-start.5 = (f32[32,8,256]{2,1,0:T(8,128)S(1)}, f32[32,8,256]{2,1,0:T(8,128)}, u32[]{:S(2)}) copy-start(f32[32,8,256]{2,1,0:T(8,128)} %w_ref.1) | copy-start | bytes 786436
  42.9 14.8 %all-to-all-start.3 = ((f32[16,72,128]{2,1,0:T(8,128)}), f32[16,72,128]{2,1,0:T(8,128)S(1)}, u32[]{:S(2)}, u32[]{:S(2)}) async-start(f32[16,72,128]{2,1,0:T(8,128)} %transform_all.1), calls=%async_computation.3 | async-start | bytes 1179648 | tf_op jit(solution)/shard_map/all_to_all | solution.py:662
  46.5 0.7 %collective-permute-start.4 = (f32[32,2,256]{2,1,0:T(2,128)S(1)}, f32[32,2,256]{2,1,0:T(2,128)S(1)}, u32[]{:S(2)}, u32[]{:S(2)}) collective-permute-start(f32[32,2,256]{2,1,0:T(2,128)S(1)} %get-tuple-element.27.refs_2_), channel_id=1, source_target_pairs={{8,16},{16,8},{9,17},{17,9},{10,18},{18,10},{11,19},{19,11},{12,20... | collective-permute-start | bytes 196616 | tf_op jit(solution)/shard_map/ppermute | solution.py:668
